TPU v7x, 256 devices: a whole 4x4x8 slice. The times are simulated.
256 devices in a mesh: lat: 64 (over z, y, core), tok: 4 (over x).
Axes of the slice: x: 4, y: 4, z: 8, core: 2. Of those that a mesh axis runs over, the one named last changes fastest.
Arguments:
- coefficients: bfloat16 [2048, 16, 128], P(('lat', 'tok')), may hold values from 0 to 2
- block_ids: int32 [2048, 16], P(('lat', 'tok')), may hold values from 0 to 1023, all different within a row; in each aligned block of 32 rows (0 to 31, 32 to 63, ...) at most 2 rows name the same one
- counts: int32 [2048], P(('lat', 'tok')), may hold values from 10 to 16
- decoder: bfloat16 [1, 131072, 5120], P(None, 'lat', 'tok'), may hold values from -0.125 to 0.125
- bias: float32 [1, 5120], P(None, 'tok'), may hold values from -3 to 3
Outputs:
- recon: bfloat16 [1, 2048, 5120], P(None, 'lat', 'tok')
Inputs may be any that keep to these rules, and one draw needn't show every extreme that they name: `block_ids`: the 16 slots of a token name different blocks. Among the tokens of one index of lat (aligned blocks of 32 rows), no block is named by more than 2 slots, live or padding, and some block is named by exactly 2. `counts`: slots below a token's count are live, the others padding.
All inputs are finite; a program needn't handle non-finite values.
Results may differ from a plain program's by a relative error of at most 0.001.
Values may be sent and summed in bfloat16 or wider, within the bound.
No kernel may reach another device: no remote copies, remote signals or barrier semaphores. Data moves between devices by JAX's collectives and lax.ppermute only.
A program may use at most 128 MiB of HBM per device.

v0:
```python
import math

import jax
import jax.numpy as jnp
from jax import lax
from jax.sharding import PartitionSpec as P


def side_by_side(arrays, axis, dim, along):
    widths = [math.prod(a.shape[along:]) for a in arrays]
    both = jnp.concatenate(
        [a.reshape(*a.shape[:along], w) for a, w in zip(arrays, widths)], axis=along
    )
    whole = lax.all_gather(both, axis, axis=dim, tiled=True)
    parts = jnp.split(whole, [sum(widths[:k]) for k in range(1, len(widths))], axis=along)
    return tuple((b.reshape(*whole.shape[:along], *a.shape[along:]) for a, b in zip(arrays, parts)))


def shards(coefficients, block_ids, counts, decoder, bias):
    lat_count = lax.axis_size("lat")
    gathered_coeffs, gathered_ids, gathered_counts = (
        lax.all_gather(coefficients, "tok", axis=0, tiled=True),
        *side_by_side((block_ids, counts), "tok", 0, 1),
    )
    tok_rows, slot_count = gathered_ids.shape
    block_size = gathered_coeffs.shape[2]
    layers, lat_latents, width_part = decoder.shape
    blocks_dev = lat_latents // block_size
    blocks_total = blocks_dev * lat_count
    capacity = max(2, tok_rows * slot_count * 2 // blocks_total)
    is_live = lax.broadcasted_iota(jnp.int32, (tok_rows, slot_count), 1) < gathered_counts[:, None]
    live_coeffs = jnp.where(
        is_live[:, :, None], gathered_coeffs, jnp.zeros((), gathered_coeffs.dtype)
    )
    flat_ids = gathered_ids.reshape(-1)
    serial = jnp.arange(flat_ids.shape[0], dtype=jnp.int32)
    matches = (flat_ids[:, None] == flat_ids[None, :]) & (serial[None, :] < serial[:, None])
    ranked = jnp.sum(matches.astype(jnp.int32), axis=1)
    position = flat_ids * capacity + ranked
    outgoing = jnp.zeros((blocks_total * capacity, block_size), gathered_coeffs.dtype)
    outgoing = outgoing.at[position].set(live_coeffs.reshape(-1, block_size))
    outgoing = outgoing.reshape(lat_count, blocks_dev * capacity, block_size)
    local_blocks = decoder.reshape(layers, blocks_dev, block_size, width_part)
    token_of = (
        jnp.full((blocks_total * capacity,), -1, jnp.int32).at[position].set(serial // slot_count)
    )
    token_of = token_of.reshape(lat_count, blocks_dev * capacity)
    incoming, tokens_in = (
        lax.all_to_all(outgoing, "lat", split_axis=0, concat_axis=0, tiled=True),
        lax.all_to_all(token_of, "lat", split_axis=0, concat_axis=0, tiled=True),
    )
    incoming = incoming.reshape(lat_count, blocks_dev, capacity, block_size)
    partial_rows = jnp.einsum(
        "sbmk,lbkd->sbmld", incoming, local_blocks, preferred_element_type=jnp.float32
    )
    partial_rows = partial_rows.reshape(-1, layers, width_part)
    source_base = lax.broadcasted_iota(jnp.int32, tokens_in.shape, 0) * tok_rows
    global_row = jnp.where(tokens_in >= 0, source_base + tokens_in, -1).reshape(-1)
    row_count = tok_rows * lax.axis_size("lat")
    target = global_row - jnp.int32(0)
    in_range = (global_row >= 0) & (target >= 0) & (target < row_count)
    target = jnp.where(in_range, target, row_count)
    empty_rows = jnp.zeros((row_count, layers, width_part), jnp.float32)
    summed_rows = lax.psum_scatter(
        empty_rows.at[target].add(partial_rows, mode="drop"), "lat", scatter_dimension=0, tiled=True
    )
    summed = jnp.transpose(summed_rows, (1, 0, 2))
    return (summed + bias[:, None, :]).astype(jnp.bfloat16)


def solution(mesh):
    in_specs = (
        P(("lat", "tok"), None, None),
        P(("lat", "tok"), None),
        P(("lat", "tok")),
        P(None, "lat", "tok"),
        P(None, "tok"),
    )
    out_specs = P(None, "lat", "tok")
    return jax.shard_map(shards, mesh=mesh, in_specs=in_specs, out_specs=out_specs, check_vma=False)
```

profile of v0, /device:TPU:1, one launch (start us, length us, event | category | flops | bytes accessed | tf_op | source)
XLA Modules:
  0.0 292.8 jit_solution(10523026924757773755)
XLA Ops:
  6.5 0.7 copy.14
  7.3 0.8 pad_add_fusion
  8.0 10.3 %all_gather.6 = s32[32,17]{1,0:T(8,128)S(1)} all-gather(s32[8,17]{1,0:T(8,128)S(1)} %pad_add_fusion), channel_id=1, replica_groups=mesh['lat'=64,'tok'=4] {'tok'}, dimensions={0}, use_global_device_ids=true | all-gather | bytes 2720 | tf_op jit(solution)/shard_map/all_gather | solution.py:14
  18.4 0.3 convert_reduce_fusion
  18.7 2.5 scatter_custom_fusion
  21.2 0.7 all_to_all.11
  21.9 15.2 %all-to-all-start = ((s32[64,1,32]{2,1,0:T(1,128)}), s32[64,1,32]{2,1,0:T(1,128)S(1)}, u32[]{:S(2)}, u32[]{:S(2)}) async-start(s32[64,1,32]{2,1,0:T(1,128)} %bitcast.3), calls=%async_computation | async-start | bytes 65536 | tf_op jit(solution)/shard_map/all_to_all | solution.py:50
  37.1 0.2 slice_reduce_fusion
  37.4 9.9 %all_gather.7 = bf16[32,16,128]{2,1,0:T(8,128)(2,1)S(1)} all-gather(bf16[8,16,128]{2,1,0:T(8,128)(2,1)} %param.5), channel_id=1, replica_groups=mesh['lat'=64,'tok'=4] {'tok'}, dimensions={0}, use_global_device_ids=true | all-gather | bytes 163840 | tf_op jit(solution)/shard_map/all_gather | solution.py:22
  47.3 0.1 broadcast_select_fusion
  47.4 2.6 scatter_custom_fusion.1
  50.0 12.6 %all-to-all-start.1 = ((bf16[64,32,128]{2,1,0:T(8,128)(2,1)}), bf16[64,32,128]{2,1,0:T(8,128)(2,1)S(1)}, u32[]{:S(2)}, u32[]{:S(2)}) async-start(bf16[64,32,128]{2,1,0:T(8,128)(2,1)} %bitcast.6), calls=%async_computation.1 | async-start | bytes 1048576 | tf_op jit(solution)/shard_map/all_to_all | solution.py:49
  62.6 0.2 reduce-scatter.2.cloned.1.call-start
  62.9 0.1 iota.27
  63.0 0.5 broadcast.146
  63.5 0.7 reduce.6
  64.4 15.9 %all-to-all-done.1 = bf16[64,32,128]{2,1,0:T(8,128)(2,1)S(1)} async-done(((bf16[64,32,128]{2,1,0:T(8,128)(2,1)}), bf16[64,32,128]{2,1,0:T(8,128)(2,1)S(1)}, u32[]{:S(2)}, u32[]{:S(2)}) %all-to-all-start.1) | async-done | bytes 524320 | tf_op jit(solution)/shard_map/all_to_all | solution.py:49
  80.3 0.2 copy.16
  80.5 4.0 %convolution_bitcast_fusion = f32[64,16,2,1,1280]{4,0,2,1,3:T(8,128)S(1)} fusion(bf16[64,16,2,128]{3,0,2,1:T(8,128)(2,1)S(1)} %bitcast.30, bf16[16,128,1280,1]{2,1,3,0:T(8,128)(2,1)} %bitcast.29), kind=kOutput, calls=%fused_computation.3 | convolution fusion | flops 671088640 | bytes 16252928 | tf_op jit(solution)/shard_map/sbmk,lbkd->sbmld/dot_general | solution.py:53
  84.5 13.0 %copy.17 = f32[64,16,2,1,1280]{4,2,1,0,3:T(2,128)} copy(f32[64,16,2,1,1280]{4,0,2,1,3:T(8,128)S(1)} %convolution_bitcast_fusion) | data formatting | bytes 20971520 | tf_op jit(solution)/shard_map/sbmk,lbkd->sbmld/transpose | solution.py:53
  97.5 13.3 %reshape.203 = f32[2048,1280]{1,0:T(8,128)} reshape(f32[64,16,2,1,1280]{4,2,1,0,3:T(2,128)} %copy.17) | data formatting | bytes 20971520 | tf_op jit(solution)/shard_map/reshape | solution.py:56
  110.8 24.7 %scatter_custom_fusion.2 = f32[2048,1280]{1,0:T(8,128)} fusion(s32[2048]{0:T(1024)S(1)} %bitcast.32, f32[2048,1280]{1,0:T(8,128)} %reshape.203, f32[]{:T(128)} %constant.10.clone.1), kind=kCustom, calls=%fused_computation.4 | custom fusion | flops 2621440 | bytes 10486272 | tf_op jit(solution)/shard_map/scatter-add | solution.py:65
  135.5 148.9 %reduce-scatter.2.cloned.1.call-done = f32[32,1,1280]{2,0,1:T(8,128)} async-done(((f32[2048,1,1280]{2,0,1:T(8,128)}), f32[32,1,1280]{2,0,1:T(8,128)}) %reduce-scatter.2.cloned.1.call-update) | async-done | bytes 163856 | tf_op jit(solution)/shard_map/reduce_scatter | solution.py:64
  284.4 1.6 fusion.5
  (15 shorter events, 0.5 us)
Async XLA Ops:
  21.9 28.1 %all-to-all-start = ((s32[64,1,32]{2,1,0:T(1,128)}), s32[64,1,32]{2,1,0:T(1,128)S(1)}, u32[]{:S(2)}, u32[]{:S(2)}) async-start(s32[64,1,32]{2,1,0:T(1,128)} %bitcast.3), calls=%async_computation | async-start | bytes 65536 | tf_op jit(solution)/shard_map/all_to_all | solution.py:50
  50.0 30.3 %all-to-all-start.1 = ((bf16[64,32,128]{2,1,0:T(8,128)(2,1)}), bf16[64,32,128]{2,1,0:T(8,128)(2,1)S(1)}, u32[]{:S(2)}, u32[]{:S(2)}) async-start(bf16[64,32,128]{2,1,0:T(8,128)(2,1)} %bitcast.6), calls=%async_computation.1 | async-start | bytes 1048576 | tf_op jit(solution)/shard_map/all_to_all | solution.py:49
  62.6 221.8 %reduce-scatter.2.cloned.1.call-start = ((), (), s32[]{:S(2)}) async-start(), calls=%async_computation.3 | async-start | bytes 10649600 | tf_op jit(solution)/shard_map/reduce_scatter | solution.py:64
  110.8 24.7 %copy-start = (f32[1,1280]{1,0:T(1,128)S(1)}, f32[1,1280]{1,0:T(1,128)}, u32[]{:S(2)}) copy-start(f32[1,1280]{1,0:T(1,128)} %param.9) | copy-start | bytes 15364
Sparse Core Ops, SparseCore 0:
  135.6 148.7 reduce-scatter.1
where the time goes:
time: 297 us; the launch traced here: 293 us
  waiting for transfers between devices  165 us (56%)
  local copies, waits for them, and re-layouts  34 us (11%)
  other arithmetic  28.3 us (10%)
  starting transfers between devices  28 us (9%)
  blocking collectives  20.2 us (7%)
  between operations  13.5 us (5%)
  matrix products  4 us (1%)
    reduce_scatter x1, waiting for transfers between devices, shards(): lax.psum_scatter(empty_rows.at[target].add(partial_rows, mode='drop'), 'l...  149 us
    scatter-add x1, other arithmetic, shards(): empty_rows.at[target].add(partial_rows, mode='drop')  24.7 us
    all_to_all x1, waiting for transfers between devices, shards(): lax.all_to_all(outgoing, 'lat', split_axis=0, concat_axis=0, tiled=True)  15.9 us
    all_to_all x1, starting transfers between devices, shards(): lax.all_to_all(token_of, 'lat', split_axis=0, concat_axis=0, tiled=True)  15.2 us
    reshape x1, local copies, waits for them, and re-layouts, shards(): partial_rows = partial_rows.reshape(-1, layers, width_part)  13.3 us
    transpose x1, local copies, waits for them, and re-layouts, shards(): jnp.einsum('sbmk,lbkd->sbmld', incoming, local_blocks, preferred_element_...  13 us
    all_to_all x1, starting transfers between devices, shards(): lax.all_to_all(outgoing, 'lat', split_axis=0, concat_axis=0, tiled=True)  12.6 us
    all_gather x1, blocking collectives, side_by_side(): whole = lax.all_gather(both, axis, axis=dim, tiled=True)  10.3 us
  transfers between devices with their start and end apart: 3, of which 2 were waited for; matrix products, arithmetic and copies ran while one was open for 2% of the time, Pallas kernels for 0%

commit v1 on v0

v1 whole, which is shorter than its diff:
```python
import functools

import jax
import jax.numpy as jnp
from jax import lax
from jax.experimental import pallas as pl
from jax.experimental.pallas import tpu as pltpu
from jax.sharding import Mesh
from jax.sharding import PartitionSpec as P

BLOCK = 128
MOST = 2
NZ, NY, NC, NX = 8, 4, 2, 4
N_LAT = NZ * NY * NC
TOK = 32
OWN = 8
ACTIVE = 16
BLOCKS_DEV = 16
SLOTS = BLOCKS_DEV * MOST
ROWS = SLOTS + 8
CHUNK = 16
CHUNKS = TOK // CHUNK
LIMIT = 32700.0
FLOOR = 2.0**-104
STEP = 256.0
LN2 = 0.6931471805599453

VMEM = pl.BlockSpec(memory_space=pltpu.VMEM)
ANY = pl.BlockSpec(memory_space=pl.ANY)
SMEM = pl.BlockSpec(memory_space=pltpu.SMEM)


def ring(n, k):
    return [(i, (i + k) % n) for i in range(n)]


def column(row):
    return jnp.transpose(jnp.broadcast_to(row, (128, 128)))


def pack_kernel(x_ref, part0, part1, part2, part3, out_ref):
    parts = (part0, part1, part2, part3)
    n_part = OWN * ACTIVE
    ids = []
    for part in parts:
        meta = part[n_part : n_part + 8, :].astype(jnp.float32)
        ids.append(meta[0:1, :] * 32.0 + meta[1:2, :])
    ids_lane = jnp.concatenate(ids, axis=1)
    total = n_part * NX
    count = jnp.zeros((1, total), jnp.float32)
    lane = lax.broadcasted_iota(jnp.int32, (n_part, total), 1)
    sub = lax.broadcasted_iota(jnp.int32, (n_part, total), 0)
    for r in range(NX):
        col = column(ids[r])
        same = jnp.concatenate([col] * NX, axis=1) == ids_lane
        before = sub + r * n_part < lane
        count = count + jnp.sum(jnp.where(same & before, 1.0, 0.0), axis=0, keepdims=True)
    pos = ids_lane * float(MOST) + count
    dst = jnp.floor(pos * (1.0 / SLOTS))
    slot = pos - dst * SLOTS
    dst_row = lax.broadcasted_iota(jnp.int32, (N_LAT, n_part), 0).astype(jnp.float32)
    slot_lane = lax.broadcasted_iota(jnp.int32, (n_part, 128), 1).astype(jnp.float32)
    token = lax.broadcasted_iota(jnp.int32, (n_part, 128), 0) // ACTIVE
    meta = jnp.zeros((N_LAT, 128), jnp.float32)
    for r in range(NX):
        here = slice(r * n_part, (r + 1) * n_part)
        pick = jnp.where(dst[:, here] == dst_row, 1.0, 0.0).astype(jnp.bfloat16)
        first = lax.rem(x_ref[0] - r + NX, NX) * OWN + 1
        named = (token + first).astype(jnp.float32)
        put = jnp.where(column(slot[:, here]) == slot_lane, named, 0.0).astype(jnp.bfloat16)
        meta = meta + jnp.dot(pick, put, preferred_element_type=jnp.float32)
    group = 8
    row = lax.broadcasted_iota(jnp.int32, (group * SLOTS, n_part), 0)
    for g in range(N_LAT // group):
        acc = jnp.zeros((group * SLOTS, BLOCK), jnp.float32)
        at = (row + g * group * SLOTS).astype(jnp.float32)
        for r in range(NX):
            here = slice(r * n_part, (r + 1) * n_part)
            hot = jnp.where(pos[:, here] == at, 1.0, 0.0).astype(jnp.bfloat16)
            acc = acc + jnp.dot(hot, parts[r][0:n_part, :], preferred_element_type=jnp.float32)
        acc = acc.astype(jnp.bfloat16)
        for k in range(group):
            d = g * group + k
            out_ref[d, 0:SLOTS, :] = acc[k * SLOTS : (k + 1) * SLOTS, :]
            out_ref[d, SLOTS:ROWS, :] = jnp.broadcast_to(meta[d : d + 1, :], (8, 128)).astype(
                jnp.bfloat16
            )


def quantized(acc):
    top = jnp.max(jnp.abs(acc), axis=1, keepdims=True)
    top = jnp.maximum(top, FLOOR) * (1.0 / LIMIT)
    code = jnp.ceil(jnp.log(top) * (STEP / LN2))
    scale = jnp.exp(code * (-LN2 / STEP))
    q = jnp.clip(jnp.floor(acc * scale + 0.5), -32767.0, 32767.0)
    return q.astype(jnp.int32).astype(jnp.int16), code


def expand_kernel(
    first, c_ref, own, other, w_own, w_other, out_ref, x_buf, w_buf, tok_buf, coef_buf, sems
):
    depth = w_other.shape[0]
    width = w_other.shape[1]
    at = pl.multiple_of(c_ref[0] * width, 128)
    copies = [
        pltpu.make_async_copy(w_own.at[0, :, pl.ds(at, width)], w_buf.at[0:depth], sems.at[0]),
        pltpu.make_async_copy(w_other, w_buf.at[depth : 2 * depth], sems.at[1]),
    ]
    for copy in copies:
        copy.start()
    for h, ref in enumerate((own, other)):
        meta = jnp.concatenate(
            [ref[s, SLOTS:ROWS, :].astype(jnp.float32)[0:1, :] for s in range(N_LAT)]
            + [jnp.zeros((128 - N_LAT, 128), jnp.float32)],
            axis=0,
        )
        turned = jnp.transpose(meta)
        for s in range(N_LAT):
            tok_buf[s, h * SLOTS : (h + 1) * SLOTS, :] = jnp.broadcast_to(
                turned[0:SLOTS, s : s + 1], (SLOTS, 128)
            )
            coef_buf[s, h * SLOTS : (h + 1) * SLOTS, :] = ref[s, 0:SLOTS, :].astype(jnp.float32)
    t = lax.broadcasted_iota(jnp.int32, (CHUNK, 128), 0).astype(jnp.float32) + float(first + 1)

    def build(s, carry):
        z = s // (NY * NC)
        y = (s // NC) % NY
        c = s % NC
        base = pl.multiple_of(((y * NZ + z) * NC + c) * CHUNK, CHUNK)
        for b in range(2 * BLOCKS_DEV):
            row = jnp.zeros((CHUNK, 128), jnp.float32)
            for m in range(MOST):
                k = b * MOST + m
                hit = jnp.broadcast_to(tok_buf[s, k : k + 1, :], (CHUNK, 128)) == t
                row = jnp.where(
                    hit, jnp.broadcast_to(coef_buf[s, k : k + 1, :], (CHUNK, 128)), row
                )
            x_buf[pl.ds(base, CHUNK), b * BLOCK : (b + 1) * BLOCK] = row.astype(jnp.bfloat16)
        return carry

    lax.fori_loop(0, N_LAT, build, 0)
    for copy in copies:
        copy.wait()
    part = NZ * NC * CHUNK
    for y in range(NY):
        acc = jnp.dot(
            x_buf[y * part : (y + 1) * part, :], w_buf[...], preferred_element_type=jnp.float32
        )
        q, code = quantized(acc)
        out_ref[y, 0:part, :] = q
        for k in range(part // 128):
            lanes = jnp.transpose(jnp.broadcast_to(code[k * 128 : (k + 1) * 128, :], (128, 128)))
            out_ref[y, part : part + 8, k * 128 : (k + 1) * 128] = (
                lanes[0:8, :].astype(jnp.int32).astype(jnp.int16)
            )


def middle_kernel(in_ref, out_ref):
    part = NZ * NC * CHUNK
    width = in_ref.shape[2]
    for k in range(part // 128):
        acc = jnp.zeros((128, width), jnp.float32)
        for y in range(NY):
            code = in_ref[y, part : part + 8, k * 128 : (k + 1) * 128]
            code = code.astype(jnp.int32).astype(jnp.float32)[0:1, :]
            scale = jnp.exp(column(code) * (LN2 / STEP))[:, 0:1]
            q = in_ref[y, k * 128 : (k + 1) * 128, :].astype(jnp.int32).astype(jnp.float32)
            acc = acc + q * scale
        q, code = quantized(acc)
        code = jnp.broadcast_to(code, (128, 128)).astype(jnp.int32).astype(jnp.int16)
        for j in range(128 // CHUNK):
            d = k * (128 // CHUNK) + j
            out_ref[d, :, 0:width] = q[j * CHUNK : (j + 1) * CHUNK, :]
            out_ref[d, :, width : width + 128] = code[j * CHUNK : (j + 1) * CHUNK, :]


def final_kernel(*refs):
    ins, bias, out_ref = refs[:CHUNKS], refs[CHUNKS], refs[CHUNKS + 1]
    width = out_ref.shape[2] // NC
    for k, ref in enumerate(ins):
        for c in range(NC):
            acc = jnp.broadcast_to(bias[:, c * width : (c + 1) * width], (CHUNK, width))
            for z in range(NZ):
                both = ref[z * NC + c].astype(jnp.int32).astype(jnp.float32)
                scale = jnp.exp(both[:, width : width + 1] * (LN2 / STEP))
                acc = acc + both[:, 0:width] * scale
            out_ref[0, k * CHUNK : (k + 1) * CHUNK, c * width : (c + 1) * width] = acc.astype(
                jnp.bfloat16
            )


def shards(coefficients, block_ids, counts, decoder, bias):
    core = lax.axis_index("c").astype(jnp.int32)
    x = lax.axis_index("x").astype(jnp.int32)
    depth, full = decoder.shape[1], decoder.shape[2]
    width = full // NC
    sent = lax.dynamic_slice(decoder[0], (0, (1 - core) * width), (depth, width))
    w_other = lax.ppermute(sent, "c", ring(NC, 1))

    live = lax.broadcasted_iota(jnp.int32, (OWN, ACTIVE), 1) < counts[:, None]
    coeffs = jnp.where(live[:, :, None], coefficients, jnp.zeros((), coefficients.dtype))
    flat = block_ids.reshape(1, OWN * ACTIVE)
    packed = jnp.concatenate(
        [
            coeffs.reshape(OWN * ACTIVE, BLOCK),
            (flat // 32).astype(jnp.bfloat16),
            (flat % 32).astype(jnp.bfloat16),
            jnp.zeros((6, BLOCK), jnp.bfloat16),
        ],
        axis=0,
    )
    parts = [packed] + [lax.ppermute(packed, "x", ring(NX, k)) for k in range(1, NX)]
    outgoing = pl.pallas_call(
        pack_kernel,
        out_shape=jax.ShapeDtypeStruct((N_LAT, ROWS, BLOCK), jnp.bfloat16),
        in_specs=[SMEM] + [VMEM] * NX,
        out_specs=VMEM,
        name="pack",
    )(x.reshape(1), *parts)
    own = lax.all_to_all(outgoing, ("z", "y", "c"), 0, 0, tiled=True)
    other = lax.ppermute(own, "c", ring(NC, 1))

    part = NZ * NC * CHUNK
    arrived = []
    for q in range(CHUNKS):
        sums = pl.pallas_call(
            functools.partial(expand_kernel, q * CHUNK),
            out_shape=jax.ShapeDtypeStruct((NY, part + 8, width), jnp.int16),
            in_specs=[SMEM, VMEM, VMEM, ANY, ANY],
            out_specs=VMEM,
            scratch_shapes=[
                pltpu.VMEM((NY * part, 2 * depth), jnp.bfloat16),
                pltpu.VMEM((2 * depth, width), jnp.bfloat16),
                pltpu.VMEM((N_LAT, 2 * SLOTS, BLOCK), jnp.float32),
                pltpu.VMEM((N_LAT, 2 * SLOTS, BLOCK), jnp.float32),
                pltpu.SemaphoreType.DMA((2,)),
            ],
            compiler_params=pltpu.CompilerParams(vmem_limit_bytes=40 * 1024 * 1024),
            cost_estimate=pl.CostEstimate(
                flops=2 * NY * part * 2 * depth * width,
                bytes_accessed=8 * 1024 * 1024,
                transcendentals=0,
            ),
            name=f"expand{q}",
        )(core.reshape(1), own, other, decoder, w_other)
        crossed = lax.all_to_all(sums, "y", 0, 0, tiled=True)
        halfway = pl.pallas_call(
            middle_kernel,
            out_shape=jax.ShapeDtypeStruct((NZ * NC, CHUNK, width + 128), jnp.int16),
            in_specs=[VMEM],
            out_specs=VMEM,
            name=f"middle{q}",
        )(crossed)
        arrived.append(lax.all_to_all(halfway, ("z", "c"), 0, 0, tiled=True))
    return pl.pallas_call(
        final_kernel,
        out_shape=jax.ShapeDtypeStruct((1, TOK, full), jnp.bfloat16),
        in_specs=[VMEM] * (CHUNKS + 1),
        out_specs=VMEM,
        name="final",
    )(*arrived, bias)


def solution(mesh):
    split = Mesh(mesh.devices.reshape(NZ, NY, NC, NX), ("z", "y", "c", "x"))
    lat = ("z", "y", "c")
    in_specs = (
        P((*lat, "x"), None, None),
        P((*lat, "x"), None),
        P((*lat, "x")),
        P(None, lat, "x"),
        P(None, "x"),
    )
    return jax.shard_map(
        shards, mesh=split, in_specs=in_specs, out_specs=P(None, lat, "x"), check_vma=False
    )
```

time: 297 us -> 152 us (0.51); the launches traced: 293 us -> 151 us
  waiting for transfers between devices: 165 us -> 33.1 us
  Pallas kernels: 0 us -> 35.7 us
  blocking collectives: 20.2 us -> 51.1 us
  other arithmetic: 28.3 us -> 0.26 us
  local copies, waits for them, and re-layouts: 34 us -> 11.2 us
  between operations: 13.5 us -> 0.11 us
  starting transfers between devices: 28 us -> 20 us
  matrix products: 4 us -> 0 us
    reduce_scatter x1 -> x0, waiting for transfers between devices: 149 us -> none  [shards(): lax.psum_scatter(empty_rows.at[target].add(partial_rows, mode='drop'), 'l...]
    all_to_all x0 -> x2, blocking collectives: none -> 51.1 us  [the longest x1 33.3 us: shards(): own = lax.all_to_all(outgoing, ('z', 'y', 'c'), 0, 0, tiled=True)]
    pallas_call x0 -> x6, Pallas kernels: none -> 35.7 us  [the longest x2 25.5 us: shards(): pl.pallas_call(functools.partial(expand_kernel, q * CHUNK), out_shape=jax...]
    scatter-add x1 -> x0, other arithmetic: 24.7 us -> none  [shards(): empty_rows.at[target].add(partial_rows, mode='drop')]
    all_gather x2 -> x0, blocking collectives: 20.2 us -> none  [the longest x1 10.3 us: side_by_side(): whole = lax.all_gather(both, axis, axis=dim, tiled=True)]
    reshape x2 -> x1, local copies, waits for them, and re-layouts: 14 us -> 0.08 us  [shards(): flat = block_ids.reshape(1, OWN * ACTIVE)]
    all_to_all x2 -> x3, starting transfers between devices: 27.8 us -> 14.3 us  [the longest x2 8.07 us: shards(): crossed = lax.all_to_all(sums, 'y', 0, 0, tiled=True)]
    transpose x1 -> x0, local copies, waits for them, and re-layouts: 13 us -> none  [shards(): jnp.einsum('sbmk,lbkd->sbmld', incoming, local_blocks, preferred_element_...]
  transfers between devices with their start and end apart: 3 -> 8, of which waited for: 2 -> 7; matrix products, arithmetic and copies ran while one was open for 2% -> 0% of each run, Pallas kernels for 0% -> 14%
where the time goes in v1:
time: 152 us; the launch traced here: 151 us
  blocking collectives  51.1 us (34%)
  Pallas kernels  35.7 us (23%)
  waiting for transfers between devices  33.1 us (22%)
  starting transfers between devices  20 us (13%)
  local copies, waits for them, and re-layouts  11.2 us (7%)
    all_to_all x1, blocking collectives, shards(): own = lax.all_to_all(outgoing, ('z', 'y', 'c'), 0, 0, tiled=True)  33.3 us
    pallas_call x2, Pallas kernels, shards(): pl.pallas_call(functools.partial(expand_kernel, q * CHUNK), out_shape=jax...  25.5 us
    all_to_all x1, blocking collectives, shards(): arrived.append(lax.all_to_all(halfway, ('z', 'c'), 0, 0, tiled=True))  17.8 us
    all_to_all x2, waiting for transfers between devices, shards(): crossed = lax.all_to_all(sums, 'y', 0, 0, tiled=True)  15.9 us
    all_to_all x1, waiting for transfers between devices, shards(): arrived.append(lax.all_to_all(halfway, ('z', 'c'), 0, 0, tiled=True))  11.7 us
    all_to_all x2, starting transfers between devices, shards(): crossed = lax.all_to_all(sums, 'y', 0, 0, tiled=True)  8.07 us
    unnamed x26, local copies, waits for them, and re-layouts  7.54 us
    all_to_all x1, starting transfers between devices, shards(): arrived.append(lax.all_to_all(halfway, ('z', 'c'), 0, 0, tiled=True))  6.21 us
  transfers between devices with their start and end apart: 8, of which 7 were waited for; matrix products, arithmetic and copies ran while one was open for 0% of the time, Pallas kernels for 14%

profile of v1, /device:TPU:1, one launch (start us, length us, event | category | flops | bytes accessed | tf_op | source)
XLA Modules:
  0.0 151.4 jit_solution(5233630039023735713)
XLA Ops:
  0.0 3.5 %dynamic-slice_bitcast_fusion = bf16[2048,640]{1,0:T(8,128)(2,1)} fusion(bf16[1,2048,1280]{2,1,0:T(8,128)(2,1)} %w_own.3, s32[]{:T(128)S(6)} %select_n.38), kind=kLoop, calls=%fused_computation | loop fusion | bytes 5242884 | tf_op jit(solution)/shard_map/dynamic_slice | solution.py:197
  3.5 3.2 %collective-permute-start.4 = (bf16[2048,640]{1,0:T(8,128)(2,1)}, bf16[2048,640]{1,0:T(8,128)(2,1)S(1)}, u32[]{:S(2)}, u32[]{:S(2)}) collective-permute-start(bf16[2048,640]{1,0:T(8,128)(2,1)} %dynamic-slice_bitcast_fusion), channel_id=1, source_target_pairs={{0,4},{4,0},{1,5},{5,1},{2,6},{6,2},{3,7},{7,3},{8,12},{12,8},{9,1... | collective-permute-start | bytes 7864328 | tf_op jit(solution)/shard_map/ppermute | solution.py:198
  7.2 0.9 collective-permute-start.2
  9.2 0.9 collective-permute-done.2.part3
  10.0 2.3 %collective-permute-done.1.part2 = bf16[136,128]{1,0:T(8,128)(2,1)S(1)} collective-permute-done((bf16[136,128]{1,0:T(8,128)(2,1)S(1)}, bf16[136,128]{1,0:T(8,128)(2,1)S(1)}, u32[]{:S(2)}, u32[]{:S(2)}) %collective-permute-start.1) | collective-permute-done | bytes 34848 | tf_op jit(solution)/shard_map/ppermute | solution.py:212
  13.6 2.6 %pack.1 = bf16[64,40,128]{2,1,0:T(8,128)(2,1)} custom-call(s32[1]{0:T(128)} %bitcast.1.x_ref, bf16[136,128]{1,0:T(8,128)(2,1)} %copy-done.6, bf16[136,128]{1,0:T(8,128)(2,1)} %copy-done.9, bf16[136,128]{1,0:T(8,128)(2,1)} %copy-done.8, bf16[136,128]{1,0:T(8,128)(2,1)} %copy-done.7), custom_call_target="tpu_custom_call" | custom-call | tf_op jit(solution)/shard_map/pack/pallas_call | solution.py:213
  16.2 33.3 %all_to_all.25.own = bf16[64,40,128]{2,1,0:T(8,128)(2,1)S(1)} all-to-all(bf16[64,40,128]{2,1,0:T(8,128)(2,1)} %pack.1), channel_id=1, replica_groups=mesh['z'=8,'y'=4,'c'=2,'x'=4] {'z','y','c'}, dimensions={0} | all-to-all | bytes 1310720 | tf_op jit(solution)/shard_map/all_to_all | solution.py:220
  50.0 1.7 %collective-permute-done.3.other = bf16[64,40,128]{2,1,0:T(8,128)(2,1)S(1)} collective-permute-done((bf16[64,40,128]{2,1,0:T(8,128)(2,1)S(1)}, bf16[64,40,128]{2,1,0:T(8,128)(2,1)S(1)}, u32[]{:S(2)}, u32[]{:S(2)}) %collective-permute-start.3) | collective-permute-done | bytes 655392 | tf_op jit(solution)/shard_map/ppermute | solution.py:221
  51.8 2.5 %copy-done = bf16[1,2048,1280]{2,1,0:T(8,128)(2,1)S(1)} copy-done((bf16[1,2048,1280]{2,1,0:T(8,128)(2,1)S(1)}, bf16[1,2048,1280]{2,1,0:T(8,128)(2,1)}, u32[]{:S(2)}) %copy-start) | copy-done | bytes 5242904
  54.2 12.7 %expand0.1 = s16[4,264,640]{2,1,0:T(8,128)(2,1)} custom-call(s32[1]{0:T(128)} %bitcast.c_ref, bf16[64,40,128]{2,1,0:T(8,128)(2,1)S(1)} %all_to_all.25.own, bf16[64,40,128]{2,1,0:T(8,128)(2,1)S(1)} %collective-permute-done.3.other, bf16[1,2048,1280]{2,1,0:T(8,128)(2,1)S(1)} %copy-done, bf16[2048,640]{1,0:T(8,128)(2,1)S(1)} %collective-permute-done.4.w_other), custom_call_target="tpu_custom_call" | custom-call | flops 5368709120 | bytes 8388608 | tf_op jit(solution)/shard_map/expand0/pallas_call | solution.py:226
  67.0 0.8 copy-done.2
  67.8 4.5 %all-to-all-start.1 = ((s16[4,264,640]{2,1,0:T(8,128)(2,1)}), s16[4,264,640]{2,1,0:T(8,128)(2,1)}, u32[]{:S(2)}, u32[]{:S(2)}) async-start(s16[4,264,640]{2,1,0:T(8,128)(2,1)} %expand0.1), calls=%async_computation.1 | async-start | bytes 2703360 | tf_op jit(solution)/shard_map/all_to_all | solution.py:246
  72.4 2.5 %copy-done.1 = bf16[1,2048,1280]{2,1,0:T(8,128)(2,1)S(1)} copy-done((bf16[1,2048,1280]{2,1,0:T(8,128)(2,1)S(1)}, bf16[1,2048,1280]{2,1,0:T(8,128)(2,1)}, u32[]{:S(2)}) %copy-start.1) | copy-done | bytes 5242904
  74.8 1.1 copy-done.3
  75.9 12.7 %expand1.1 = s16[4,264,640]{2,1,0:T(8,128)(2,1)} custom-call(s32[1]{0:T(128)} %bitcast.c_ref, bf16[64,40,128]{2,1,0:T(8,128)(2,1)S(1)} %all_to_all.25.own, bf16[64,40,128]{2,1,0:T(8,128)(2,1)S(1)} %copy-done.3, bf16[1,2048,1280]{2,1,0:T(8,128)(2,1)S(1)} %copy-done.1, bf16[2048,640]{1,0:T(8,128)(2,1)S(1)} %collective-permute-done.4.w_other), custom_call_target="tpu_custom_call" | custom-call | flops 5368709120 | bytes 8388608 | tf_op jit(solution)/shard_map/expand1/pallas_call | solution.py:226
  88.7 1.6 %all-to-all-done.1.in_ref = s16[4,264,640]{2,1,0:T(8,128)(2,1)} async-done(((s16[4,264,640]{2,1,0:T(8,128)(2,1)}), s16[4,264,640]{2,1,0:T(8,128)(2,1)}, u32[]{:S(2)}, u32[]{:S(2)}) %all-to-all-start.1) | async-done | bytes 1351712 | tf_op jit(solution)/shard_map/all_to_all | solution.py:246
  90.2 3.5 %all-to-all-start.3 = ((s16[4,264,640]{2,1,0:T(8,128)(2,1)}), s16[4,264,640]{2,1,0:T(8,128)(2,1)S(1)}, u32[]{:S(2)}, u32[]{:S(2)}) async-start(s16[4,264,640]{2,1,0:T(8,128)(2,1)} %expand1.1), calls=%async_computation.3 | async-start | bytes 2703360 | tf_op jit(solution)/shard_map/all_to_all | solution.py:246
  93.8 2.8 %middle0.1 = s16[16,16,768]{2,1,0:T(8,128)(2,1)} custom-call(s16[4,264,640]{2,1,0:T(8,128)(2,1)} %all-to-all-done.1.in_ref), custom_call_target="tpu_custom_call" | custom-call | tf_op jit(solution)/shard_map/middle0/pallas_call | solution.py:247
  96.6 14.3 %all-to-all-done.3.in_ref = s16[4,264,640]{2,1,0:T(8,128)(2,1)S(1)} async-done(((s16[4,264,640]{2,1,0:T(8,128)(2,1)}), s16[4,264,640]{2,1,0:T(8,128)(2,1)S(1)}, u32[]{:S(2)}, u32[]{:S(2)}) %all-to-all-start.3) | async-done | bytes 1351712 | tf_op jit(solution)/shard_map/all_to_all | solution.py:246
  111.0 6.2 %all-to-all-start.2 = ((s16[16,16,768]{2,1,0:T(8,128)(2,1)}), s16[16,16,768]{2,1,0:T(8,128)(2,1)S(1)}, u32[]{:S(2)}, u32[]{:S(2)}) async-start(s16[16,16,768]{2,1,0:T(8,128)(2,1)} %middle0.1), calls=%async_computation.2 | async-start | bytes 786432 | tf_op jit(solution)/shard_map/all_to_all | solution.py:254
  117.2 2.8 %middle1.1 = s16[16,16,768]{2,1,0:T(8,128)(2,1)} custom-call(s16[4,264,640]{2,1,0:T(8,128)(2,1)} %copy-done.4), custom_call_target="tpu_custom_call" | custom-call | tf_op jit(solution)/shard_map/middle1/pallas_call | solution.py:247
  120.0 11.7 %all-to-all-done.2.refs_0_ = s16[16,16,768]{2,1,0:T(8,128)(2,1)S(1)} async-done(((s16[16,16,768]{2,1,0:T(8,128)(2,1)}), s16[16,16,768]{2,1,0:T(8,128)(2,1)S(1)}, u32[]{:S(2)}, u32[]{:S(2)}) %all-to-all-start.2) | async-done | bytes 393248 | tf_op jit(solution)/shard_map/all_to_all | solution.py:254
  131.7 17.8 %all_to_all.26.refs_1_ = s16[16,16,768]{2,1,0:T(8,128)(2,1)} all-to-all(s16[16,16,768]{2,1,0:T(8,128)(2,1)} %middle1.1), channel_id=1, replica_groups=mesh['z'=8,'y'=4,'c'=2,'x'=4] {'z','c'}, dimensions={0} | all-to-all | bytes 786432 | tf_op jit(solution)/shard_map/all_to_all | solution.py:254
  149.5 2.0 %final.1 = bf16[1,32,1280]{2,1,0:T(8,128)(2,1)} custom-call(s16[16,16,768]{2,1,0:T(8,128)(2,1)} %copy-done.5, s16[16,16,768]{2,1,0:T(8,128)(2,1)} %all_to_all.26.refs_1_, f32[1,1280]{1,0:T(1,128)} %refs_2_.1), custom_call_target="tpu_custom_call" | custom-call | tf_op jit(solution)/shard_map/final/pallas_call | solution.py:255
  (34 shorter events, 3.4 us)
Async XLA Ops:
  0.0 6.7 %copy-start.11 = (s32[8,16]{1,0:T(8,128)S(1)}, s32[8,16]{1,0:T(8,128)}, u32[]{:S(2)}) copy-start(s32[8,16]{1,0:T(8,128)} %param.6) | copy-start | bytes 1540
  0.0 6.9 %copy-start.12 = (s32[8]{0:T(128)S(1)}, s32[8]{0:T(128)}, u32[]{:S(2)}) copy-start(s32[8]{0:T(128)} %param.7) | copy-start | bytes 100
  0.0 7.0 %copy-start.10 = (bf16[8,16,128]{2,1,0:T(8,128)(2,1)S(1)}, bf16[8,16,128]{2,1,0:T(8,128)(2,1)}, u32[]{:S(2)}) copy-start(bf16[8,16,128]{2,1,0:T(8,128)(2,1)} %param.5) | copy-start | bytes 98308
  3.5 48.2 %collective-permute-start.4 = (bf16[2048,640]{1,0:T(8,128)(2,1)}, bf16[2048,640]{1,0:T(8,128)(2,1)S(1)}, u32[]{:S(2)}, u32[]{:S(2)}) collective-permute-start(bf16[2048,640]{1,0:T(8,128)(2,1)} %dynamic-slice_bitcast_fusion), channel_id=1, source_target_pairs={{0,4},{4,0},{1,5},{5,1},{2,6},{6,2},{3,7},{7,3},{8,12},{12,8},{9,1... | collective-permute-start | bytes 7864328 | tf_op jit(solution)/shard_map/ppermute | solution.py:198
  7.2 5.8 %copy-start.6 = (bf16[136,128]{1,0:T(8,128)(2,1)}, bf16[136,128]{1,0:T(8,128)(2,1)S(1)}, u32[]{:S(2)}) copy-start(bf16[136,128]{1,0:T(8,128)(2,1)S(1)} %maximum_maximum_fusion.part0) | copy-start | bytes 104452
  7.2 2.9 %collective-permute-start.2 = (bf16[136,128]{1,0:T(8,128)(2,1)S(1)}, bf16[136,128]{1,0:T(8,128)(2,1)S(1)}, u32[]{:S(2)}, u32[]{:S(2)}) collective-permute-start(bf16[136,128]{1,0:T(8,128)(2,1)S(1)} %maximum_maximum_fusion.part0), channel_id=1, source_target_pairs={{0,3},{1,0},{2,1},{3,2},{4,7},{5,4},{6,5},{7,6},{8,11},{9,8},{10,9... | collective-permute-start | bytes 104456 | tf_op jit(solution)/shard_map/ppermute | solution.py:212
  8.0 4.3 %collective-permute-start.1 = (bf16[136,128]{1,0:T(8,128)(2,1)S(1)}, bf16[136,128]{1,0:T(8,128)(2,1)S(1)}, u32[]{:S(2)}, u32[]{:S(2)}) collective-permute-start(bf16[136,128]{1,0:T(8,128)(2,1)S(1)} %maximum_maximum_fusion.part0), channel_id=1, source_target_pairs={{0,2},{1,3},{2,0},{3,1},{4,6},{5,7},{6,4},{7,5},{8,10},{9,11},{10,... | collective-permute-start | bytes 104456 | tf_op jit(solution)/shard_map/ppermute | solution.py:212
  8.6 4.4 %collective-permute-start = (bf16[136,128]{1,0:T(8,128)(2,1)S(1)}, bf16[136,128]{1,0:T(8,128)(2,1)S(1)}, u32[]{:S(2)}, u32[]{:S(2)}) collective-permute-start(bf16[136,128]{1,0:T(8,128)(2,1)S(1)} %maximum_maximum_fusion.part0), channel_id=1, source_target_pairs={{0,1},{1,2},{2,3},{3,0},{4,5},{5,6},{6,7},{7,4},{8,9},{9,10},{10,1... | collective-permute-start | bytes 104456 | tf_op jit(solution)/shard_map/ppermute | solution.py:212
  10.0 3.0 %copy-start.7 = (bf16[136,128]{1,0:T(8,128)(2,1)}, bf16[136,128]{1,0:T(8,128)(2,1)S(1)}, u32[]{:S(2)}) copy-start(bf16[136,128]{1,0:T(8,128)(2,1)S(1)} %collective-permute-done.2.part3) | copy-start | bytes 104452
  12.3 0.7 copy-start.8
  13.0 0.6 copy-start.9
  49.5 2.3 %collective-permute-start.3 = (bf16[64,40,128]{2,1,0:T(8,128)(2,1)S(1)}, bf16[64,40,128]{2,1,0:T(8,128)(2,1)S(1)}, u32[]{:S(2)}, u32[]{:S(2)}) collective-permute-start(bf16[64,40,128]{2,1,0:T(8,128)(2,1)S(1)} %all_to_all.25.own), channel_id=1, source_target_pairs={{0,4},{4,0},{1,5},{5,1},{2,6},{6,2},{3,7},{7,3},{8,12},{12,8},{9,1... | collective-permute-start | bytes 1966088 | tf_op jit(solution)/shard_map/ppermute | solution.py:221
  51.8 2.5 %copy-start = (bf16[1,2048,1280]{2,1,0:T(8,128)(2,1)S(1)}, bf16[1,2048,1280]{2,1,0:T(8,128)(2,1)}, u32[]{:S(2)}) copy-start(bf16[1,2048,1280]{2,1,0:T(8,128)(2,1)} %w_own.3) | copy-start | bytes 15728644
  67.0 0.8 copy-start.2
  67.8 22.4 %all-to-all-start.1 = ((s16[4,264,640]{2,1,0:T(8,128)(2,1)}), s16[4,264,640]{2,1,0:T(8,128)(2,1)}, u32[]{:S(2)}, u32[]{:S(2)}) async-start(s16[4,264,640]{2,1,0:T(8,128)(2,1)} %expand0.1), calls=%async_computation.1 | async-start | bytes 2703360 | tf_op jit(solution)/shard_map/all_to_all | solution.py:246
  72.3 2.5 %copy-start.1 = (bf16[1,2048,1280]{2,1,0:T(8,128)(2,1)S(1)}, bf16[1,2048,1280]{2,1,0:T(8,128)(2,1)}, u32[]{:S(2)}) copy-start(bf16[1,2048,1280]{2,1,0:T(8,128)(2,1)} %w_own.3) | copy-start | bytes 15728644
  74.8 1.1 copy-start.3
  90.2 20.7 %all-to-all-start.3 = ((s16[4,264,640]{2,1,0:T(8,128)(2,1)}), s16[4,264,640]{2,1,0:T(8,128)(2,1)S(1)}, u32[]{:S(2)}, u32[]{:S(2)}) async-start(s16[4,264,640]{2,1,0:T(8,128)(2,1)} %expand1.1), calls=%async_computation.3 | async-start | bytes 2703360 | tf_op jit(solution)/shard_map/all_to_all | solution.py:246
  111.0 6.2 %copy-start.4 = (s16[4,264,640]{2,1,0:T(8,128)(2,1)}, s16[4,264,640]{2,1,0:T(8,128)(2,1)S(1)}, u32[]{:S(2)}) copy-start(s16[4,264,640]{2,1,0:T(8,128)(2,1)S(1)} %all-to-all-done.3.in_ref) | copy-start | bytes 4055044
  111.0 20.7 %all-to-all-start.2 = ((s16[16,16,768]{2,1,0:T(8,128)(2,1)}), s16[16,16,768]{2,1,0:T(8,128)(2,1)S(1)}, u32[]{:S(2)}, u32[]{:S(2)}) async-start(s16[16,16,768]{2,1,0:T(8,128)(2,1)} %middle0.1), calls=%async_computation.2 | async-start | bytes 786432 | tf_op jit(solution)/shard_map/all_to_all | solution.py:254
  131.7 17.8 %copy-start.5 = (s16[16,16,768]{2,1,0:T(8,128)(2,1)}, s16[16,16,768]{2,1,0:T(8,128)(2,1)S(1)}, u32[]{:S(2)}) copy-start(s16[16,16,768]{2,1,0:T(8,128)(2,1)S(1)} %all-to-all-done.2.refs_0_) | copy-start | bytes 1179652

commit v2 on v1

v2 whole, which is shorter than its diff:
```python
import functools

import jax
import jax.numpy as jnp
from jax import lax
from jax.experimental import pallas as pl
from jax.experimental.pallas import tpu as pltpu
from jax.sharding import Mesh
from jax.sharding import PartitionSpec as P


BLOCK = 128
MOST = 2
NZ, NY, NC, NX = 8, 4, 2, 4
CHIPS = NZ * NY
TOK = 32
OWN = 8
ACTIVE = 16
BLOCKS_DEV = 16
BLOCKS_CHIP = BLOCKS_DEV * NC
HALF = BLOCKS_DEV * MOST
SLOTS = BLOCKS_CHIP * MOST
ROWS = SLOTS + 8
CHUNK = 16
CHUNKS = TOK // CHUNK
PART = NZ // 2 * NC * CHUNK
LIMIT = 32700.0
FLOOR = 2.0**-104
STEP = 256.0
LN2 = 0.6931471805599453
MIB = 1024 * 1024

VMEM = pl.BlockSpec(memory_space=pltpu.VMEM)
SMEM = pl.BlockSpec(memory_space=pltpu.SMEM)
HBM = pl.BlockSpec(memory_space=pltpu.HBM)
ANY = pl.BlockSpec(memory_space=pl.ANY)
PIECES = 2
GRANT = 48


def ring(n, k):
    return [(i, (i + k) % n) for i in range(n)]


def call(kernel, out_shape, in_specs, mib, flops=0, scratch=()):
    return pl.pallas_call(
        kernel,
        out_shape=out_shape,
        in_specs=in_specs,
        out_specs=jax.tree.map(lambda _: VMEM, out_shape),
        scratch_shapes=list(scratch),
        compiler_params=pltpu.CompilerParams(vmem_limit_bytes=mib * MIB),
        cost_estimate=pl.CostEstimate(flops=flops, bytes_accessed=2 * MIB, transcendentals=0),
    )


def column(row):
    return jnp.transpose(jnp.broadcast_to(row, (128, 128)))


def pack_kernel(info, part0, part1, part2, part3, out_ref):
    parts = (part0, part1, part2, part3)
    n_part = OWN * ACTIVE
    ids = []
    for part in parts:
        meta = part[n_part : n_part + 8, :].astype(jnp.float32)
        ids.append(meta[0:1, :] * 32.0 + meta[1:2, :])
    ids_lane = jnp.concatenate(ids, axis=1)
    total = n_part * NX
    count = jnp.zeros((1, total), jnp.float32)
    lane = lax.broadcasted_iota(jnp.int32, (n_part, total), 1)
    sub = lax.broadcasted_iota(jnp.int32, (n_part, total), 0)
    for r in range(NX):
        col = column(ids[r])
        same = jnp.concatenate([col] * NX, axis=1) == ids_lane
        before = sub + r * n_part < lane
        count = count + jnp.sum(jnp.where(same & before, 1.0, 0.0), axis=0, keepdims=True)
    pos = ids_lane * float(MOST) + count
    dst = jnp.floor(pos * (1.0 / SLOTS))
    slot = pos - dst * SLOTS
    dst_row = lax.broadcasted_iota(jnp.int32, (CHIPS, n_part), 0).astype(jnp.float32)
    slot_lane = lax.broadcasted_iota(jnp.int32, (n_part, 128), 1).astype(jnp.float32)
    token = lax.broadcasted_iota(jnp.int32, (n_part, 128), 0) // ACTIVE
    meta = jnp.zeros((CHIPS, 128), jnp.float32)
    for r in range(NX):
        here = slice(r * n_part, (r + 1) * n_part)
        pick = jnp.where(dst[:, here] == dst_row, 1.0, 0.0).astype(jnp.bfloat16)
        first = lax.rem(info[0] - r + NX, NX) * OWN + 1
        named = (token + first).astype(jnp.float32)
        put = jnp.where(column(slot[:, here]) == slot_lane, named, 0.0).astype(jnp.bfloat16)
        meta = meta + jnp.dot(pick, put, preferred_element_type=jnp.float32)
    group = 4
    row = lax.broadcasted_iota(jnp.int32, (group * SLOTS, n_part), 0)
    for g in range(CHIPS // group):
        acc = jnp.zeros((group * SLOTS, BLOCK), jnp.float32)
        at = (row + g * group * SLOTS).astype(jnp.float32)
        for r in range(NX):
            here = slice(r * n_part, (r + 1) * n_part)
            hot = jnp.where(pos[:, here] == at, 1.0, 0.0).astype(jnp.bfloat16)
            acc = acc + jnp.dot(hot, parts[r][0:n_part, :], preferred_element_type=jnp.float32)
        acc = acc.astype(jnp.bfloat16)
        for k in range(group):
            d = g * group + k
            out_ref[d, 0:SLOTS, :] = acc[k * SLOTS : (k + 1) * SLOTS, :]
            out_ref[d, SLOTS:ROWS, :] = jnp.broadcast_to(meta[d : d + 1, :], (8, 128)).astype(
                jnp.bfloat16
            )


def prepare_kernel(info, own, other, tok_ref, coef_ref):
    core = info[0]
    sources = (own, other)
    meta = jnp.concatenate(
        [
            ref[s, SLOTS:ROWS, :].astype(jnp.float32)[0:1, :]
            for ref in sources
            for s in range(CHIPS)
        ]
        + [jnp.zeros((128 - 2 * CHIPS, 128), jnp.float32)],
        axis=0,
    )
    turned = jnp.transpose(meta)
    for n in range(2 * CHIPS):
        ref, s = sources[n // CHIPS], n % CHIPS
        for h in range(NC):
            to = pl.ds(pl.multiple_of(lax.rem(core + h, NC) * HALF, HALF), HALF)
            here = slice(h * HALF, (h + 1) * HALF)
            tok_ref[n, to, :] = jnp.broadcast_to(turned[here, n : n + 1], (HALF, 128))
            coef_ref[n, to, :] = ref[s, here, :].astype(jnp.float32)


def quantized(acc):
    top = jnp.max(jnp.abs(acc), axis=1, keepdims=True)
    top = jnp.maximum(top, FLOOR) * (1.0 / LIMIT)
    code = jnp.ceil(jnp.log(top) * (STEP / LN2))
    scale = jnp.exp(code * (-LN2 / STEP))
    q = jnp.clip(jnp.floor(acc * scale + 0.5), -32767.0, 32767.0)
    return q.astype(jnp.int32).astype(jnp.int16), code


def write_message(out_ref, acc):
    n = acc.shape[0]
    q, code = quantized(acc)
    out_ref[0:n, :] = q
    for k in range(n // 128):
        lanes = jnp.transpose(jnp.broadcast_to(code[k * 128 : (k + 1) * 128, :], (128, 128)))
        out_ref[n : n + 8, k * 128 : (k + 1) * 128] = (
            lanes[0:8, :].astype(jnp.int32).astype(jnp.int16)
        )


def read_message(ref, k):
    n = ref.shape[0] - 8
    code = ref[n : n + 8, k * 128 : (k + 1) * 128]
    code = code.astype(jnp.int32).astype(jnp.float32)[0:1, :]
    scale = jnp.exp(column(code) * (LN2 / STEP))[:, 0:1]
    return ref[k * 128 : (k + 1) * 128, :].astype(jnp.int32).astype(jnp.float32) * scale


def expand_kernel(first, send, info, tok, coef, w_own, w_other, after, *rest):
    outs, (x_buf, w_buf, acc, sems) = rest[:-4], rest[-4:]
    depth = w_own.shape[1]
    width = w_buf.shape[1]
    core = info[0]
    columns = pl.ds(pl.multiple_of(core * width, 128), width)
    deep = depth // PIECES
    copies = []
    for g in range(NC * PIECES):
        ref = (w_own, w_other)[g // PIECES]
        k = g % PIECES
        copies.append(
            pltpu.make_async_copy(
                ref.at[0, k * deep : (k + 1) * deep, columns],
                w_buf.at[g * deep : (g + 1) * deep],
                sems.at[g],
            )
        )
    for copy in copies:
        copy.start()
    t = lax.broadcasted_iota(jnp.int32, (CHUNK, 128), 0).astype(jnp.float32) + float(first + 1)
    blocks = BLOCKS_CHIP // (NC * PIECES)
    for g, copy in enumerate(copies):

        def build(i, carry, g=g):
            h, j, z, c = i // 16, (i // 8) % 2, (i // 2) % 4, i % 2
            n = lax.rem(c + core, NC) * CHIPS + (h * 4 + z) * NY + info[1 + h * 2 + j]
            base = pl.multiple_of(i * CHUNK, CHUNK)
            for b in range(g * blocks, (g + 1) * blocks):
                row = jnp.zeros((CHUNK, 128), jnp.float32)
                for m in range(MOST):
                    k = b * MOST + m
                    hit = jnp.broadcast_to(tok[n, k : k + 1, :], (CHUNK, 128)) == t
                    row = jnp.where(
                        hit, jnp.broadcast_to(coef[n, k : k + 1, :], (CHUNK, 128)), row
                    )
                x_buf[pl.ds(base, CHUNK), b * BLOCK : (b + 1) * BLOCK] = row.astype(jnp.bfloat16)
            return carry

        lax.fori_loop(0, 4 * PART // CHUNK, build, 0)
        copy.wait()
        here = slice(g * deep, (g + 1) * deep)
        term = jnp.dot(x_buf[:, here], w_buf[here, :], preferred_element_type=jnp.float32)
        if g == 0:
            acc[...] = term
        elif send or g < NC * PIECES - 1:
            acc[...] += term
        else:
            outs[0][...] = acc[...] + term
    if send:
        for h in range(2):
            write_message(outs[h], acc[h * 2 * PART : (h + 1) * 2 * PART, :])


def middle_kernel(kept, in0, in1, after, keep_ref, out0, out1):
    for h, (ref, out) in enumerate(((in0, out0), (in1, out1))):
        keep_ref[h * PART : (h + 1) * PART, :] = kept[
            2 * h * PART : (2 * h + 1) * PART, :
        ] + read_message(ref, 0)
        write_message(
            out, kept[(2 * h + 1) * PART : (2 * h + 2) * PART, :] + read_message(ref, 1)
        )


def last_kernel(*refs):
    ins, out_ref = refs[:-1], refs[-1]
    width = ins[0].shape[1]
    for q in range(CHUNKS):
        kept, messages = ins[3 * q], ins[3 * q + 1 : 3 * q + 3]
        for h, ref in enumerate(messages):
            acc = kept[h * PART : (h + 1) * PART, :] + read_message(ref, 0)
            v, code = quantized(acc)
            code = jnp.broadcast_to(code, (PART, 128)).astype(jnp.int32).astype(jnp.int16)
            for j in range(PART // CHUNK):
                d = h * (PART // CHUNK) + j
                at, here = slice(q * CHUNK, (q + 1) * CHUNK), slice(j * CHUNK, (j + 1) * CHUNK)
                out_ref[d, at, 0:width] = v[here, :]
                out_ref[d, at, width : width + 128] = code[here, :]


def final_kernel(ref, bias, out_ref):
    width = out_ref.shape[2] // NC
    for c in range(NC):
        acc = jnp.broadcast_to(bias[:, c * width : (c + 1) * width], (TOK, width))
        for z in range(NZ):
            both = ref[z * NC + c].astype(jnp.int32).astype(jnp.float32)
            scale = jnp.exp(both[:, width : width + 1] * (LN2 / STEP))
            acc = acc + both[:, 0:width] * scale
        out_ref[0, :, c * width : (c + 1) * width] = acc.astype(jnp.bfloat16)


def run(coefficients, block_ids, counts, decoder, bias):
    core = lax.axis_index("c").astype(jnp.int32)
    x = lax.axis_index("x").astype(jnp.int32)
    y = lax.axis_index("y").astype(jnp.int32)
    depth, full = decoder.shape[1], decoder.shape[2]
    width = full // NC
    w_other = lax.ppermute(decoder, "c", ring(NC, 1))

    live = lax.broadcasted_iota(jnp.int32, (OWN, ACTIVE), 1) < counts[:, None]
    coeffs = jnp.where(live[:, :, None], coefficients, jnp.zeros((), coefficients.dtype))
    flat = block_ids.reshape(1, OWN * ACTIVE)
    packed = jnp.concatenate(
        [
            coeffs.reshape(OWN * ACTIVE, BLOCK),
            (flat // 32).astype(jnp.bfloat16),
            (flat % 32).astype(jnp.bfloat16),
            jnp.zeros((6, BLOCK), jnp.bfloat16),
        ],
        axis=0,
    )
    parts = [packed] + [lax.ppermute(packed, "x", ring(NX, k)) for k in range(1, NX)]
    shape = jax.ShapeDtypeStruct
    outgoing = call(
        pack_kernel, shape((CHIPS, ROWS, BLOCK), jnp.bfloat16), [SMEM] + [VMEM] * NX, 10
    )(x.reshape(1), *parts)
    own = lax.all_to_all(outgoing, ("z", "y"), 0, 0, tiled=True)
    other = lax.ppermute(own, "c", ring(NC, 1))
    slots = shape((2 * CHIPS, SLOTS, BLOCK), jnp.float32)
    tok, coef = call(prepare_kernel, [slots, slots], [SMEM, VMEM, VMEM], 10)(
        core.reshape(1), own, other
    )

    pair_a, pair_b = [(i, i ^ 1) for i in range(NY)], [(i, NY - 1 - i) for i in range(NY)]
    a, b = y ^ 1, NY - 1 - y
    opposite = NY - 1 - a
    sent_to = jnp.stack([core, a, opposite, b, opposite])
    kept_for = jnp.stack([core, y, b, y, a])
    message = shape((2 * PART + 8, width), jnp.int16)
    small = shape((PART + 8, width), jnp.int16)

    def expand(q, send, after):
        return call(
            functools.partial(expand_kernel, q * CHUNK, send),
            [message, message] if send else [shape((4 * PART, width), jnp.float32)],
            [SMEM, VMEM, VMEM, HBM, HBM, ANY],
            GRANT,
            flops=2 * 4 * PART * 2 * depth * width,
            scratch=[
                pltpu.VMEM((4 * PART, 2 * depth), jnp.bfloat16),
                pltpu.VMEM((2 * depth, width), jnp.bfloat16),
                pltpu.VMEM((4 * PART, width), jnp.float32),
                pltpu.SemaphoreType.DMA((NC * PIECES,)),
            ],
        )(sent_to if send else kept_for, tok, coef, decoder, w_other, after)

    after = own
    crossing = []
    for q in range(CHUNKS):
        m0, m1 = expand(q, True, after)
        after = m0
        crossing.append((lax.ppermute(m0, "y", pair_a), lax.ppermute(m1, "y", pair_b)))
    arrived = []
    for q in range(CHUNKS):
        (kept,) = expand(q, False, after)
        kept, m0, m1 = call(
            middle_kernel,
            [shape((2 * PART, width), jnp.float32), small, small],
            [VMEM] * 3 + [ANY],
            10,
        )(kept, *crossing[q], after)
        after = m0
        m0 = lax.ppermute(m0, "y", pair_b)
        m1 = lax.ppermute(m1, "y", pair_a)
        arrived += [kept, m0, m1]
    out = call(
        last_kernel, shape((NZ * NC, TOK, width + 128), jnp.int16), [VMEM] * 3 * CHUNKS, 10
    )(*arrived)
    return call(
        final_kernel, shape((1, TOK, full), jnp.bfloat16), [VMEM] * 2, 10
    )(lax.all_to_all(out, ("z", "c"), 0, 0, tiled=True), bias)


def solution(mesh):
    split = Mesh(mesh.devices.reshape(NZ, NY, NC, NX), ("z", "y", "c", "x"))
    lat = ("z", "y", "c")
    in_specs = (
        P((*lat, "x"), None, None),
        P((*lat, "x"), None),
        P((*lat, "x")),
        P(None, lat, "x"),
        P(None, "x"),
    )
    return jax.shard_map(
        run, mesh=split, in_specs=in_specs, out_specs=P(None, lat, "x"), check_vma=False
    )
```

time: 152 us -> 134 us (0.88)
  waiting for transfers between devices: 33.1 us -> 10.1 us
  Pallas kernels: 35.7 us -> 47.5 us
  local copies, waits for them, and re-layouts: 11.2 us -> 1.02 us
  blocking collectives: 51.1 us -> 55.3 us
  starting transfers between devices: 20 us -> 17.9 us
    all_to_all x3 -> x0, waiting for transfers between devices: 27.6 us -> none  [the longest x2 15.9 us: shards(): crossed = lax.all_to_all(sums, 'y', 0, 0, tiled=True)]
    all_to_all x3 -> x0, starting transfers between devices: 14.3 us -> none  [the longest x2 8.07 us: shards(): crossed = lax.all_to_all(sums, 'y', 0, 0, tiled=True)]
    ppermute x5 -> x13, starting transfers between devices: 5.72 us -> 17.9 us  [the longest x1 3.5 us: run(): other = lax.ppermute(own, 'c', ring(NC, 1))]
    pallas_call x6 -> x10, Pallas kernels: 35.7 us -> 47.5 us  [the longest x4 43 us: expand(): call(functools.partial(expand_kernel, q * CHUNK, send), [message, message...]
    unnamed x26 -> x2, local copies, waits for them, and re-layouts: 7.54 us -> 0.01 us
    ppermute x5 -> x13, waiting for transfers between devices: 5.55 us -> 10.1 us  [the longest x2 3.33 us: run(): m1 = lax.ppermute(m1, 'y', pair_a)]
    all_to_all x2, blocking collectives: 51.1 us -> 55.3 us  [the longest x1 28.1 us: run(): lax.all_to_all(out, ('z', 'c'), 0, 0, tiled=True)]
    dynamic_slice x1 -> x0, local copies, waits for them, and re-layouts: 3.51 us -> none  [shards(): lax.dynamic_slice(decoder[0], (0, (1 - core) * width), (depth, width))]
  transfers between devices with their start and end apart: 8 -> 13, of which waited for: 7 -> 6; matrix products, arithmetic and copies ran while one was open for 0% -> 2% of each run, Pallas kernels for 14% -> 26%
where the time goes in v2:
time: 134 us
  blocking collectives  55.3 us (41%)
  Pallas kernels  47.5 us (35%)
  starting transfers between devices  17.9 us (13%)
  waiting for transfers between devices  10.1 us (8%)
  other arithmetic  1.67 us (1%)
    pallas_call x4, Pallas kernels, expand(): call(functools.partial(expand_kernel, q * CHUNK, send), [message, message...  43 us
    all_to_all x1, blocking collectives, run(): lax.all_to_all(out, ('z', 'c'), 0, 0, tiled=True)  28.1 us
    all_to_all x1, blocking collectives, run(): own = lax.all_to_all(outgoing, ('z', 'y'), 0, 0, tiled=True)  27.2 us
    ppermute x1, starting transfers between devices, run(): other = lax.ppermute(own, 'c', ring(NC, 1))  3.5 us
    ppermute x2, waiting for transfers between devices, run(): m1 = lax.ppermute(m1, 'y', pair_a)  3.33 us
    ppermute x1, starting transfers between devices, run(): w_other = lax.ppermute(decoder, 'c', ring(NC, 1))  3.2 us
    ppermute x3, starting transfers between devices, run(): lax.ppermute(packed, 'x', ring(NX, k))  3.18 us
    ppermute x2, waiting for transfers between devices, run(): m0 = lax.ppermute(m0, 'y', pair_b)  3.14 us
  transfers between devices with their start and end apart: 13, of which 6 were waited for; matrix products, arithmetic and copies ran while one was open for 2% of the time, Pallas kernels for 26%

profile of v2, /device:TPU:1, one launch (start us, length us, event | category | flops | bytes accessed | tf_op | source)
XLA Modules:
  0.0 133.7 jit_solution(12841616122243761039)
XLA Ops:
  0.0 3.2 %collective-permute-start.4 = (bf16[1,2048,1280]{2,1,0:T(8,128)(2,1)}, bf16[1,2048,1280]{2,1,0:T(8,128)(2,1)}, u32[]{:S(2)}, u32[]{:S(2)}) collective-permute-start(bf16[1,2048,1280]{2,1,0:T(8,128)(2,1)} %w_own.7), channel_id=1, source_target_pairs={{0,4},{4,0},{1,5},{5,1},{2,6},{6,2},{3,7},{7,3},{8,12},{12,8},{9,1... | collective-permute-start | bytes 15728648 | tf_op jit(solution)/shard_map/ppermute | solution.py:257
  4.8 0.8 broadcast_select_fusion
  5.8 1.9 %collective-permute-start.1 = (bf16[136,128]{1,0:T(8,128)(2,1)S(1)}, bf16[136,128]{1,0:T(8,128)(2,1)S(1)}, u32[]{:S(2)}, u32[]{:S(2)}) collective-permute-start(bf16[136,128]{1,0:T(8,128)(2,1)S(1)} %maximum_maximum_fusion.part0), channel_id=1, source_target_pairs={{0,2},{1,3},{2,0},{3,1},{4,6},{5,7},{6,4},{7,5},{8,10},{9,11},{10,... | collective-permute-start | bytes 104456 | tf_op jit(solution)/shard_map/ppermute | solution.py:271
  7.8 1.2 collective-permute-start.2
  8.9 0.9 collective-permute-done.part1
  10.2 0.8 collective-permute-done.2.part3
  11.1 0.9 shard_map.55
  12.0 27.2 %all_to_all.10.own.after = bf16[32,72,128]{2,1,0:T(8,128)(2,1)S(1)} all-to-all(bf16[32,72,128]{2,1,0:T(8,128)(2,1)S(1)} %shard_map.55), channel_id=1, replica_groups=mesh['z'=8,'y'=4,'c'=2,'x'=4] {'z','y'}, dimensions={0} | all-to-all | bytes 1179648 | tf_op jit(solution)/shard_map/all_to_all | solution.py:276
  39.2 3.5 %collective-permute-start.3 = (bf16[32,72,128]{2,1,0:T(8,128)(2,1)S(1)}, bf16[32,72,128]{2,1,0:T(8,128)(2,1)S(1)}, u32[]{:S(2)}, u32[]{:S(2)}) collective-permute-start(bf16[32,72,128]{2,1,0:T(8,128)(2,1)S(1)} %all_to_all.10.own.after), channel_id=1, source_target_pairs={{0,4},{4,0},{1,5},{5,1},{2,6},{6,2},{3,7},{7,3},{8,12},{12,8},{9,1... | collective-permute-start | bytes 1769480 | tf_op jit(solution)/shard_map/ppermute | solution.py:277
  42.8 1.5 %collective-permute-done.3.other = bf16[32,72,128]{2,1,0:T(8,128)(2,1)S(1)} collective-permute-done((bf16[32,72,128]{2,1,0:T(8,128)(2,1)S(1)}, bf16[32,72,128]{2,1,0:T(8,128)(2,1)S(1)}, u32[]{:S(2)}, u32[]{:S(2)}) %collective-permute-start.3) | collective-permute-done | bytes 589856 | tf_op jit(solution)/shard_map/ppermute | solution.py:277
  44.9 10.9 %shard_map.57 = (s16[264,640]{1,0:T(8,128)(2,1)S(1)}, s16[264,640]{1,0:T(8,128)(2,1)S(1)}) custom-call(s32[5]{0:T(128)S(1)} %stack.32.info, f32[64,64,128]{2,1,0:T(8,128)S(1)} %get-tuple-element.17.tok, f32[64,64,128]{2,1,0:T(8,128)S(1)} %get-tuple-element.18.coef, bf16[1,2048,1280]{2,1,0:T(8,128)(2,1)} %w_own.7, ...), custom_call_target="tpu_custom_call" | custom-call | flops 2684354560 | bytes 2097152 | tf_op jit(solution)/shard_map/pallas_call | solution.py:292
  56.6 1.8 %collective-permute-start.6 = (s16[264,640]{1,0:T(8,128)(2,1)S(1)}, s16[264,640]{1,0:T(8,128)(2,1)S(1)}, u32[]{:S(2)}, u32[]{:S(2)}) collective-permute-start(s16[264,640]{1,0:T(8,128)(2,1)S(1)} %get-tuple-element.21), channel_id=1, source_target_pairs={{0,24},{8,16},{16,8},{24,0},{1,25},{9,17},{17,9},{25,1},{2,26},{10... | collective-permute-start | bytes 1013768 | tf_op jit(solution)/shard_map/ppermute | solution.py:311
  58.4 10.9 %shard_map.58 = (s16[264,640]{1,0:T(8,128)(2,1)S(1)}, s16[264,640]{1,0:T(8,128)(2,1)S(1)}) custom-call(s32[5]{0:T(128)S(1)} %stack.32.info, f32[64,64,128]{2,1,0:T(8,128)S(1)} %get-tuple-element.17.tok, f32[64,64,128]{2,1,0:T(8,128)S(1)} %get-tuple-element.18.coef, bf16[1,2048,1280]{2,1,0:T(8,128)(2,1)} %w_own.7, ...), custom_call_target="tpu_custom_call" | custom-call | flops 2684354560 | bytes 2097152 | tf_op jit(solution)/shard_map/pallas_call | solution.py:292
  69.3 1.0 collective-permute-start.10
  70.3 10.6 %shard_map.59.kept = f32[512,640]{1,0:T(8,128)S(1)} custom-call(s32[5]{0:T(128)S(1)} %stack.30.info, f32[64,64,128]{2,1,0:T(8,128)S(1)} %get-tuple-element.17.tok, f32[64,64,128]{2,1,0:T(8,128)S(1)} %get-tuple-element.18.coef, bf16[1,2048,1280]{2,1,0:T(8,128)(2,1)} %w_own.7, bf16[1,2048,1280]{2,1,0:T(8,128)(2,1)} %collective-permute-done.4.w_other, ...), custom_call_target="tpu_custom_call" | custom-call | flops 2684354560 | bytes 2097152 | tf_op jit(solution)/shard_map/pallas_call | solution.py:292
  81.6 2.1 %collective-permute-start.7 = (s16[136,640]{1,0:T(8,128)(2,1)S(1)}, s16[136,640]{1,0:T(8,128)(2,1)S(1)}, u32[]{:S(2)}, u32[]{:S(2)}) collective-permute-start(s16[136,640]{1,0:T(8,128)(2,1)S(1)} %get-tuple-element.23.after), channel_id=1, source_target_pairs={{0,24},{8,16},{16,8},{24,0},{1,25},{9,17},{17,9},{25,1},{2,26},{10... | collective-permute-start | bytes 522248 | tf_op jit(solution)/shard_map/ppermute | solution.py:322
  83.7 10.6 %shard_map.61.kept = f32[512,640]{1,0:T(8,128)S(1)} custom-call(s32[5]{0:T(128)S(1)} %stack.30.info, f32[64,64,128]{2,1,0:T(8,128)S(1)} %get-tuple-element.17.tok, f32[64,64,128]{2,1,0:T(8,128)S(1)} %get-tuple-element.18.coef, bf16[1,2048,1280]{2,1,0:T(8,128)(2,1)} %w_own.7, bf16[1,2048,1280]{2,1,0:T(8,128)(2,1)} %collective-permute-done.4.w_other, ...), custom_call_target="tpu_custom_call" | custom-call | flops 2684354560 | bytes 2097152 | tf_op jit(solution)/shard_map/pallas_call | solution.py:292
  94.9 1.0 collective-permute-start.11
  96.2 1.2 collective-permute-start.8
  97.4 3.1 %collective-permute-done.11.refs_4_ = s16[136,640]{1,0:T(8,128)(2,1)S(1)} collective-permute-done((s16[136,640]{1,0:T(8,128)(2,1)S(1)}, s16[136,640]{1,0:T(8,128)(2,1)S(1)}, u32[]{:S(2)}, u32[]{:S(2)}) %collective-permute-start.11) | collective-permute-done | bytes 174112 | tf_op jit(solution)/shard_map/ppermute | solution.py:322
  100.5 3.3 %collective-permute-done.8.refs_2_ = s16[136,640]{1,0:T(8,128)(2,1)S(1)} collective-permute-done((s16[136,640]{1,0:T(8,128)(2,1)S(1)}, s16[136,640]{1,0:T(8,128)(2,1)S(1)}, u32[]{:S(2)}, u32[]{:S(2)}) %collective-permute-start.8) | collective-permute-done | bytes 174112 | tf_op jit(solution)/shard_map/ppermute | solution.py:323
  103.9 0.8 shard_map.63
  104.7 28.1 %all_to_all.11.ref = s16[16,32,768]{2,1,0:T(8,128)(2,1)S(1)} all-to-all(s16[16,32,768]{2,1,0:T(8,128)(2,1)S(1)} %shard_map.63), channel_id=1, replica_groups=mesh['z'=8,'y'=4,'c'=2,'x'=4] {'z','c'}, dimensions={0} | all-to-all | bytes 1572864 | tf_op jit(solution)/shard_map/all_to_all | solution.py:330
  132.8 0.9 shard_map.64
  (25 shorter events, 5.3 us)
Async XLA Ops:
  0.0 44.9 %collective-permute-start.4 = (bf16[1,2048,1280]{2,1,0:T(8,128)(2,1)}, bf16[1,2048,1280]{2,1,0:T(8,128)(2,1)}, u32[]{:S(2)}, u32[]{:S(2)}) collective-permute-start(bf16[1,2048,1280]{2,1,0:T(8,128)(2,1)} %w_own.7), channel_id=1, source_target_pairs={{0,4},{4,0},{1,5},{5,1},{2,6},{6,2},{3,7},{7,3},{8,12},{12,8},{9,1... | collective-permute-start | bytes 15728648 | tf_op jit(solution)/shard_map/ppermute | solution.py:257
  5.7 4.1 %collective-permute-start = (bf16[136,128]{1,0:T(8,128)(2,1)S(1)}, bf16[136,128]{1,0:T(8,128)(2,1)S(1)}, u32[]{:S(2)}, u32[]{:S(2)}) collective-permute-start(bf16[136,128]{1,0:T(8,128)(2,1)S(1)} %maximum_maximum_fusion.part0), channel_id=1, source_target_pairs={{0,1},{1,2},{2,3},{3,0},{4,5},{5,6},{6,7},{7,4},{8,9},{9,10},{10,1... | collective-permute-start | bytes 104456 | tf_op jit(solution)/shard_map/ppermute | solution.py:271
  5.8 4.4 %collective-permute-start.1 = (bf16[136,128]{1,0:T(8,128)(2,1)S(1)}, bf16[136,128]{1,0:T(8,128)(2,1)S(1)}, u32[]{:S(2)}, u32[]{:S(2)}) collective-permute-start(bf16[136,128]{1,0:T(8,128)(2,1)S(1)} %maximum_maximum_fusion.part0), channel_id=1, source_target_pairs={{0,2},{1,3},{2,0},{3,1},{4,6},{5,7},{6,4},{7,5},{8,10},{9,11},{10,... | collective-permute-start | bytes 104456 | tf_op jit(solution)/shard_map/ppermute | solution.py:271
  7.8 3.3 %collective-permute-start.2 = (bf16[136,128]{1,0:T(8,128)(2,1)S(1)}, bf16[136,128]{1,0:T(8,128)(2,1)S(1)}, u32[]{:S(2)}, u32[]{:S(2)}) collective-permute-start(bf16[136,128]{1,0:T(8,128)(2,1)S(1)} %maximum_maximum_fusion.part0), channel_id=1, source_target_pairs={{0,3},{1,0},{2,1},{3,2},{4,7},{5,4},{6,5},{7,6},{8,11},{9,8},{10,9... | collective-permute-start | bytes 104456 | tf_op jit(solution)/shard_map/ppermute | solution.py:271
  39.2 5.1 %collective-permute-start.3 = (bf16[32,72,128]{2,1,0:T(8,128)(2,1)S(1)}, bf16[32,72,128]{2,1,0:T(8,128)(2,1)S(1)}, u32[]{:S(2)}, u32[]{:S(2)}) collective-permute-start(bf16[32,72,128]{2,1,0:T(8,128)(2,1)S(1)} %all_to_all.10.own.after), channel_id=1, source_target_pairs={{0,4},{4,0},{1,5},{5,1},{2,6},{6,2},{3,7},{7,3},{8,12},{12,8},{9,1... | collective-permute-start | bytes 1769480 | tf_op jit(solution)/shard_map/ppermute | solution.py:277
  55.9 25.0 %collective-permute-start.5 = (s16[264,640]{1,0:T(8,128)(2,1)S(1)}, s16[264,640]{1,0:T(8,128)(2,1)S(1)}, u32[]{:S(2)}, u32[]{:S(2)}) collective-permute-start(s16[264,640]{1,0:T(8,128)(2,1)S(1)} %get-tuple-element.19.after), channel_id=1, source_target_pairs={{0,8},{8,0},{16,24},{24,16},{1,9},{9,1},{17,25},{25,17},{2,10},{10... | collective-permute-start | bytes 1013768 | tf_op jit(solution)/shard_map/ppermute | solution.py:311
  56.6 24.3 %collective-permute-start.6 = (s16[264,640]{1,0:T(8,128)(2,1)S(1)}, s16[264,640]{1,0:T(8,128)(2,1)S(1)}, u32[]{:S(2)}, u32[]{:S(2)}) collective-permute-start(s16[264,640]{1,0:T(8,128)(2,1)S(1)} %get-tuple-element.21), channel_id=1, source_target_pairs={{0,24},{8,16},{16,8},{24,0},{1,25},{9,17},{17,9},{25,1},{2,26},{10... | collective-permute-start | bytes 1013768 | tf_op jit(solution)/shard_map/ppermute | solution.py:311
  69.3 24.9 %collective-permute-start.10 = (s16[264,640]{1,0:T(8,128)(2,1)S(1)}, s16[264,640]{1,0:T(8,128)(2,1)S(1)}, u32[]{:S(2)}, u32[]{:S(2)}) collective-permute-start(s16[264,640]{1,0:T(8,128)(2,1)S(1)} %get-tuple-element.25), channel_id=1, source_target_pairs={{0,24},{8,16},{16,8},{24,0},{1,25},{9,17},{17,9},{25,1},{2,26},{10... | collective-permute-start | bytes 1013768 | tf_op jit(solution)/shard_map/ppermute | solution.py:311
  70.3 24.0 %collective-permute-start.9 = (s16[264,640]{1,0:T(8,128)(2,1)S(1)}, s16[264,640]{1,0:T(8,128)(2,1)S(1)}, u32[]{:S(2)}, u32[]{:S(2)}) collective-permute-start(s16[264,640]{1,0:T(8,128)(2,1)S(1)} %get-tuple-element.20.after), channel_id=1, source_target_pairs={{0,8},{8,0},{16,24},{24,16},{1,9},{9,1},{17,25},{25,17},{2,10},{10... | collective-permute-start | bytes 1013768 | tf_op jit(solution)/shard_map/ppermute | solution.py:311
  81.6 19.0 %collective-permute-start.7 = (s16[136,640]{1,0:T(8,128)(2,1)S(1)}, s16[136,640]{1,0:T(8,128)(2,1)S(1)}, u32[]{:S(2)}, u32[]{:S(2)}) collective-permute-start(s16[136,640]{1,0:T(8,128)(2,1)S(1)} %get-tuple-element.23.after), channel_id=1, source_target_pairs={{0,24},{8,16},{16,8},{24,0},{1,25},{9,17},{17,9},{25,1},{2,26},{10... | collective-permute-start | bytes 522248 | tf_op jit(solution)/shard_map/ppermute | solution.py:322
  94.9 5.6 %collective-permute-start.11 = (s16[136,640]{1,0:T(8,128)(2,1)S(1)}, s16[136,640]{1,0:T(8,128)(2,1)S(1)}, u32[]{:S(2)}, u32[]{:S(2)}) collective-permute-start(s16[136,640]{1,0:T(8,128)(2,1)S(1)} %get-tuple-element.27), channel_id=1, source_target_pairs={{0,24},{8,16},{16,8},{24,0},{1,25},{9,17},{17,9},{25,1},{2,26},{10... | collective-permute-start | bytes 522248 | tf_op jit(solution)/shard_map/ppermute | solution.py:322
  95.9 4.6 %collective-permute-start.12 = (s16[136,640]{1,0:T(8,128)(2,1)S(1)}, s16[136,640]{1,0:T(8,128)(2,1)S(1)}, u32[]{:S(2)}, u32[]{:S(2)}) collective-permute-start(s16[136,640]{1,0:T(8,128)(2,1)S(1)} %get-tuple-element.28), channel_id=1, source_target_pairs={{0,8},{8,0},{16,24},{24,16},{1,9},{9,1},{17,25},{25,17},{2,10},{10... | collective-permute-start | bytes 522248 | tf_op jit(solution)/shard_map/ppermute | solution.py:323
  96.2 7.7 %collective-permute-start.8 = (s16[136,640]{1,0:T(8,128)(2,1)S(1)}, s16[136,640]{1,0:T(8,128)(2,1)S(1)}, u32[]{:S(2)}, u32[]{:S(2)}) collective-permute-start(s16[136,640]{1,0:T(8,128)(2,1)S(1)} %get-tuple-element.24), channel_id=1, source_target_pairs={{0,8},{8,0},{16,24},{24,16},{1,9},{9,1},{17,25},{25,17},{2,10},{10... | collective-permute-start | bytes 522248 | tf_op jit(solution)/shard_map/ppermute | solution.py:323
  103.9 28.9 %copy-start = (f32[1,1280]{1,0:T(1,128)S(1)}, f32[1,1280]{1,0:T(1,128)}, u32[]{:S(2)}) copy-start(f32[1,1280]{1,0:T(1,128)} %bias.1) | copy-start | bytes 15364

commit v3 on v2

--- a/solution.py
+++ b/solution.py
@@ -35,7 +35,8 @@
 HBM = pl.BlockSpec(memory_space=pltpu.HBM)
 ANY = pl.BlockSpec(memory_space=pl.ANY)
 PIECES = 2
-GRANT = 48
+GRANT = 24
+WEIGHT_GRANT = 8
 
 
 def ring(n, k):
@@ -157,12 +158,9 @@
     return ref[k * 128 : (k + 1) * 128, :].astype(jnp.int32).astype(jnp.float32) * scale
 
 
-def expand_kernel(first, send, info, tok, coef, w_own, w_other, after, *rest):
-    outs, (x_buf, w_buf, acc, sems) = rest[:-4], rest[-4:]
-    depth = w_own.shape[1]
-    width = w_buf.shape[1]
-    core = info[0]
-    columns = pl.ds(pl.multiple_of(core * width, 128), width)
+def weights_kernel(core_ref, w_own, w_other, after, out_ref, sems):
+    depth, width = w_own.shape[1], out_ref.shape[1]
+    columns = pl.ds(pl.multiple_of(core_ref[0] * width, 128), width)
     deep = depth // PIECES
     copies = []
     for g in range(NC * PIECES):
@@ -171,44 +169,44 @@
         copies.append(
             pltpu.make_async_copy(
                 ref.at[0, k * deep : (k + 1) * deep, columns],
-                w_buf.at[g * deep : (g + 1) * deep],
+                out_ref.at[g * deep : (g + 1) * deep],
                 sems.at[g],
             )
         )
     for copy in copies:
         copy.start()
+    for copy in copies:
+        copy.wait()
+
+
+def expand_kernel(first, send, info, tok, coef, weights, after, *rest):
+    outs, x_buf = rest[:-1], rest[-1]
+    core = info[0]
     t = lax.broadcasted_iota(jnp.int32, (CHUNK, 128), 0).astype(jnp.float32) + float(first + 1)
-    blocks = BLOCKS_CHIP // (NC * PIECES)
-    for g, copy in enumerate(copies):
-
-        def build(i, carry, g=g):
-            h, j, z, c = i // 16, (i // 8) % 2, (i // 2) % 4, i % 2
-            n = lax.rem(c + core, NC) * CHIPS + (h * 4 + z) * NY + info[1 + h * 2 + j]
-            base = pl.multiple_of(i * CHUNK, CHUNK)
-            for b in range(g * blocks, (g + 1) * blocks):
-                row = jnp.zeros((CHUNK, 128), jnp.float32)
-                for m in range(MOST):
-                    k = b * MOST + m
-                    hit = jnp.broadcast_to(tok[n, k : k + 1, :], (CHUNK, 128)) == t
-                    row = jnp.where(
-                        hit, jnp.broadcast_to(coef[n, k : k + 1, :], (CHUNK, 128)), row
-                    )
-                x_buf[pl.ds(base, CHUNK), b * BLOCK : (b + 1) * BLOCK] = row.astype(jnp.bfloat16)
-            return carry
-
-        lax.fori_loop(0, 4 * PART // CHUNK, build, 0)
-        copy.wait()
-        here = slice(g * deep, (g + 1) * deep)
-        term = jnp.dot(x_buf[:, here], w_buf[here, :], preferred_element_type=jnp.float32)
-        if g == 0:
-            acc[...] = term
-        elif send or g < NC * PIECES - 1:
-            acc[...] += term
+
+    def build(i, carry):
+        h, j, z, c = i // 16, (i // 8) % 2, (i // 2) % 4, i % 2
+        n = lax.rem(c + core, NC) * CHIPS + (h * 4 + z) * NY + info[1 + h * 2 + j]
+        base = pl.multiple_of(i * CHUNK, CHUNK)
+        for b in range(BLOCKS_CHIP):
+            row = jnp.zeros((CHUNK, 128), jnp.float32)
+            for m in range(MOST):
+                k = b * MOST + m
+                hit = jnp.broadcast_to(tok[n, k : k + 1, :], (CHUNK, 128)) == t
+                row = jnp.where(
+                    hit, jnp.broadcast_to(coef[n, k : k + 1, :], (CHUNK, 128)), row
+                )
+            x_buf[pl.ds(base, CHUNK), b * BLOCK : (b + 1) * BLOCK] = row.astype(jnp.bfloat16)
+        return carry
+
+    lax.fori_loop(0, 4 * PART // CHUNK, build, 0)
+    for h in range(2):
+        here = slice(h * 2 * PART, (h + 1) * 2 * PART)
+        acc = jnp.dot(x_buf[here, :], weights[...], preferred_element_type=jnp.float32)
+        if send:
+            write_message(outs[h], acc)
         else:
-            outs[0][...] = acc[...] + term
-    if send:
-        for h in range(2):
-            write_message(outs[h], acc[h * 2 * PART : (h + 1) * 2 * PART, :])
+            outs[0][here, :] = acc
 
 
 def middle_kernel(kept, in0, in1, after, keep_ref, out0, out1):
@@ -274,6 +272,14 @@
         pack_kernel, shape((CHIPS, ROWS, BLOCK), jnp.bfloat16), [SMEM] + [VMEM] * NX, 10
     )(x.reshape(1), *parts)
     own = lax.all_to_all(outgoing, ("z", "y"), 0, 0, tiled=True)
+    weights = call(
+        weights_kernel,
+        shape((NC * depth, width), jnp.bfloat16),
+        [SMEM, HBM, HBM, ANY],
+        WEIGHT_GRANT,
+        flops=10**10,
+        scratch=[pltpu.SemaphoreType.DMA((NC * PIECES,))],
+    )(core.reshape(1), decoder, w_other, outgoing)
     other = lax.ppermute(own, "c", ring(NC, 1))
     slots = shape((2 * CHIPS, SLOTS, BLOCK), jnp.float32)
     tok, coef = call(prepare_kernel, [slots, slots], [SMEM, VMEM, VMEM], 10)(
@@ -292,16 +298,11 @@
         return call(
             functools.partial(expand_kernel, q * CHUNK, send),
             [message, message] if send else [shape((4 * PART, width), jnp.float32)],
-            [SMEM, VMEM, VMEM, HBM, HBM, ANY],
+            [SMEM, VMEM, VMEM, VMEM, ANY],
             GRANT,
             flops=2 * 4 * PART * 2 * depth * width,
-            scratch=[
-                pltpu.VMEM((4 * PART, 2 * depth), jnp.bfloat16),
-                pltpu.VMEM((2 * depth, width), jnp.bfloat16),
-                pltpu.VMEM((4 * PART, width), jnp.float32),
-                pltpu.SemaphoreType.DMA((NC * PIECES,)),
-            ],
-        )(sent_to if send else kept_for, tok, coef, decoder, w_other, after)
+            scratch=[pltpu.VMEM((4 * PART, 2 * depth), jnp.bfloat16)],
+        )(sent_to if send else kept_for, tok, coef, weights, after)
 
     after = own
     crossing = []

time: 134 us -> 121 us (0.903)
  Pallas kernels: 47.5 us -> 31.7 us
  local copies, waits for them, and re-layouts: 1.02 us -> 3.5 us
    pallas_call x4, Pallas kernels: 43 us -> 25.2 us  [expand(): call(functools.partial(expand_kernel, q * CHUNK, send), [message, message...]
    unnamed x2 -> x4, local copies, waits for them, and re-layouts: 0.01 us -> 2.49 us
    pallas_call x0 -> x1, Pallas kernels: none -> 1.97 us  [run(): call(weights_kernel, shape((NC * depth, width), jnp.bfloat16), [SMEM, HBM...]
  transfers between devices with their start and end apart: 13 -> 13, of which waited for: 6 -> 6; matrix products, arithmetic and copies ran while one was open for 2% -> 2% of each run, Pallas kernels for 26% -> 18%
where the time goes in v3:
time: 121 us; the launch traced here: 120 us
  blocking collectives  55.3 us (46%)
  Pallas kernels  31.7 us (26%)
  starting transfers between devices  17.9 us (15%)
  waiting for transfers between devices  10.1 us (8%)
  local copies, waits for them, and re-layouts  3.5 us (3%)
  other arithmetic  1.67 us (1%)
    all_to_all x1, blocking collectives, run(): lax.all_to_all(out, ('z', 'c'), 0, 0, tiled=True)  28.1 us
    all_to_all x1, blocking collectives, run(): own = lax.all_to_all(outgoing, ('z', 'y'), 0, 0, tiled=True)  27.2 us
    pallas_call x4, Pallas kernels, expand(): call(functools.partial(expand_kernel, q * CHUNK, send), [message, message...  25.2 us
    ppermute x1, starting transfers between devices, run(): other = lax.ppermute(own, 'c', ring(NC, 1))  3.5 us
    ppermute x2, waiting for transfers between devices, run(): m1 = lax.ppermute(m1, 'y', pair_a)  3.33 us
    ppermute x1, starting transfers between devices, run(): w_other = lax.ppermute(decoder, 'c', ring(NC, 1))  3.2 us
    ppermute x3, starting transfers between devices, run(): lax.ppermute(packed, 'x', ring(NX, k))  3.18 us
    ppermute x2, waiting for transfers between devices, run(): m0 = lax.ppermute(m0, 'y', pair_b)  3.14 us
  transfers between devices with their start and end apart: 13, of which 6 were waited for; matrix products, arithmetic and copies ran while one was open for 2% of the time, Pallas kernels for 18%

profile of v3, /device:TPU:1, one launch (start us, length us, event | category | flops | bytes accessed | tf_op | source)
XLA Modules:
  0.0 120.3 jit_solution(264538021203751490)
XLA Ops:
  0.0 3.2 %collective-permute-start.4 = (bf16[1,2048,1280]{2,1,0:T(8,128)(2,1)}, bf16[1,2048,1280]{2,1,0:T(8,128)(2,1)}, u32[]{:S(2)}, u32[]{:S(2)}) collective-permute-start(bf16[1,2048,1280]{2,1,0:T(8,128)(2,1)} %w_own.1), channel_id=1, source_target_pairs={{0,4},{4,0},{1,5},{5,1},{2,6},{6,2},{3,7},{7,3},{8,12},{12,8},{9,1... | collective-permute-start | bytes 15728648 | tf_op jit(solution)/shard_map/ppermute | solution.py:255
  4.8 0.8 broadcast_select_fusion
  5.8 1.9 %collective-permute-start.1 = (bf16[136,128]{1,0:T(8,128)(2,1)S(1)}, bf16[136,128]{1,0:T(8,128)(2,1)S(1)}, u32[]{:S(2)}, u32[]{:S(2)}) collective-permute-start(bf16[136,128]{1,0:T(8,128)(2,1)S(1)} %maximum_maximum_fusion.part0), channel_id=1, source_target_pairs={{0,2},{1,3},{2,0},{3,1},{4,6},{5,7},{6,4},{7,5},{8,10},{9,11},{10,... | collective-permute-start | bytes 104456 | tf_op jit(solution)/shard_map/ppermute | solution.py:269
  7.8 1.2 collective-permute-start.2
  8.9 0.9 collective-permute-done.part1
  11.1 0.9 shard_map.55.after
  12.0 27.2 %all_to_all.10.own.after = bf16[32,72,128]{2,1,0:T(8,128)(2,1)S(1)} all-to-all(bf16[32,72,128]{2,1,0:T(8,128)(2,1)S(1)} %shard_map.55.after), channel_id=1, replica_groups=mesh['z'=8,'y'=4,'c'=2,'x'=4] {'z','y'}, dimensions={0} | all-to-all | bytes 1179648 | tf_op jit(solution)/shard_map/all_to_all | solution.py:274
  39.2 3.5 %collective-permute-start.3 = (bf16[32,72,128]{2,1,0:T(8,128)(2,1)S(1)}, bf16[32,72,128]{2,1,0:T(8,128)(2,1)S(1)}, u32[]{:S(2)}, u32[]{:S(2)}) collective-permute-start(bf16[32,72,128]{2,1,0:T(8,128)(2,1)S(1)} %all_to_all.10.own.after), channel_id=1, source_target_pairs={{0,4},{4,0},{1,5},{5,1},{2,6},{6,2},{3,7},{7,3},{8,12},{12,8},{9,1... | collective-permute-start | bytes 1769480 | tf_op jit(solution)/shard_map/ppermute | solution.py:283
  42.8 1.5 %collective-permute-done.3.other = bf16[32,72,128]{2,1,0:T(8,128)(2,1)S(1)} collective-permute-done((bf16[32,72,128]{2,1,0:T(8,128)(2,1)S(1)}, bf16[32,72,128]{2,1,0:T(8,128)(2,1)S(1)}, u32[]{:S(2)}, u32[]{:S(2)}) %collective-permute-start.3) | collective-permute-done | bytes 589856 | tf_op jit(solution)/shard_map/ppermute | solution.py:283
  44.9 2.5 %copy-done.1 = bf16[1,2048,1280]{2,1,0:T(8,128)(2,1)S(1)} copy-done((bf16[1,2048,1280]{2,1,0:T(8,128)(2,1)S(1)}, bf16[1,2048,1280]{2,1,0:T(8,128)(2,1)}, u32[]{:S(2)}) %copy-start.1) | copy-done | bytes 5242904
  47.4 2.0 %shard_map.57.weights = bf16[4096,640]{1,0:T(8,128)(2,1)S(1)} custom-call(s32[1]{0:T(128)} %bitcast.info.core_ref, bf16[1,2048,1280]{2,1,0:T(8,128)(2,1)S(1)} %copy-done.1, bf16[1,2048,1280]{2,1,0:T(8,128)(2,1)} %collective-permute-done.4.w_other, bf16[32,72,128]{2,1,0:T(8,128)(2,1)S(1)} %shard_map.55.after), custom_call_target="tpu_custom_call" | custom-call | flops 10000000000 | bytes 2097152 | tf_op jit(solution)/shard_map/pallas_call | solution.py:275
  49.4 6.4 %shard_map.58 = (s16[264,640]{1,0:T(8,128)(2,1)S(1)}, s16[264,640]{1,0:T(8,128)(2,1)S(1)}) custom-call(s32[5]{0:T(128)S(1)} %stack.32.info, f32[64,64,128]{2,1,0:T(8,128)S(1)} %get-tuple-element.17.tok, f32[64,64,128]{2,1,0:T(8,128)S(1)} %get-tuple-element.18.coef, bf16[4096,640]{1,0:T(8,128)(2,1)S(1)} %shard_map.57.weights, ...), custom_call_target="tpu_custom_call" | custom-call | flops 2684354560 | bytes 2097152 | tf_op jit(solution)/shard_map/pallas_call | solution.py:298
  56.5 1.8 %collective-permute-start.6 = (s16[264,640]{1,0:T(8,128)(2,1)S(1)}, s16[264,640]{1,0:T(8,128)(2,1)S(1)}, u32[]{:S(2)}, u32[]{:S(2)}) collective-permute-start(s16[264,640]{1,0:T(8,128)(2,1)S(1)} %get-tuple-element.21), channel_id=1, source_target_pairs={{0,24},{8,16},{16,8},{24,0},{1,25},{9,17},{17,9},{25,1},{2,26},{10... | collective-permute-start | bytes 1013768 | tf_op jit(solution)/shard_map/ppermute | solution.py:312
  58.3 6.4 %shard_map.59 = (s16[264,640]{1,0:T(8,128)(2,1)S(1)}, s16[264,640]{1,0:T(8,128)(2,1)S(1)}) custom-call(s32[5]{0:T(128)S(1)} %stack.32.info, f32[64,64,128]{2,1,0:T(8,128)S(1)} %get-tuple-element.17.tok, f32[64,64,128]{2,1,0:T(8,128)S(1)} %get-tuple-element.18.coef, bf16[4096,640]{1,0:T(8,128)(2,1)S(1)} %shard_map.57.weights, ...), custom_call_target="tpu_custom_call" | custom-call | flops 2684354560 | bytes 2097152 | tf_op jit(solution)/shard_map/pallas_call | solution.py:298
  64.7 1.0 collective-permute-start.10
  65.7 6.2 %shard_map.60.kept = f32[512,640]{1,0:T(8,128)S(1)} custom-call(s32[5]{0:T(128)S(1)} %stack.30.info, f32[64,64,128]{2,1,0:T(8,128)S(1)} %get-tuple-element.17.tok, f32[64,64,128]{2,1,0:T(8,128)S(1)} %get-tuple-element.18.coef, bf16[4096,640]{1,0:T(8,128)(2,1)S(1)} %shard_map.57.weights, s16[264,640]{1,0:T(8,128)(2,1)S(1)} %get-tuple-element.20.after), custom_call_target="tpu_custom_call" | custom-call | flops 2684354560 | bytes 2097152 | tf_op jit(solution)/shard_map/pallas_call | solution.py:298
  72.6 2.1 %collective-permute-start.7 = (s16[136,640]{1,0:T(8,128)(2,1)S(1)}, s16[136,640]{1,0:T(8,128)(2,1)S(1)}, u32[]{:S(2)}, u32[]{:S(2)}) collective-permute-start(s16[136,640]{1,0:T(8,128)(2,1)S(1)} %get-tuple-element.23.after), channel_id=1, source_target_pairs={{0,24},{8,16},{16,8},{24,0},{1,25},{9,17},{17,9},{25,1},{2,26},{10... | collective-permute-start | bytes 522248 | tf_op jit(solution)/shard_map/ppermute | solution.py:323
  74.7 6.2 %shard_map.62.kept = f32[512,640]{1,0:T(8,128)S(1)} custom-call(s32[5]{0:T(128)S(1)} %stack.30.info, f32[64,64,128]{2,1,0:T(8,128)S(1)} %get-tuple-element.17.tok, f32[64,64,128]{2,1,0:T(8,128)S(1)} %get-tuple-element.18.coef, bf16[4096,640]{1,0:T(8,128)(2,1)S(1)} %shard_map.57.weights, s16[136,640]{1,0:T(8,128)(2,1)S(1)} %get-tuple-element.23.after), custom_call_target="tpu_custom_call" | custom-call | flops 2684354560 | bytes 2097152 | tf_op jit(solution)/shard_map/pallas_call | solution.py:298
  81.6 1.0 collective-permute-start.11
  82.8 1.2 %collective-permute-start.8 = (s16[136,640]{1,0:T(8,128)(2,1)S(1)}, s16[136,640]{1,0:T(8,128)(2,1)S(1)}, u32[]{:S(2)}, u32[]{:S(2)}) collective-permute-start(s16[136,640]{1,0:T(8,128)(2,1)S(1)} %get-tuple-element.24), channel_id=1, source_target_pairs={{0,8},{8,0},{16,24},{24,16},{1,9},{9,1},{17,25},{25,17},{2,10},{10... | collective-permute-start | bytes 522248 | tf_op jit(solution)/shard_map/ppermute | solution.py:324
  84.0 3.1 %collective-permute-done.11.refs_4_ = s16[136,640]{1,0:T(8,128)(2,1)S(1)} collective-permute-done((s16[136,640]{1,0:T(8,128)(2,1)S(1)}, s16[136,640]{1,0:T(8,128)(2,1)S(1)}, u32[]{:S(2)}, u32[]{:S(2)}) %collective-permute-start.11) | collective-permute-done | bytes 174112 | tf_op jit(solution)/shard_map/ppermute | solution.py:323
  87.2 3.3 %collective-permute-done.8.refs_2_ = s16[136,640]{1,0:T(8,128)(2,1)S(1)} collective-permute-done((s16[136,640]{1,0:T(8,128)(2,1)S(1)}, s16[136,640]{1,0:T(8,128)(2,1)S(1)}, u32[]{:S(2)}, u32[]{:S(2)}) %collective-permute-start.8) | collective-permute-done | bytes 174112 | tf_op jit(solution)/shard_map/ppermute | solution.py:324
  91.3 28.1 %all_to_all.11.ref = s16[16,32,768]{2,1,0:T(8,128)(2,1)S(1)} all-to-all(s16[16,32,768]{2,1,0:T(8,128)(2,1)S(1)} %shard_map.64), channel_id=1, replica_groups=mesh['z'=8,'y'=4,'c'=2,'x'=4] {'z','c'}, dimensions={0} | all-to-all | bytes 1572864 | tf_op jit(solution)/shard_map/all_to_all | solution.py:331
  119.4 0.9 shard_map.65
  (28 shorter events, 6.9 us)
Async XLA Ops:
  0.0 44.9 %collective-permute-start.4 = (bf16[1,2048,1280]{2,1,0:T(8,128)(2,1)}, bf16[1,2048,1280]{2,1,0:T(8,128)(2,1)}, u32[]{:S(2)}, u32[]{:S(2)}) collective-permute-start(bf16[1,2048,1280]{2,1,0:T(8,128)(2,1)} %w_own.1), channel_id=1, source_target_pairs={{0,4},{4,0},{1,5},{5,1},{2,6},{6,2},{3,7},{7,3},{8,12},{12,8},{9,1... | collective-permute-start | bytes 15728648 | tf_op jit(solution)/shard_map/ppermute | solution.py:255
  5.7 4.1 %collective-permute-start = (bf16[136,128]{1,0:T(8,128)(2,1)S(1)}, bf16[136,128]{1,0:T(8,128)(2,1)S(1)}, u32[]{:S(2)}, u32[]{:S(2)}) collective-permute-start(bf16[136,128]{1,0:T(8,128)(2,1)S(1)} %maximum_maximum_fusion.part0), channel_id=1, source_target_pairs={{0,1},{1,2},{2,3},{3,0},{4,5},{5,6},{6,7},{7,4},{8,9},{9,10},{10,1... | collective-permute-start | bytes 104456 | tf_op jit(solution)/shard_map/ppermute | solution.py:269
  5.8 4.4 %collective-permute-start.1 = (bf16[136,128]{1,0:T(8,128)(2,1)S(1)}, bf16[136,128]{1,0:T(8,128)(2,1)S(1)}, u32[]{:S(2)}, u32[]{:S(2)}) collective-permute-start(bf16[136,128]{1,0:T(8,128)(2,1)S(1)} %maximum_maximum_fusion.part0), channel_id=1, source_target_pairs={{0,2},{1,3},{2,0},{3,1},{4,6},{5,7},{6,4},{7,5},{8,10},{9,11},{10,... | collective-permute-start | bytes 104456 | tf_op jit(solution)/shard_map/ppermute | solution.py:269
  7.8 3.3 %collective-permute-start.2 = (bf16[136,128]{1,0:T(8,128)(2,1)S(1)}, bf16[136,128]{1,0:T(8,128)(2,1)S(1)}, u32[]{:S(2)}, u32[]{:S(2)}) collective-permute-start(bf16[136,128]{1,0:T(8,128)(2,1)S(1)} %maximum_maximum_fusion.part0), channel_id=1, source_target_pairs={{0,3},{1,0},{2,1},{3,2},{4,7},{5,4},{6,5},{7,6},{8,11},{9,8},{10,9... | collective-permute-start | bytes 104456 | tf_op jit(solution)/shard_map/ppermute | solution.py:269
  39.2 5.1 %collective-permute-start.3 = (bf16[32,72,128]{2,1,0:T(8,128)(2,1)S(1)}, bf16[32,72,128]{2,1,0:T(8,128)(2,1)S(1)}, u32[]{:S(2)}, u32[]{:S(2)}) collective-permute-start(bf16[32,72,128]{2,1,0:T(8,128)(2,1)S(1)} %all_to_all.10.own.after), channel_id=1, source_target_pairs={{0,4},{4,0},{1,5},{5,1},{2,6},{6,2},{3,7},{7,3},{8,12},{12,8},{9,1... | collective-permute-start | bytes 1769480 | tf_op jit(solution)/shard_map/ppermute | solution.py:283
  44.9 2.5 %copy-start.1 = (bf16[1,2048,1280]{2,1,0:T(8,128)(2,1)S(1)}, bf16[1,2048,1280]{2,1,0:T(8,128)(2,1)}, u32[]{:S(2)}) copy-start(bf16[1,2048,1280]{2,1,0:T(8,128)(2,1)} %w_own.1) | copy-start | bytes 15728644
  55.8 16.1 %collective-permute-start.5 = (s16[264,640]{1,0:T(8,128)(2,1)S(1)}, s16[264,640]{1,0:T(8,128)(2,1)S(1)}, u32[]{:S(2)}, u32[]{:S(2)}) collective-permute-start(s16[264,640]{1,0:T(8,128)(2,1)S(1)} %get-tuple-element.19.after), channel_id=1, source_target_pairs={{0,8},{8,0},{16,24},{24,16},{1,9},{9,1},{17,25},{25,17},{2,10},{10... | collective-permute-start | bytes 1013768 | tf_op jit(solution)/shard_map/ppermute | solution.py:312
  56.5 15.4 %collective-permute-start.6 = (s16[264,640]{1,0:T(8,128)(2,1)S(1)}, s16[264,640]{1,0:T(8,128)(2,1)S(1)}, u32[]{:S(2)}, u32[]{:S(2)}) collective-permute-start(s16[264,640]{1,0:T(8,128)(2,1)S(1)} %get-tuple-element.21), channel_id=1, source_target_pairs={{0,24},{8,16},{16,8},{24,0},{1,25},{9,17},{17,9},{25,1},{2,26},{10... | collective-permute-start | bytes 1013768 | tf_op jit(solution)/shard_map/ppermute | solution.py:312
  64.7 16.1 %collective-permute-start.10 = (s16[264,640]{1,0:T(8,128)(2,1)S(1)}, s16[264,640]{1,0:T(8,128)(2,1)S(1)}, u32[]{:S(2)}, u32[]{:S(2)}) collective-permute-start(s16[264,640]{1,0:T(8,128)(2,1)S(1)} %get-tuple-element.25), channel_id=1, source_target_pairs={{0,24},{8,16},{16,8},{24,0},{1,25},{9,17},{17,9},{25,1},{2,26},{10... | collective-permute-start | bytes 1013768 | tf_op jit(solution)/shard_map/ppermute | solution.py:312
  65.7 15.2 %collective-permute-start.9 = (s16[264,640]{1,0:T(8,128)(2,1)S(1)}, s16[264,640]{1,0:T(8,128)(2,1)S(1)}, u32[]{:S(2)}, u32[]{:S(2)}) collective-permute-start(s16[264,640]{1,0:T(8,128)(2,1)S(1)} %get-tuple-element.20.after), channel_id=1, source_target_pairs={{0,8},{8,0},{16,24},{24,16},{1,9},{9,1},{17,25},{25,17},{2,10},{10... | collective-permute-start | bytes 1013768 | tf_op jit(solution)/shard_map/ppermute | solution.py:312
  72.6 14.6 %collective-permute-start.7 = (s16[136,640]{1,0:T(8,128)(2,1)S(1)}, s16[136,640]{1,0:T(8,128)(2,1)S(1)}, u32[]{:S(2)}, u32[]{:S(2)}) collective-permute-start(s16[136,640]{1,0:T(8,128)(2,1)S(1)} %get-tuple-element.23.after), channel_id=1, source_target_pairs={{0,24},{8,16},{16,8},{24,0},{1,25},{9,17},{17,9},{25,1},{2,26},{10... | collective-permute-start | bytes 522248 | tf_op jit(solution)/shard_map/ppermute | solution.py:323
  81.6 5.6 %collective-permute-start.11 = (s16[136,640]{1,0:T(8,128)(2,1)S(1)}, s16[136,640]{1,0:T(8,128)(2,1)S(1)}, u32[]{:S(2)}, u32[]{:S(2)}) collective-permute-start(s16[136,640]{1,0:T(8,128)(2,1)S(1)} %get-tuple-element.27), channel_id=1, source_target_pairs={{0,24},{8,16},{16,8},{24,0},{1,25},{9,17},{17,9},{25,1},{2,26},{10... | collective-permute-start | bytes 522248 | tf_op jit(solution)/shard_map/ppermute | solution.py:323
  82.6 4.6 %collective-permute-start.12 = (s16[136,640]{1,0:T(8,128)(2,1)S(1)}, s16[136,640]{1,0:T(8,128)(2,1)S(1)}, u32[]{:S(2)}, u32[]{:S(2)}) collective-permute-start(s16[136,640]{1,0:T(8,128)(2,1)S(1)} %get-tuple-element.28), channel_id=1, source_target_pairs={{0,8},{8,0},{16,24},{24,16},{1,9},{9,1},{17,25},{25,17},{2,10},{10... | collective-permute-start | bytes 522248 | tf_op jit(solution)/shard_map/ppermute | solution.py:324
  82.8 7.7 %collective-permute-start.8 = (s16[136,640]{1,0:T(8,128)(2,1)S(1)}, s16[136,640]{1,0:T(8,128)(2,1)S(1)}, u32[]{:S(2)}, u32[]{:S(2)}) collective-permute-start(s16[136,640]{1,0:T(8,128)(2,1)S(1)} %get-tuple-element.24), channel_id=1, source_target_pairs={{0,8},{8,0},{16,24},{24,16},{1,9},{9,1},{17,25},{25,17},{2,10},{10... | collective-permute-start | bytes 522248 | tf_op jit(solution)/shard_map/ppermute | solution.py:324
  90.5 28.9 %copy-start = (f32[1,1280]{1,0:T(1,128)S(1)}, f32[1,1280]{1,0:T(1,128)}, u32[]{:S(2)}) copy-start(f32[1,1280]{1,0:T(1,128)} %bias.1) | copy-start | bytes 15364

commit v4 on v3

--- a/solution.py
+++ b/solution.py
@@ -1,5 +1,3 @@
-import functools
-
 import jax
 import jax.numpy as jnp
 from jax import lax
@@ -21,9 +19,7 @@
 HALF = BLOCKS_DEV * MOST
 SLOTS = BLOCKS_CHIP * MOST
 ROWS = SLOTS + 8
-CHUNK = 16
-CHUNKS = TOK // CHUNK
-PART = NZ // 2 * NC * CHUNK
+PART = NZ // 2 * TOK
 LIMIT = 32700.0
 FLOOR = 2.0**-104
 STEP = 256.0
@@ -34,9 +30,9 @@
 SMEM = pl.BlockSpec(memory_space=pltpu.SMEM)
 HBM = pl.BlockSpec(memory_space=pltpu.HBM)
 ANY = pl.BlockSpec(memory_space=pl.ANY)
-PIECES = 2
-GRANT = 24
-WEIGHT_GRANT = 8
+PIECES = 4
+GRANT = 48
+WEIGHT_GRANT = 50
 
 
 def ring(n, k):
@@ -57,6 +53,31 @@
 
 def column(row):
     return jnp.transpose(jnp.broadcast_to(row, (128, 128)))
+
+
+def wrap_kernel(counts, coeffs, ids, out_ref):
+    n = OWN * ACTIVE
+    slot = lax.broadcasted_iota(jnp.int32, (ACTIVE, BLOCK), 0)
+    for i in range(OWN):
+        live = slot < counts[i]
+        rows = jnp.where(live, coeffs[i].astype(jnp.float32), 0.0)
+        out_ref[i * ACTIVE : (i + 1) * ACTIVE, :] = rows.astype(jnp.bfloat16)
+    high = (ids[...] // 32).astype(jnp.float32)
+    low = ids[...].astype(jnp.float32) - high * 32.0
+    repeat = lax.broadcasted_iota(jnp.int32, (ACTIVE, n), 1) % ACTIVE
+    repeat = jnp.where(repeat == lax.broadcasted_iota(jnp.int32, (ACTIVE, n), 0), 1.0, 0.0)
+    token = lax.broadcasted_iota(jnp.int32, (OWN, n), 0)
+    mine = lax.broadcasted_iota(jnp.int32, (OWN, n), 1) // ACTIVE == token
+    meta = jnp.zeros((OWN, n), jnp.float32)
+    for k, part in enumerate((high, low)):
+        wide = jnp.dot(
+            part.astype(jnp.bfloat16),
+            repeat.astype(jnp.bfloat16),
+            preferred_element_type=jnp.float32,
+        )
+        row = jnp.sum(jnp.where(mine, wide, 0.0), axis=0, keepdims=True)
+        meta = jnp.where(token == k, jnp.broadcast_to(row, (OWN, n)), meta)
+    out_ref[n : n + OWN, :] = meta.astype(jnp.bfloat16)
 
 
 def pack_kernel(info, part0, part1, part2, part3, out_ref):
@@ -108,26 +129,20 @@
             )
 
 
-def prepare_kernel(info, own, other, tok_ref, coef_ref):
+def prepare(info, arrived, tok_ref, coef_ref):
     core = info[0]
-    sources = (own, other)
     meta = jnp.concatenate(
-        [
-            ref[s, SLOTS:ROWS, :].astype(jnp.float32)[0:1, :]
-            for ref in sources
-            for s in range(CHIPS)
-        ]
-        + [jnp.zeros((128 - 2 * CHIPS, 128), jnp.float32)],
+        [arrived[s, SLOTS:ROWS, :].astype(jnp.float32)[0:1, :] for s in range(CHIPS)]
+        + [jnp.zeros((128 - CHIPS, 128), jnp.float32)],
         axis=0,
     )
     turned = jnp.transpose(meta)
-    for n in range(2 * CHIPS):
-        ref, s = sources[n // CHIPS], n % CHIPS
+    for s in range(CHIPS):
         for h in range(NC):
             to = pl.ds(pl.multiple_of(lax.rem(core + h, NC) * HALF, HALF), HALF)
             here = slice(h * HALF, (h + 1) * HALF)
-            tok_ref[n, to, :] = jnp.broadcast_to(turned[here, n : n + 1], (HALF, 128))
-            coef_ref[n, to, :] = ref[s, here, :].astype(jnp.float32)
+            tok_ref[s, to, :] = jnp.broadcast_to(turned[here, s : s + 1], (HALF, 128))
+            coef_ref[s, to, :] = arrived[s, here, :].astype(jnp.float32)
 
 
 def quantized(acc):
@@ -161,11 +176,11 @@
 def weights_kernel(core_ref, w_own, w_other, after, out_ref, sems):
     depth, width = w_own.shape[1], out_ref.shape[1]
     columns = pl.ds(pl.multiple_of(core_ref[0] * width, 128), width)
-    deep = depth // PIECES
+    deep = NC * depth // PIECES
     copies = []
-    for g in range(NC * PIECES):
-        ref = (w_own, w_other)[g // PIECES]
-        k = g % PIECES
+    for g in range(PIECES):
+        ref = (w_own, w_other)[g // (PIECES // NC)]
+        k = g % (PIECES // NC)
         copies.append(
             pltpu.make_async_copy(
                 ref.at[0, k * deep : (k + 1) * deep, columns],
@@ -179,37 +194,63 @@
         copy.wait()
 
 
-def expand_kernel(first, send, info, tok, coef, weights, after, *rest):
-    outs, x_buf = rest[:-1], rest[-1]
-    core = info[0]
-    t = lax.broadcasted_iota(jnp.int32, (CHUNK, 128), 0).astype(jnp.float32) + float(first + 1)
-
-    def build(i, carry):
-        h, j, z, c = i // 16, (i // 8) % 2, (i // 2) % 4, i % 2
-        n = lax.rem(c + core, NC) * CHIPS + (h * 4 + z) * NY + info[1 + h * 2 + j]
-        base = pl.multiple_of(i * CHUNK, CHUNK)
+def build(info, tok, coef, x_buf):
+    t = lax.broadcasted_iota(jnp.int32, (TOK, 128), 0).astype(jnp.float32) + 1.0
+
+    def source(i, carry):
+        h, j, z = i // 8, (i // 4) % 2, i % 4
+        n = (h * 4 + z) * NY + info[1 + h * 2 + j]
+        base = pl.multiple_of(i * TOK, TOK)
         for b in range(BLOCKS_CHIP):
-            row = jnp.zeros((CHUNK, 128), jnp.float32)
+            row = jnp.zeros((TOK, 128), jnp.float32)
             for m in range(MOST):
                 k = b * MOST + m
-                hit = jnp.broadcast_to(tok[n, k : k + 1, :], (CHUNK, 128)) == t
-                row = jnp.where(
-                    hit, jnp.broadcast_to(coef[n, k : k + 1, :], (CHUNK, 128)), row
-                )
-            x_buf[pl.ds(base, CHUNK), b * BLOCK : (b + 1) * BLOCK] = row.astype(jnp.bfloat16)
+                hit = jnp.broadcast_to(tok[n, k : k + 1, :], (TOK, 128)) == t
+                row = jnp.where(hit, jnp.broadcast_to(coef[n, k : k + 1, :], (TOK, 128)), row)
+            x_buf[pl.ds(base, TOK), b * BLOCK : (b + 1) * BLOCK] = row.astype(jnp.bfloat16)
         return carry
 
-    lax.fori_loop(0, 4 * PART // CHUNK, build, 0)
-    for h in range(2):
-        here = slice(h * 2 * PART, (h + 1) * 2 * PART)
-        acc = jnp.dot(x_buf[here, :], weights[...], preferred_element_type=jnp.float32)
-        if send:
-            write_message(outs[h], acc)
-        else:
-            outs[0][here, :] = acc
-
-
-def middle_kernel(kept, in0, in1, after, keep_ref, out0, out1):
+    lax.fori_loop(0, 4 * PART // TOK, source, 0)
+
+
+def multiply(info, arrived, weights, tok, coef, x_buf, w_buf, sems, acc):
+    deep = w_buf.shape[0] // PIECES
+    copies = []
+    for g in range(PIECES):
+        here = slice(g * deep, (g + 1) * deep)
+        copies.append(pltpu.make_async_copy(weights.at[here], w_buf.at[here], sems.at[g]))
+    for copy in copies:
+        copy.start()
+    prepare(info, arrived, tok, coef)
+    build(info, tok, coef, x_buf)
+    for g, copy in enumerate(copies):
+        here = slice(g * deep, (g + 1) * deep)
+        copy.wait()
+        term = jnp.dot(x_buf[:, here], w_buf[here, :], preferred_element_type=jnp.float32)
+        acc[...] = term if g == 0 else acc[...] + term
+
+
+def send_kernel(info, arrived, weights, after, out0, out1, acc, *scratch):
+    multiply(info, arrived, weights, *scratch, acc)
+    for h, out in enumerate((out0, out1)):
+        write_message(out, acc[h * 2 * PART : (h + 1) * 2 * PART, :])
+
+
+def keep_kernel(info, arrived, weights, after, out_ref, *scratch):
+    multiply(info, arrived, weights, *scratch, out_ref)
+
+
+def keep_middle_kernel(
+    info, arrived, weights, after, in0, in1, keep_ref, out0, out1, acc, *scratch
+):
+    multiply(info, arrived, weights, *scratch, acc)
+    for h, (ref, out) in enumerate(((in0, out0), (in1, out1))):
+        low, high = 2 * h * PART, (2 * h + 1) * PART
+        keep_ref[h * PART : (h + 1) * PART, :] = acc[low:high, :] + read_message(ref, 0)
+        write_message(out, acc[high : high + PART, :] + read_message(ref, 1))
+
+
+def middle_kernel(kept, in0, in1, keep_ref, out0, out1):
     for h, (ref, out) in enumerate(((in0, out0), (in1, out1))):
         keep_ref[h * PART : (h + 1) * PART, :] = kept[
             2 * h * PART : (2 * h + 1) * PART, :
@@ -219,20 +260,21 @@
         )
 
 
-def last_kernel(*refs):
+def last_kernel(info, *refs):
     ins, out_ref = refs[:-1], refs[-1]
     width = ins[0].shape[1]
-    for q in range(CHUNKS):
+    for q in range(NC):
         kept, messages = ins[3 * q], ins[3 * q + 1 : 3 * q + 3]
+        c = lax.rem(info[0] + q, NC)
         for h, ref in enumerate(messages):
             acc = kept[h * PART : (h + 1) * PART, :] + read_message(ref, 0)
             v, code = quantized(acc)
             code = jnp.broadcast_to(code, (PART, 128)).astype(jnp.int32).astype(jnp.int16)
-            for j in range(PART // CHUNK):
-                d = h * (PART // CHUNK) + j
-                at, here = slice(q * CHUNK, (q + 1) * CHUNK), slice(j * CHUNK, (j + 1) * CHUNK)
-                out_ref[d, at, 0:width] = v[here, :]
-                out_ref[d, at, width : width + 128] = code[here, :]
+            for j in range(PART // TOK):
+                d = (h * (PART // TOK) + j) * NC + c
+                here = slice(j * TOK, (j + 1) * TOK)
+                out_ref[d, :, 0:width] = v[here, :]
+                out_ref[d, :, width : width + 128] = code[here, :]
 
 
 def final_kernel(ref, bias, out_ref):
@@ -254,20 +296,11 @@
     width = full // NC
     w_other = lax.ppermute(decoder, "c", ring(NC, 1))
 
-    live = lax.broadcasted_iota(jnp.int32, (OWN, ACTIVE), 1) < counts[:, None]
-    coeffs = jnp.where(live[:, :, None], coefficients, jnp.zeros((), coefficients.dtype))
-    flat = block_ids.reshape(1, OWN * ACTIVE)
-    packed = jnp.concatenate(
-        [
-            coeffs.reshape(OWN * ACTIVE, BLOCK),
-            (flat // 32).astype(jnp.bfloat16),
-            (flat % 32).astype(jnp.bfloat16),
-            jnp.zeros((6, BLOCK), jnp.bfloat16),
-        ],
-        axis=0,
-    )
+    shape = jax.ShapeDtypeStruct
+    packed = call(
+        wrap_kernel, shape((OWN * (ACTIVE + 1), BLOCK), jnp.bfloat16), [SMEM, VMEM, VMEM], 10
+    )(counts, coefficients, block_ids)
     parts = [packed] + [lax.ppermute(packed, "x", ring(NX, k)) for k in range(1, NX)]
-    shape = jax.ShapeDtypeStruct
     outgoing = call(
         pack_kernel, shape((CHIPS, ROWS, BLOCK), jnp.bfloat16), [SMEM] + [VMEM] * NX, 10
     )(x.reshape(1), *parts)
@@ -278,14 +311,9 @@
         [SMEM, HBM, HBM, ANY],
         WEIGHT_GRANT,
         flops=10**10,
-        scratch=[pltpu.SemaphoreType.DMA((NC * PIECES,))],
+        scratch=[pltpu.SemaphoreType.DMA((PIECES,))],
     )(core.reshape(1), decoder, w_other, outgoing)
     other = lax.ppermute(own, "c", ring(NC, 1))
-    slots = shape((2 * CHIPS, SLOTS, BLOCK), jnp.float32)
-    tok, coef = call(prepare_kernel, [slots, slots], [SMEM, VMEM, VMEM], 10)(
-        core.reshape(1), own, other
-    )
-
     pair_a, pair_b = [(i, i ^ 1) for i in range(NY)], [(i, NY - 1 - i) for i in range(NY)]
     a, b = y ^ 1, NY - 1 - y
     opposite = NY - 1 - a
@@ -294,38 +322,53 @@
     message = shape((2 * PART + 8, width), jnp.int16)
     small = shape((PART + 8, width), jnp.int16)
 
-    def expand(q, send, after):
-        return call(
-            functools.partial(expand_kernel, q * CHUNK, send),
-            [message, message] if send else [shape((4 * PART, width), jnp.float32)],
-            [SMEM, VMEM, VMEM, VMEM, ANY],
-            GRANT,
-            flops=2 * 4 * PART * 2 * depth * width,
-            scratch=[pltpu.VMEM((4 * PART, 2 * depth), jnp.bfloat16)],
-        )(sent_to if send else kept_for, tok, coef, weights, after)
-
-    after = own
-    crossing = []
-    for q in range(CHUNKS):
-        m0, m1 = expand(q, True, after)
-        after = m0
-        crossing.append((lax.ppermute(m0, "y", pair_a), lax.ppermute(m1, "y", pair_b)))
-    arrived = []
-    for q in range(CHUNKS):
-        (kept,) = expand(q, False, after)
-        kept, m0, m1 = call(
-            middle_kernel,
-            [shape((2 * PART, width), jnp.float32), small, small],
-            [VMEM] * 3 + [ANY],
-            10,
-        )(kept, *crossing[q], after)
-        after = m0
-        m0 = lax.ppermute(m0, "y", pair_b)
-        m1 = lax.ppermute(m1, "y", pair_a)
-        arrived += [kept, m0, m1]
+    kept = shape((2 * PART, width), jnp.float32)
+    product = {"flops": 2 * 4 * PART * NC * depth * width}
+    total = pltpu.VMEM((4 * PART, width), jnp.float32)
+    scratch = [
+        pltpu.VMEM((CHIPS, SLOTS, BLOCK), jnp.float32),
+        pltpu.VMEM((CHIPS, SLOTS, BLOCK), jnp.float32),
+        pltpu.VMEM((4 * PART, NC * depth), jnp.bfloat16),
+        pltpu.VMEM((NC * depth, width), jnp.bfloat16),
+        pltpu.SemaphoreType.DMA((PIECES,)),
+    ]
+    given = [SMEM, VMEM, HBM, ANY]
+
+    def cross(m0, m1, pair0, pair1):
+        m0 = lax.ppermute(m0, "y", pair0)
+        m1 = lax.ppermute(m1, "y", pair1)
+        return m0, m1
+
+    m0, m1 = call(
+        send_kernel, [message, message], given, GRANT, scratch=[total] + scratch, **product
+    )(sent_to, own, weights, own)
+    crossing0 = cross(m0, m1, pair_a, pair_b)
+    m0, m1 = call(
+        send_kernel, [message, message], given, GRANT, scratch=[total] + scratch, **product
+    )(sent_to, other, weights, m0)
+    crossing1 = cross(m0, m1, pair_a, pair_b)
+    (sums,) = call(
+        keep_kernel,
+        [shape((4 * PART, width), jnp.float32)],
+        given,
+        GRANT,
+        scratch=scratch,
+        **product,
+    )(kept_for, own, weights, m0)
+    kept0, m0, m1 = call(middle_kernel, [kept, small, small], [VMEM] * 3, 10)(sums, *crossing0)
+    arrived0 = cross(m0, m1, pair_b, pair_a)
+    kept1, m0, m1 = call(
+        keep_middle_kernel,
+        [kept, small, small],
+        given + [VMEM] * 2,
+        GRANT,
+        scratch=[total] + scratch,
+        **product,
+    )(kept_for, other, weights, m0, *crossing1)
+    arrived1 = cross(m0, m1, pair_b, pair_a)
     out = call(
-        last_kernel, shape((NZ * NC, TOK, width + 128), jnp.int16), [VMEM] * 3 * CHUNKS, 10
-    )(*arrived)
+        last_kernel, shape((NZ * NC, TOK, width + 128), jnp.int16), [SMEM] + [VMEM] * 6, 10
+    )(core.reshape(1), kept0, *arrived0, kept1, *arrived1)
     return call(
         final_kernel, shape((1, TOK, full), jnp.bfloat16), [VMEM] * 2, 10
     )(lax.all_to_all(out, ("z", "c"), 0, 0, tiled=True), bias)

time: 121 us -> 126 us (1.041)
  blocking collectives: 55.3 us -> 27.8 us
  waiting for transfers between devices: 10.1 us -> 25.4 us
  starting transfers between devices: 17.9 us -> 28.7 us
  Pallas kernels: 31.7 us -> 41.6 us
  other arithmetic: 1.67 us -> 0 us
    all_to_all x1 -> x0, blocking collectives: 27.2 us -> none  [run(): own = lax.all_to_all(outgoing, ('z', 'y'), 0, 0, tiled=True)]
    all_to_all x0 -> x1, waiting for transfers between devices: none -> 16.5 us  [run(): own = lax.all_to_all(outgoing, ('z', 'y'), 0, 0, tiled=True)]
    all_to_all x0 -> x1, starting transfers between devices: none -> 10.8 us  [run(): own = lax.all_to_all(outgoing, ('z', 'y'), 0, 0, tiled=True)]
    pallas_call x8 -> x7, Pallas kernels: 27.9 us -> 34.1 us  [the longest x2 17.3 us: run(): call(send_kernel, [message, message], given, GRANT, scratch=[total] + scr...]
    pallas_call x1, Pallas kernels: 1.97 us -> 4.86 us  [run(): call(weights_kernel, shape((NC * depth, width), jnp.bfloat16), [SMEM, HBM...]
    ppermute x1, waiting for transfers between devices: 1.46 us -> 0.01 us  [run(): other = lax.ppermute(own, 'c', ring(NC, 1))]
  transfers between devices with their start and end apart: 13 -> 14, of which waited for: 6 -> 6; matrix products, arithmetic and copies ran while one was open for 2% -> 0% of each run, Pallas kernels for 18% -> 32%
where the time goes in v4:
time: 126 us
  Pallas kernels  41.6 us (33%)
  starting transfers between devices  28.7 us (23%)
  blocking collectives  27.8 us (22%)
  waiting for transfers between devices  25.4 us (20%)
  local copies, waits for them, and re-layouts  2.27 us (2%)
    all_to_all x1, blocking collectives, run(): lax.all_to_all(out, ('z', 'c'), 0, 0, tiled=True)  27.8 us
    pallas_call x2, Pallas kernels, run(): call(send_kernel, [message, message], given, GRANT, scratch=[total] + scr...  17.3 us
    all_to_all x1, waiting for transfers between devices, run(): own = lax.all_to_all(outgoing, ('z', 'y'), 0, 0, tiled=True)  16.5 us
    all_to_all x1, starting transfers between devices, run(): own = lax.all_to_all(outgoing, ('z', 'y'), 0, 0, tiled=True)  10.8 us
    pallas_call x1, Pallas kernels, run(): call(keep_kernel, [shape((4 * PART, width), jnp.float32)], given, GRANT,...  7.86 us
    pallas_call x1, Pallas kernels, run(): call(keep_middle_kernel, [kept, small, small], given + [VMEM] * 2, GRANT,...  6.79 us
    pallas_call x1, Pallas kernels, run(): call(weights_kernel, shape((NC * depth, width), jnp.bfloat16), [SMEM, HBM...  4.86 us
    ppermute x4, starting transfers between devices, cross(): m1 = lax.ppermute(m1, 'y', pair1)  4.23 us
  transfers between devices with their start and end apart: 14, of which 6 were waited for; matrix products, arithmetic and copies ran while one was open for 0% of the time, Pallas kernels for 32%

profile of v4, /device:TPU:1, one launch (start us, length us, event | category | flops | bytes accessed | tf_op | source)
XLA Modules:
  0.0 125.9 jit_solution(9195219916737913311)
XLA Ops:
  0.0 3.2 %collective-permute-start.3 = (bf16[1,2048,1280]{2,1,0:T(8,128)(2,1)}, bf16[1,2048,1280]{2,1,0:T(8,128)(2,1)}, u32[]{:S(2)}, u32[]{:S(2)}) collective-permute-start(bf16[1,2048,1280]{2,1,0:T(8,128)(2,1)} %w_own.1), channel_id=1, source_target_pairs={{0,4},{4,0},{1,5},{5,1},{2,6},{6,2},{3,7},{7,3},{8,12},{12,8},{9,1... | collective-permute-start | bytes 15728648 | tf_op jit(solution)/shard_map/ppermute | solution.py:297
  6.0 1.9 %collective-permute-start.1 = (bf16[136,128]{1,0:T(8,128)(2,1)S(1)}, bf16[136,128]{1,0:T(8,128)(2,1)S(1)}, u32[]{:S(2)}, u32[]{:S(2)}) collective-permute-start(bf16[136,128]{1,0:T(8,128)(2,1)S(1)} %shard_map.55.part0), channel_id=1, source_target_pairs={{0,2},{1,3},{2,0},{3,1},{4,6},{5,7},{6,4},{7,5},{8,10},{9,11},{10,... | collective-permute-start | bytes 104456 | tf_op jit(solution)/shard_map/ppermute | solution.py:303
  8.0 1.2 collective-permute-start.2
  9.1 0.9 collective-permute-done.part1
  10.4 0.8 collective-permute-done.2.part3
  11.3 1.8 %shard_map.56.after = bf16[32,72,128]{2,1,0:T(8,128)(2,1)} custom-call(s32[1]{0:T(128)} %bitcast.4.info, bf16[136,128]{1,0:T(8,128)(2,1)S(1)} %shard_map.55.part0, bf16[136,128]{1,0:T(8,128)(2,1)S(1)} %collective-permute-done.part1, bf16[136,128]{1,0:T(8,128)(2,1)S(1)} %collective-permute-done.1.part2, bf16[136,128]{1,0:T(8,128)(2,1)S(1)} %collective-permute-done.2.part3), custom_call_target="tpu_custom_call" | custom-call | bytes 2097152 | tf_op jit(solution)/shard_map/pallas_call | solution.py:304
  13.1 10.8 %all-to-all-start = ((bf16[32,72,128]{2,1,0:T(8,128)(2,1)}), bf16[32,72,128]{2,1,0:T(8,128)(2,1)S(1)}, u32[]{:S(2)}, u32[]{:S(2)}) async-start(bf16[32,72,128]{2,1,0:T(8,128)(2,1)} %shard_map.56.after), calls=%async_computation | async-start | bytes 1179648 | tf_op jit(solution)/shard_map/all_to_all | solution.py:307
  23.9 16.5 %all-to-all-done.arrived.after = bf16[32,72,128]{2,1,0:T(8,128)(2,1)S(1)} async-done(((bf16[32,72,128]{2,1,0:T(8,128)(2,1)}), bf16[32,72,128]{2,1,0:T(8,128)(2,1)S(1)}, u32[]{:S(2)}, u32[]{:S(2)}) %all-to-all-start) | async-done | bytes 589856 | tf_op jit(solution)/shard_map/all_to_all | solution.py:307
  40.4 3.5 %collective-permute-start.4 = (bf16[32,72,128]{2,1,0:T(8,128)(2,1)S(1)}, bf16[32,72,128]{2,1,0:T(8,128)(2,1)S(1)}, u32[]{:S(2)}, u32[]{:S(2)}) collective-permute-start(bf16[32,72,128]{2,1,0:T(8,128)(2,1)S(1)} %all-to-all-done.arrived.after), channel_id=1, source_target_pairs={{0,4},{4,0},{1,5},{5,1},{2,6},{6,2},{3,7},{7,3},{8,12},{12,8},{9,1... | collective-permute-start | bytes 1769480 | tf_op jit(solution)/shard_map/ppermute | solution.py:316
  43.9 4.9 %shard_map.57.weights = bf16[4096,640]{1,0:T(8,128)(2,1)} custom-call(s32[1]{0:T(128)} %bitcast.core_ref.info, bf16[1,2048,1280]{2,1,0:T(8,128)(2,1)} %w_own.1, bf16[1,2048,1280]{2,1,0:T(8,128)(2,1)} %collective-permute-done.3.w_other, bf16[32,72,128]{2,1,0:T(8,128)(2,1)} %shard_map.56.after), custom_call_target="tpu_custom_call" | custom-call | flops 10000000000 | bytes 2097152 | tf_op jit(solution)/shard_map/pallas_call | solution.py:308
  48.8 9.1 %shard_map.58 = (s16[264,640]{1,0:T(8,128)(2,1)}, s16[264,640]{1,0:T(8,128)(2,1)}) custom-call(s32[5]{0:T(128)S(1)} %stack.29.info, bf16[32,72,128]{2,1,0:T(8,128)(2,1)S(1)} %all-to-all-done.arrived.after, bf16[4096,640]{1,0:T(8,128)(2,1)} %shard_map.57.weights, bf16[32,72,128]{2,1,0:T(8,128)(2,1)S(1)} %all-to-all-done.arrived.after), custom_call_target="tpu_custom_call" | custom-call | flops 2684354560 | bytes 2097152 | tf_op jit(solution)/shard_map/pallas_call | solution.py:342
  58.6 1.8 %collective-permute-start.6 = (s16[264,640]{1,0:T(8,128)(2,1)}, s16[264,640]{1,0:T(8,128)(2,1)S(1)}, u32[]{:S(2)}, u32[]{:S(2)}) collective-permute-start(s16[264,640]{1,0:T(8,128)(2,1)} %get-tuple-element.17), channel_id=1, source_target_pairs={{0,24},{8,16},{16,8},{24,0},{1,25},{9,17},{17,9},{25,1},{2,26},{10... | collective-permute-start | bytes 1013768 | tf_op jit(solution)/shard_map/ppermute | solution.py:339
  60.4 8.2 %shard_map.59 = (s16[264,640]{1,0:T(8,128)(2,1)S(1)}, s16[264,640]{1,0:T(8,128)(2,1)S(1)}) custom-call(s32[5]{0:T(128)S(1)} %stack.29.info, bf16[32,72,128]{2,1,0:T(8,128)(2,1)S(1)} %collective-permute-done.4.arrived, bf16[4096,640]{1,0:T(8,128)(2,1)} %shard_map.57.weights, s16[264,640]{1,0:T(8,128)(2,1)} %get-tuple-element.15.after), custom_call_target="tpu_custom_call" | custom-call | flops 2684354560 | bytes 2097152 | tf_op jit(solution)/shard_map/pallas_call | solution.py:346
  68.6 1.0 collective-permute-start.10
  69.7 7.9 %shard_map.60.kept = f32[512,640]{1,0:T(8,128)S(1)} custom-call(s32[5]{0:T(128)S(1)} %stack.27.info, bf16[32,72,128]{2,1,0:T(8,128)(2,1)S(1)} %all-to-all-done.arrived.after, bf16[4096,640]{1,0:T(8,128)(2,1)} %shard_map.57.weights, s16[264,640]{1,0:T(8,128)(2,1)S(1)} %get-tuple-element.16.after), custom_call_target="tpu_custom_call" | custom-call | flops 2684354560 | bytes 2097152 | tf_op jit(solution)/shard_map/pallas_call | solution.py:350
  78.3 2.1 %collective-permute-start.7 = (s16[136,640]{1,0:T(8,128)(2,1)S(1)}, s16[136,640]{1,0:T(8,128)(2,1)S(1)}, u32[]{:S(2)}, u32[]{:S(2)}) collective-permute-start(s16[136,640]{1,0:T(8,128)(2,1)S(1)} %get-tuple-element.19.after), channel_id=1, source_target_pairs={{0,24},{8,16},{16,8},{24,0},{1,25},{9,17},{17,9},{25,1},{2,26},{10... | collective-permute-start | bytes 522248 | tf_op jit(solution)/shard_map/ppermute | solution.py:338
  80.4 6.8 %shard_map.62 = (f32[256,640]{1,0:T(8,128)S(1)}, s16[136,640]{1,0:T(8,128)(2,1)S(1)}, s16[136,640]{1,0:T(8,128)(2,1)S(1)}) custom-call(s32[5]{0:T(128)S(1)} %stack.27.info, bf16[32,72,128]{2,1,0:T(8,128)(2,1)S(1)} %collective-permute-done.4.arrived, bf16[4096,640]{1,0:T(8,128)(2,1)} %shard_map.57.weights, s16[136,640]{1,0:T(8,128)(2,1)S(1)} %get-tuple-element.19.after, ...), custom_call_target="tpu_custom_call" | custom-call | flops 2684354560 | bytes 2097152 | tf_op jit(solution)/shard_map/pallas_call | solution.py:360
  87.2 1.0 collective-permute-start.11
  88.4 1.2 collective-permute-start.8
  89.6 3.7 %collective-permute-done.11.refs_4_ = s16[136,640]{1,0:T(8,128)(2,1)S(1)} collective-permute-done((s16[136,640]{1,0:T(8,128)(2,1)S(1)}, s16[136,640]{1,0:T(8,128)(2,1)S(1)}, u32[]{:S(2)}, u32[]{:S(2)}) %collective-permute-start.11) | collective-permute-done | bytes 174112 | tf_op jit(solution)/shard_map/ppermute | solution.py:338
  93.3 3.1 %collective-permute-done.8.refs_2_ = s16[136,640]{1,0:T(8,128)(2,1)S(1)} collective-permute-done((s16[136,640]{1,0:T(8,128)(2,1)S(1)}, s16[136,640]{1,0:T(8,128)(2,1)S(1)}, u32[]{:S(2)}, u32[]{:S(2)}) %collective-permute-start.8) | collective-permute-done | bytes 174112 | tf_op jit(solution)/shard_map/ppermute | solution.py:339
  96.4 0.8 shard_map.63
  97.2 27.8 %all_to_all.10.ref = s16[16,32,768]{2,1,0:T(8,128)(2,1)S(1)} all-to-all(s16[16,32,768]{2,1,0:T(8,128)(2,1)S(1)} %shard_map.63), channel_id=1, replica_groups=mesh['z'=8,'y'=4,'c'=2,'x'=4] {'z','c'}, dimensions={0} | all-to-all | bytes 1572864 | tf_op jit(solution)/shard_map/all_to_all | solution.py:374
  125.0 0.9 shard_map.64
  (25 shorter events, 5.1 us)
Async XLA Ops:
  0.0 43.9 %collective-permute-start.3 = (bf16[1,2048,1280]{2,1,0:T(8,128)(2,1)}, bf16[1,2048,1280]{2,1,0:T(8,128)(2,1)}, u32[]{:S(2)}, u32[]{:S(2)}) collective-permute-start(bf16[1,2048,1280]{2,1,0:T(8,128)(2,1)} %w_own.1), channel_id=1, source_target_pairs={{0,4},{4,0},{1,5},{5,1},{2,6},{6,2},{3,7},{7,3},{8,12},{12,8},{9,1... | collective-permute-start | bytes 15728648 | tf_op jit(solution)/shard_map/ppermute | solution.py:297
  3.2 0.8 copy-start
  4.0 0.7 copy-start.2
  4.6 0.7 copy-start.3
  6.0 4.0 %collective-permute-start = (bf16[136,128]{1,0:T(8,128)(2,1)S(1)}, bf16[136,128]{1,0:T(8,128)(2,1)S(1)}, u32[]{:S(2)}, u32[]{:S(2)}) collective-permute-start(bf16[136,128]{1,0:T(8,128)(2,1)S(1)} %shard_map.55.part0), channel_id=1, source_target_pairs={{0,1},{1,2},{2,3},{3,0},{4,5},{5,6},{6,7},{7,4},{8,9},{9,10},{10,1... | collective-permute-start | bytes 104456 | tf_op jit(solution)/shard_map/ppermute | solution.py:303
  6.0 4.4 %collective-permute-start.1 = (bf16[136,128]{1,0:T(8,128)(2,1)S(1)}, bf16[136,128]{1,0:T(8,128)(2,1)S(1)}, u32[]{:S(2)}, u32[]{:S(2)}) collective-permute-start(bf16[136,128]{1,0:T(8,128)(2,1)S(1)} %shard_map.55.part0), channel_id=1, source_target_pairs={{0,2},{1,3},{2,0},{3,1},{4,6},{5,7},{6,4},{7,5},{8,10},{9,11},{10,... | collective-permute-start | bytes 104456 | tf_op jit(solution)/shard_map/ppermute | solution.py:303
  8.0 3.3 %collective-permute-start.2 = (bf16[136,128]{1,0:T(8,128)(2,1)S(1)}, bf16[136,128]{1,0:T(8,128)(2,1)S(1)}, u32[]{:S(2)}, u32[]{:S(2)}) collective-permute-start(bf16[136,128]{1,0:T(8,128)(2,1)S(1)} %shard_map.55.part0), channel_id=1, source_target_pairs={{0,3},{1,0},{2,1},{3,2},{4,7},{5,4},{6,5},{7,6},{8,11},{9,8},{10,9... | collective-permute-start | bytes 104456 | tf_op jit(solution)/shard_map/ppermute | solution.py:303
  13.1 27.4 %all-to-all-start = ((bf16[32,72,128]{2,1,0:T(8,128)(2,1)}), bf16[32,72,128]{2,1,0:T(8,128)(2,1)S(1)}, u32[]{:S(2)}, u32[]{:S(2)}) async-start(bf16[32,72,128]{2,1,0:T(8,128)(2,1)} %shard_map.56.after), calls=%async_computation | async-start | bytes 1179648 | tf_op jit(solution)/shard_map/all_to_all | solution.py:307
  40.4 20.0 %collective-permute-start.4 = (bf16[32,72,128]{2,1,0:T(8,128)(2,1)S(1)}, bf16[32,72,128]{2,1,0:T(8,128)(2,1)S(1)}, u32[]{:S(2)}, u32[]{:S(2)}) collective-permute-start(bf16[32,72,128]{2,1,0:T(8,128)(2,1)S(1)} %all-to-all-done.arrived.after), channel_id=1, source_target_pairs={{0,4},{4,0},{1,5},{5,1},{2,6},{6,2},{3,7},{7,3},{8,12},{12,8},{9,1... | collective-permute-start | bytes 1769480 | tf_op jit(solution)/shard_map/ppermute | solution.py:316
  57.9 19.7 %collective-permute-start.5 = (s16[264,640]{1,0:T(8,128)(2,1)}, s16[264,640]{1,0:T(8,128)(2,1)S(1)}, u32[]{:S(2)}, u32[]{:S(2)}) collective-permute-start(s16[264,640]{1,0:T(8,128)(2,1)} %get-tuple-element.15.after), channel_id=1, source_target_pairs={{0,8},{8,0},{16,24},{24,16},{1,9},{9,1},{17,25},{25,17},{2,10},{10... | collective-permute-start | bytes 1013768 | tf_op jit(solution)/shard_map/ppermute | solution.py:338
  58.6 19.0 %collective-permute-start.6 = (s16[264,640]{1,0:T(8,128)(2,1)}, s16[264,640]{1,0:T(8,128)(2,1)S(1)}, u32[]{:S(2)}, u32[]{:S(2)}) collective-permute-start(s16[264,640]{1,0:T(8,128)(2,1)} %get-tuple-element.17), channel_id=1, source_target_pairs={{0,24},{8,16},{16,8},{24,0},{1,25},{9,17},{17,9},{25,1},{2,26},{10... | collective-permute-start | bytes 1013768 | tf_op jit(solution)/shard_map/ppermute | solution.py:339
  68.6 11.7 %collective-permute-start.10 = (s16[264,640]{1,0:T(8,128)(2,1)S(1)}, s16[264,640]{1,0:T(8,128)(2,1)S(1)}, u32[]{:S(2)}, u32[]{:S(2)}) collective-permute-start(s16[264,640]{1,0:T(8,128)(2,1)S(1)} %get-tuple-element.21), channel_id=1, source_target_pairs={{0,24},{8,16},{16,8},{24,0},{1,25},{9,17},{17,9},{25,1},{2,26},{10... | collective-permute-start | bytes 1013768 | tf_op jit(solution)/shard_map/ppermute | solution.py:339
  69.6 10.8 %collective-permute-start.9 = (s16[264,640]{1,0:T(8,128)(2,1)S(1)}, s16[264,640]{1,0:T(8,128)(2,1)S(1)}, u32[]{:S(2)}, u32[]{:S(2)}) collective-permute-start(s16[264,640]{1,0:T(8,128)(2,1)S(1)} %get-tuple-element.16.after), channel_id=1, source_target_pairs={{0,8},{8,0},{16,24},{24,16},{1,9},{9,1},{17,25},{25,17},{2,10},{10... | collective-permute-start | bytes 1013768 | tf_op jit(solution)/shard_map/ppermute | solution.py:338
  78.2 46.8 %copy-start.1 = (f32[1,1280]{1,0:T(1,128)S(1)}, f32[1,1280]{1,0:T(1,128)}, u32[]{:S(2)}) copy-start(f32[1,1280]{1,0:T(1,128)} %bias.1) | copy-start | bytes 15364
  78.3 15.0 %collective-permute-start.7 = (s16[136,640]{1,0:T(8,128)(2,1)S(1)}, s16[136,640]{1,0:T(8,128)(2,1)S(1)}, u32[]{:S(2)}, u32[]{:S(2)}) collective-permute-start(s16[136,640]{1,0:T(8,128)(2,1)S(1)} %get-tuple-element.19.after), channel_id=1, source_target_pairs={{0,24},{8,16},{16,8},{24,0},{1,25},{9,17},{17,9},{25,1},{2,26},{10... | collective-permute-start | bytes 522248 | tf_op jit(solution)/shard_map/ppermute | solution.py:338
  87.2 6.1 %collective-permute-start.11 = (s16[136,640]{1,0:T(8,128)(2,1)S(1)}, s16[136,640]{1,0:T(8,128)(2,1)S(1)}, u32[]{:S(2)}, u32[]{:S(2)}) collective-permute-start(s16[136,640]{1,0:T(8,128)(2,1)S(1)} %get-tuple-element.23), channel_id=1, source_target_pairs={{0,24},{8,16},{16,8},{24,0},{1,25},{9,17},{17,9},{25,1},{2,26},{10... | collective-permute-start | bytes 522248 | tf_op jit(solution)/shard_map/ppermute | solution.py:338
  88.1 5.2 %collective-permute-start.12 = (s16[136,640]{1,0:T(8,128)(2,1)S(1)}, s16[136,640]{1,0:T(8,128)(2,1)S(1)}, u32[]{:S(2)}, u32[]{:S(2)}) collective-permute-start(s16[136,640]{1,0:T(8,128)(2,1)S(1)} %get-tuple-element.24), channel_id=1, source_target_pairs={{0,8},{8,0},{16,24},{24,16},{1,9},{9,1},{17,25},{25,17},{2,10},{10... | collective-permute-start | bytes 522248 | tf_op jit(solution)/shard_map/ppermute | solution.py:339
  88.4 8.0 %collective-permute-start.8 = (s16[136,640]{1,0:T(8,128)(2,1)S(1)}, s16[136,640]{1,0:T(8,128)(2,1)S(1)}, u32[]{:S(2)}, u32[]{:S(2)}) collective-permute-start(s16[136,640]{1,0:T(8,128)(2,1)S(1)} %get-tuple-element.20), channel_id=1, source_target_pairs={{0,8},{8,0},{16,24},{24,16},{1,9},{9,1},{17,25},{25,17},{2,10},{10... | collective-permute-start | bytes 522248 | tf_op jit(solution)/shard_map/ppermute | solution.py:339

commit v5 on v4

--- a/solution.py
+++ b/solution.py
@@ -31,8 +31,8 @@
 HBM = pl.BlockSpec(memory_space=pltpu.HBM)
 ANY = pl.BlockSpec(memory_space=pl.ANY)
 PIECES = 4
-GRANT = 48
-WEIGHT_GRANT = 50
+GRANT = 18
+WEIGHT_GRANT = 8
 
 
 def ring(n, k):
@@ -55,8 +55,18 @@
     return jnp.transpose(jnp.broadcast_to(row, (128, 128)))
 
 
-def wrap_kernel(counts, coeffs, ids, out_ref):
+def wrap_kernel(counts_in, coeffs_in, ids_in, out_ref, counts, coeffs, ids, sems):
     n = OWN * ACTIVE
+    copies = [
+        pltpu.make_async_copy(ref, to, sems.at[k])
+        for k, (ref, to) in enumerate(
+            ((counts_in, counts), (coeffs_in, coeffs), (ids_in, ids))
+        )
+    ]
+    for copy in copies:
+        copy.start()
+    for copy in copies:
+        copy.wait()
     slot = lax.broadcasted_iota(jnp.int32, (ACTIVE, BLOCK), 0)
     for i in range(OWN):
         live = slot < counts[i]
@@ -213,21 +223,14 @@
     lax.fori_loop(0, 4 * PART // TOK, source, 0)
 
 
-def multiply(info, arrived, weights, tok, coef, x_buf, w_buf, sems, acc):
-    deep = w_buf.shape[0] // PIECES
-    copies = []
-    for g in range(PIECES):
-        here = slice(g * deep, (g + 1) * deep)
-        copies.append(pltpu.make_async_copy(weights.at[here], w_buf.at[here], sems.at[g]))
-    for copy in copies:
-        copy.start()
+def multiply(info, arrived, weights, tok, coef, x_buf, acc):
     prepare(info, arrived, tok, coef)
     build(info, tok, coef, x_buf)
-    for g, copy in enumerate(copies):
-        here = slice(g * deep, (g + 1) * deep)
-        copy.wait()
-        term = jnp.dot(x_buf[:, here], w_buf[here, :], preferred_element_type=jnp.float32)
-        acc[...] = term if g == 0 else acc[...] + term
+    for h in range(2):
+        here = slice(h * 2 * PART, (h + 1) * 2 * PART)
+        acc[here, :] = jnp.dot(
+            x_buf[here, :], weights[...], preferred_element_type=jnp.float32
+        )
 
 
 def send_kernel(info, arrived, weights, after, out0, out1, acc, *scratch):
@@ -260,32 +263,36 @@
         )
 
 
-def last_kernel(info, *refs):
+def last_kernel(info, kept, in0, in1, *rest):
+    outs, acc = rest[:-1], rest[-1]
+    width = kept.shape[1]
+    for h, ref in enumerate((in0, in1)):
+        here = slice(h * PART, (h + 1) * PART)
+        acc[here, :] = kept[here, :] + read_message(ref, 0)
+    for k, out in enumerate(outs):
+        rows = pl.ds(pl.multiple_of(lax.rem(info[1] + k, NZ) * TOK, TOK), TOK)
+        if out.shape[1] == width:
+            out[...] = acc[rows, :]
+            continue
+        v, code = quantized(acc[rows, :])
+        out[:, 0:width] = v
+        code = jnp.broadcast_to(code, (TOK, 128)).astype(jnp.int32).astype(jnp.int16)
+        out[:, width : width + 128] = code
+
+
+def final_kernel(info, bias, kept, *refs):
     ins, out_ref = refs[:-1], refs[-1]
-    width = ins[0].shape[1]
+    width = kept.shape[1]
+    acc = kept[...]
     for q in range(NC):
-        kept, messages = ins[3 * q], ins[3 * q + 1 : 3 * q + 3]
-        c = lax.rem(info[0] + q, NC)
-        for h, ref in enumerate(messages):
-            acc = kept[h * PART : (h + 1) * PART, :] + read_message(ref, 0)
-            v, code = quantized(acc)
-            code = jnp.broadcast_to(code, (PART, 128)).astype(jnp.int32).astype(jnp.int16)
-            for j in range(PART // TOK):
-                d = (h * (PART // TOK) + j) * NC + c
-                here = slice(j * TOK, (j + 1) * TOK)
-                out_ref[d, :, 0:width] = v[here, :]
-                out_ref[d, :, width : width + 128] = code[here, :]
-
-
-def final_kernel(ref, bias, out_ref):
-    width = out_ref.shape[2] // NC
-    for c in range(NC):
-        acc = jnp.broadcast_to(bias[:, c * width : (c + 1) * width], (TOK, width))
-        for z in range(NZ):
-            both = ref[z * NC + c].astype(jnp.int32).astype(jnp.float32)
+        if q > 0:
+            acc = jnp.zeros_like(acc)
+        for ref in ins[0 : NZ - 1] if q == 0 else ins[NZ - 1 :]:
+            both = ref[...].astype(jnp.int32).astype(jnp.float32)
             scale = jnp.exp(both[:, width : width + 1] * (LN2 / STEP))
             acc = acc + both[:, 0:width] * scale
-        out_ref[0, :, c * width : (c + 1) * width] = acc.astype(jnp.bfloat16)
+        at = pl.ds(pl.multiple_of(lax.rem(info[0] + q, NC) * width, 128), width)
+        out_ref[0, :, at] = (acc + bias[:, at]).astype(jnp.bfloat16)
 
 
 def run(coefficients, block_ids, counts, decoder, bias):
@@ -298,7 +305,16 @@
 
     shape = jax.ShapeDtypeStruct
     packed = call(
-        wrap_kernel, shape((OWN * (ACTIVE + 1), BLOCK), jnp.bfloat16), [SMEM, VMEM, VMEM], 10
+        wrap_kernel,
+        shape((OWN * (ACTIVE + 1), BLOCK), jnp.bfloat16),
+        [HBM, HBM, HBM],
+        10,
+        scratch=[
+            pltpu.SMEM((OWN,), jnp.int32),
+            pltpu.VMEM((OWN, ACTIVE, BLOCK), jnp.bfloat16),
+            pltpu.VMEM((OWN, ACTIVE), jnp.int32),
+            pltpu.SemaphoreType.DMA((3,)),
+        ],
     )(counts, coefficients, block_ids)
     parts = [packed] + [lax.ppermute(packed, "x", ring(NX, k)) for k in range(1, NX)]
     outgoing = call(
@@ -329,10 +345,8 @@
         pltpu.VMEM((CHIPS, SLOTS, BLOCK), jnp.float32),
         pltpu.VMEM((CHIPS, SLOTS, BLOCK), jnp.float32),
         pltpu.VMEM((4 * PART, NC * depth), jnp.bfloat16),
-        pltpu.VMEM((NC * depth, width), jnp.bfloat16),
-        pltpu.SemaphoreType.DMA((PIECES,)),
     ]
-    given = [SMEM, VMEM, HBM, ANY]
+    given = [SMEM, VMEM, VMEM, ANY]
 
     def cross(m0, m1, pair0, pair1):
         m0 = lax.ppermute(m0, "y", pair0)
@@ -366,12 +380,29 @@
         **product,
     )(kept_for, other, weights, m0, *crossing1)
     arrived1 = cross(m0, m1, pair_b, pair_a)
-    out = call(
-        last_kernel, shape((NZ * NC, TOK, width + 128), jnp.int16), [SMEM] + [VMEM] * 6, 10
-    )(core.reshape(1), kept0, *arrived0, kept1, *arrived1)
+    z = lax.axis_index("z").astype(jnp.int32)
+    place = jnp.stack([core, z])
+    piece = shape((TOK, width + 128), jnp.int16)
+    grown = [pltpu.VMEM((2 * PART, width), jnp.float32)]
+    final = []
+    for q, (kept, arrived) in enumerate(((kept0, arrived0), (kept1, arrived1))):
+        mine = shape((TOK, width), jnp.float32) if q == 0 else piece
+        pieces = call(
+            last_kernel, [mine] + [piece] * (NZ - 1), [SMEM] + [VMEM] * 3, 10, scratch=grown
+        )(place, kept, *arrived)
+        for k, sent in enumerate(pieces):
+            if q == 0:
+                final.append(sent if k == 0 else lax.ppermute(sent, "z", ring(NZ, k)))
+            else:
+                hops = [
+                    (i * NC + c, (i + k) % NZ * NC + 1 - c)
+                    for i in range(NZ)
+                    for c in range(NC)
+                ]
+                final.append(lax.ppermute(sent, ("z", "c"), hops))
     return call(
-        final_kernel, shape((1, TOK, full), jnp.bfloat16), [VMEM] * 2, 10
-    )(lax.all_to_all(out, ("z", "c"), 0, 0, tiled=True), bias)
+        final_kernel, shape((1, TOK, full), jnp.bfloat16), [SMEM] + [VMEM] * (1 + 2 * NZ), 10
+    )(place, bias, *final)
 
 
 def solution(mesh):

time: 126 us -> 127 us (level)
  starting transfers between devices: 28.7 us -> 57.3 us
  blocking collectives: 27.8 us -> 0 us
  Pallas kernels: 41.6 us -> 35.3 us
  local copies, waits for them, and re-layouts: 2.27 us -> 7.25 us
    ppermute x0 -> x15, starting transfers between devices: none -> 29.5 us  [the longest x8 15.4 us: run(): final.append(lax.ppermute(sent, ('z', 'c'), hops))]
    all_to_all x1 -> x0, blocking collectives: 27.8 us -> none  [run(): lax.all_to_all(out, ('z', 'c'), 0, 0, tiled=True)]
    unnamed x8 -> x14, local copies, waits for them, and re-layouts: 2.1 us -> 7.08 us
    ppermute x0 -> x15, waiting for transfers between devices: none -> 4.81 us  [the longest x7 4.79 us: run(): final.append(sent if k == 0 else lax.ppermute(sent, 'z', ring(NZ, k)))]
    pallas_call x2, Pallas kernels: 17.3 us -> 13.9 us  [run(): call(send_kernel, [message, message], given, GRANT, scratch=[total] + scr...]
    pallas_call x1, Pallas kernels: 4.86 us -> 1.97 us  [run(): call(weights_kernel, shape((NC * depth, width), jnp.bfloat16), [SMEM, HBM...]
    ppermute x4, waiting for transfers between devices: 3.13 us -> 0.38 us  [cross(): m1 = lax.ppermute(m1, 'y', pair1)]
    pallas_call x1, Pallas kernels: 7.86 us -> 5.99 us  [run(): call(keep_kernel, [shape((4 * PART, width), jnp.float32)], given, GRANT,...]
  transfers between devices with their start and end apart: 14 -> 29, of which waited for: 6 -> 9; matrix products, arithmetic and copies ran while one was open for 0% -> 0% of each run, Pallas kernels for 32% -> 22%
where the time goes in v5:
time: 127 us; the launch traced here: 126 us
  starting transfers between devices  57.3 us (45%)
  Pallas kernels  35.3 us (28%)
  waiting for transfers between devices  26.2 us (21%)
  local copies, waits for them, and re-layouts  7.25 us (6%)
    all_to_all x1, waiting for transfers between devices, run(): own = lax.all_to_all(outgoing, ('z', 'y'), 0, 0, tiled=True)  16.5 us
    ppermute x8, starting transfers between devices, run(): final.append(lax.ppermute(sent, ('z', 'c'), hops))  15.4 us
    ppermute x7, starting transfers between devices, run(): final.append(sent if k == 0 else lax.ppermute(sent, 'z', ring(NZ, k)))  14.2 us
    pallas_call x2, Pallas kernels, run(): call(send_kernel, [message, message], given, GRANT, scratch=[total] + scr...  13.9 us
    all_to_all x1, starting transfers between devices, run(): own = lax.all_to_all(outgoing, ('z', 'y'), 0, 0, tiled=True)  10.8 us
    unnamed x14, local copies, waits for them, and re-layouts  7.08 us
    pallas_call x1, Pallas kernels, run(): call(keep_middle_kernel, [kept, small, small], given + [VMEM] * 2, GRANT,...  6.24 us
    pallas_call x1, Pallas kernels, run(): call(keep_kernel, [shape((4 * PART, width), jnp.float32)], given, GRANT,...  5.99 us
  transfers between devices with their start and end apart: 29, of which 9 were waited for; matrix products, arithmetic and copies ran while one was open for 0% of the time, Pallas kernels for 22%

profile of v5, /device:TPU:1, one launch (start us, length us, event | category | flops | bytes accessed | tf_op | source)
XLA Modules:
  0.0 126.3 jit_solution(9299753061943599308)
XLA Ops:
  0.0 3.2 %collective-permute-start.3 = (bf16[1,2048,1280]{2,1,0:T(8,128)(2,1)}, bf16[1,2048,1280]{2,1,0:T(8,128)(2,1)}, u32[]{:S(2)}, u32[]{:S(2)}) collective-permute-start(bf16[1,2048,1280]{2,1,0:T(8,128)(2,1)} %w_own.1), channel_id=1, source_target_pairs={{0,4},{4,0},{1,5},{5,1},{2,6},{6,2},{3,7},{7,3},{8,12},{12,8},{9,1... | collective-permute-start | bytes 15728648 | tf_op jit(solution)/shard_map/ppermute | solution.py:304
  6.1 1.9 %collective-permute-start.1 = (bf16[136,128]{1,0:T(8,128)(2,1)S(1)}, bf16[136,128]{1,0:T(8,128)(2,1)S(1)}, u32[]{:S(2)}, u32[]{:S(2)}) collective-permute-start(bf16[136,128]{1,0:T(8,128)(2,1)S(1)} %shard_map.55.part0), channel_id=1, source_target_pairs={{0,2},{1,3},{2,0},{3,1},{4,6},{5,7},{6,4},{7,5},{8,10},{9,11},{10,... | collective-permute-start | bytes 104456 | tf_op jit(solution)/shard_map/ppermute | solution.py:319
  11.3 1.8 %shard_map.56.after = bf16[32,72,128]{2,1,0:T(8,128)(2,1)} custom-call(s32[1]{0:T(128)} %bitcast.5.info, bf16[136,128]{1,0:T(8,128)(2,1)S(1)} %shard_map.55.part0, bf16[136,128]{1,0:T(8,128)(2,1)S(1)} %collective-permute-done.part1, bf16[136,128]{1,0:T(8,128)(2,1)S(1)} %collective-permute-done.1.part2, bf16[136,128]{1,0:T(8,128)(2,1)S(1)} %collective-permute-done.2.part3), custom_call_target="tpu_custom_call" | custom-call | bytes 2097152 | tf_op jit(solution)/shard_map/pallas_call | solution.py:320
  13.1 10.8 %all-to-all-start = ((bf16[32,72,128]{2,1,0:T(8,128)(2,1)}), bf16[32,72,128]{2,1,0:T(8,128)(2,1)S(1)}, u32[]{:S(2)}, u32[]{:S(2)}) async-start(bf16[32,72,128]{2,1,0:T(8,128)(2,1)} %shard_map.56.after), calls=%async_computation | async-start | bytes 1179648 | tf_op jit(solution)/shard_map/all_to_all | solution.py:323
  24.0 16.5 %all-to-all-done.arrived.after = bf16[32,72,128]{2,1,0:T(8,128)(2,1)S(1)} async-done(((bf16[32,72,128]{2,1,0:T(8,128)(2,1)}), bf16[32,72,128]{2,1,0:T(8,128)(2,1)S(1)}, u32[]{:S(2)}, u32[]{:S(2)}) %all-to-all-start) | async-done | bytes 589856 | tf_op jit(solution)/shard_map/all_to_all | solution.py:323
  40.5 3.5 %collective-permute-start.4 = (bf16[32,72,128]{2,1,0:T(8,128)(2,1)S(1)}, bf16[32,72,128]{2,1,0:T(8,128)(2,1)S(1)}, u32[]{:S(2)}, u32[]{:S(2)}) collective-permute-start(bf16[32,72,128]{2,1,0:T(8,128)(2,1)S(1)} %all-to-all-done.arrived.after), channel_id=1, source_target_pairs={{0,4},{4,0},{1,5},{5,1},{2,6},{6,2},{3,7},{7,3},{8,12},{12,8},{9,1... | collective-permute-start | bytes 1769480 | tf_op jit(solution)/shard_map/ppermute | solution.py:332
  44.0 2.5 %copy-done.4 = bf16[1,2048,1280]{2,1,0:T(8,128)(2,1)S(1)} copy-done((bf16[1,2048,1280]{2,1,0:T(8,128)(2,1)S(1)}, bf16[1,2048,1280]{2,1,0:T(8,128)(2,1)}, u32[]{:S(2)}) %copy-start.4) | copy-done | bytes 5242904
  46.5 2.0 %shard_map.57.weights = bf16[4096,640]{1,0:T(8,128)(2,1)S(1)} custom-call(s32[1]{0:T(128)} %bitcast.core_ref, bf16[1,2048,1280]{2,1,0:T(8,128)(2,1)S(1)} %copy-done.4, bf16[1,2048,1280]{2,1,0:T(8,128)(2,1)} %collective-permute-done.3.w_other, bf16[32,72,128]{2,1,0:T(8,128)(2,1)} %shard_map.56.after), custom_call_target="tpu_custom_call" | custom-call | flops 10000000000 | bytes 2097152 | tf_op jit(solution)/shard_map/pallas_call | solution.py:324
  48.5 6.9 %shard_map.58 = (s16[264,640]{1,0:T(8,128)(2,1)}, s16[264,640]{1,0:T(8,128)(2,1)S(1)}) custom-call(s32[5]{0:T(128)S(1)} %stack.41.info, bf16[32,72,128]{2,1,0:T(8,128)(2,1)S(1)} %all-to-all-done.arrived.after, bf16[4096,640]{1,0:T(8,128)(2,1)S(1)} %shard_map.57.weights, bf16[32,72,128]{2,1,0:T(8,128)(2,1)S(1)} %all-to-all-done.arrived.after), custom_call_target="tpu_custom_call" | custom-call | flops 2684354560 | bytes 2097152 | tf_op jit(solution)/shard_map/pallas_call | solution.py:356
  56.0 1.8 %collective-permute-start.6 = (s16[264,640]{1,0:T(8,128)(2,1)S(1)}, s16[264,640]{1,0:T(8,128)(2,1)S(1)}, u32[]{:S(2)}, u32[]{:S(2)}) collective-permute-start(s16[264,640]{1,0:T(8,128)(2,1)S(1)} %get-tuple-element.33), channel_id=1, source_target_pairs={{0,24},{8,16},{16,8},{24,0},{1,25},{9,17},{17,9},{25,1},{2,26},{10... | collective-permute-start | bytes 1013768 | tf_op jit(solution)/shard_map/ppermute | solution.py:353
  57.8 6.9 %shard_map.59 = (s16[264,640]{1,0:T(8,128)(2,1)}, s16[264,640]{1,0:T(8,128)(2,1)S(1)}) custom-call(s32[5]{0:T(128)S(1)} %stack.41.info, bf16[32,72,128]{2,1,0:T(8,128)(2,1)S(1)} %collective-permute-done.4.arrived, bf16[4096,640]{1,0:T(8,128)(2,1)S(1)} %shard_map.57.weights, s16[264,640]{1,0:T(8,128)(2,1)} %get-tuple-element.31.after), custom_call_target="tpu_custom_call" | custom-call | flops 2684354560 | bytes 2097152 | tf_op jit(solution)/shard_map/pallas_call | solution.py:360
  66.0 2.5 %copy-done.6 = bf16[4096,640]{1,0:T(8,128)(2,1)S(1)} copy-done((bf16[4096,640]{1,0:T(8,128)(2,1)S(1)}, bf16[4096,640]{1,0:T(8,128)(2,1)}, u32[]{:S(2)}) %copy-start.6) | copy-done | bytes 5242904
  68.5 6.0 %shard_map.60.kept = f32[512,640]{1,0:T(8,128)S(1)} custom-call(s32[5]{0:T(128)S(1)} %stack.39.info, bf16[32,72,128]{2,1,0:T(8,128)(2,1)S(1)} %all-to-all-done.arrived.after, bf16[4096,640]{1,0:T(8,128)(2,1)S(1)} %copy-done.6, s16[264,640]{1,0:T(8,128)(2,1)} %get-tuple-element.32.after), custom_call_target="tpu_custom_call" | custom-call | flops 2684354560 | bytes 2097152 | tf_op jit(solution)/shard_map/pallas_call | solution.py:364
  75.8 6.2 %shard_map.63 = (f32[256,640]{1,0:T(8,128)S(1)}, s16[136,640]{1,0:T(8,128)(2,1)S(1)}, s16[136,640]{1,0:T(8,128)(2,1)S(1)}) custom-call(s32[5]{0:T(128)S(1)} %stack.39.info, bf16[32,72,128]{2,1,0:T(8,128)(2,1)S(1)} %collective-permute-done.4.arrived, bf16[4096,640]{1,0:T(8,128)(2,1)S(1)} %copy-done.6, s16[136,640]{1,0:T(8,128)(2,1)} %get-tuple-element.35.after, ...), custom_call_target="tpu_custom_call" | custom-call | flops 2684354560 | bytes 2097152 | tf_op jit(solution)/shard_map/pallas_call | solution.py:374
  82.0 1.9 %collective-permute-start.18 = (s16[136,640]{1,0:T(8,128)(2,1)S(1)}, s16[136,640]{1,0:T(8,128)(2,1)S(1)}, u32[]{:S(2)}, u32[]{:S(2)}) collective-permute-start(s16[136,640]{1,0:T(8,128)(2,1)S(1)} %get-tuple-element.47), channel_id=1, source_target_pairs={{0,24},{8,16},{16,8},{24,0},{1,25},{9,17},{17,9},{25,1},{2,26},{10... | collective-permute-start | bytes 522248 | tf_op jit(solution)/shard_map/ppermute | solution.py:352
  85.7 2.4 %collective-permute-done.18.in0 = s16[136,640]{1,0:T(8,128)(2,1)S(1)} collective-permute-done((s16[136,640]{1,0:T(8,128)(2,1)S(1)}, s16[136,640]{1,0:T(8,128)(2,1)S(1)}, u32[]{:S(2)}, u32[]{:S(2)}) %collective-permute-start.18) | collective-permute-done | bytes 174112 | tf_op jit(solution)/shard_map/ppermute | solution.py:352
  89.6 4.2 %collective-permute-start.20 = (s16[32,768]{1,0:T(8,128)(2,1)S(1)}, s16[32,768]{1,0:T(8,128)(2,1)S(1)}, u32[]{:S(2)}, u32[]{:S(2)}) collective-permute-start(s16[32,768]{1,0:T(8,128)(2,1)S(1)} %get-tuple-element.49), channel_id=1, source_target_pairs={{0,4},{4,0},{32,36},{36,32},{64,68},{68,64},{96,100},{100,96},{128... | collective-permute-start | bytes 147464 | tf_op jit(solution)/shard_map/ppermute | solution.py:402
  95.1 1.7 %collective-permute-start.23 = (s16[32,768]{1,0:T(8,128)(2,1)S(1)}, s16[32,768]{1,0:T(8,128)(2,1)S(1)}, u32[]{:S(2)}, u32[]{:S(2)}) collective-permute-start(s16[32,768]{1,0:T(8,128)(2,1)S(1)} %get-tuple-element.52), channel_id=1, source_target_pairs={{0,100},{4,96},{32,132},{36,128},{64,164},{68,160},{96,196},{100,1... | collective-permute-start | bytes 147464 | tf_op jit(solution)/shard_map/ppermute | solution.py:402
  96.8 3.9 %collective-permute-start.24 = (s16[32,768]{1,0:T(8,128)(2,1)S(1)}, s16[32,768]{1,0:T(8,128)(2,1)S(1)}, u32[]{:S(2)}, u32[]{:S(2)}) collective-permute-start(s16[32,768]{1,0:T(8,128)(2,1)S(1)} %get-tuple-element.53), channel_id=1, source_target_pairs={{0,132},{4,128},{32,164},{36,160},{64,196},{68,192},{96,228},{100,... | collective-permute-start | bytes 147464 | tf_op jit(solution)/shard_map/ppermute | solution.py:402
  102.4 2.8 %collective-permute-start.26 = (s16[32,768]{1,0:T(8,128)(2,1)S(1)}, s16[32,768]{1,0:T(8,128)(2,1)S(1)}, u32[]{:S(2)}, u32[]{:S(2)}) collective-permute-start(s16[32,768]{1,0:T(8,128)(2,1)S(1)} %get-tuple-element.55), channel_id=1, source_target_pairs={{0,196},{4,192},{32,228},{36,224},{64,4},{68,0},{96,36},{100,32},{... | collective-permute-start | bytes 147464 | tf_op jit(solution)/shard_map/ppermute | solution.py:402
  107.4 3.5 %collective-permute-start.11 = (s16[32,768]{1,0:T(8,128)(2,1)S(1)}, s16[32,768]{1,0:T(8,128)(2,1)S(1)}, u32[]{:S(2)}, u32[]{:S(2)}) collective-permute-start(s16[32,768]{1,0:T(8,128)(2,1)S(1)} %get-tuple-element.40), channel_id=1, source_target_pairs={{0,96},{32,128},{64,160},{96,192},{128,224},{160,0},{192,32},{224,... | collective-permute-start | bytes 147464 | tf_op jit(solution)/shard_map/ppermute | solution.py:395
  112.1 3.1 %collective-permute-start.13 = (s16[32,768]{1,0:T(8,128)(2,1)S(1)}, s16[32,768]{1,0:T(8,128)(2,1)S(1)}, u32[]{:S(2)}, u32[]{:S(2)}) collective-permute-start(s16[32,768]{1,0:T(8,128)(2,1)S(1)} %get-tuple-element.42), channel_id=1, source_target_pairs={{0,160},{32,192},{64,224},{96,0},{128,32},{160,64},{192,96},{224,1... | collective-permute-start | bytes 147464 | tf_op jit(solution)/shard_map/ppermute | solution.py:395
  115.3 3.4 %collective-permute-start.14 = (s16[32,768]{1,0:T(8,128)(2,1)S(1)}, s16[32,768]{1,0:T(8,128)(2,1)S(1)}, u32[]{:S(2)}, u32[]{:S(2)}) collective-permute-start(s16[32,768]{1,0:T(8,128)(2,1)S(1)} %get-tuple-element.43), channel_id=1, source_target_pairs={{0,192},{32,224},{64,0},{96,32},{128,64},{160,96},{192,128},{224,1... | collective-permute-start | bytes 147464 | tf_op jit(solution)/shard_map/ppermute | solution.py:395
  120.7 3.6 %collective-permute-done.14.refs_5_ = s16[32,768]{1,0:T(8,128)(2,1)S(1)} collective-permute-done((s16[32,768]{1,0:T(8,128)(2,1)S(1)}, s16[32,768]{1,0:T(8,128)(2,1)S(1)}, u32[]{:S(2)}, u32[]{:S(2)}) %collective-permute-start.14) | collective-permute-done | bytes 49184 | tf_op jit(solution)/shard_map/ppermute | solution.py:395
  (62 shorter events, 23.0 us)
Async XLA Ops:
  0.0 44.0 %collective-permute-start.3 = (bf16[1,2048,1280]{2,1,0:T(8,128)(2,1)}, bf16[1,2048,1280]{2,1,0:T(8,128)(2,1)}, u32[]{:S(2)}, u32[]{:S(2)}) collective-permute-start(bf16[1,2048,1280]{2,1,0:T(8,128)(2,1)} %w_own.1), channel_id=1, source_target_pairs={{0,4},{4,0},{1,5},{5,1},{2,6},{6,2},{3,7},{7,3},{8,12},{12,8},{9,1... | collective-permute-start | bytes 15728648 | tf_op jit(solution)/shard_map/ppermute | solution.py:304
  13.1 27.4 %all-to-all-start = ((bf16[32,72,128]{2,1,0:T(8,128)(2,1)}), bf16[32,72,128]{2,1,0:T(8,128)(2,1)S(1)}, u32[]{:S(2)}, u32[]{:S(2)}) async-start(bf16[32,72,128]{2,1,0:T(8,128)(2,1)} %shard_map.56.after), calls=%async_computation | async-start | bytes 1179648 | tf_op jit(solution)/shard_map/all_to_all | solution.py:323
  40.5 17.3 %collective-permute-start.4 = (bf16[32,72,128]{2,1,0:T(8,128)(2,1)S(1)}, bf16[32,72,128]{2,1,0:T(8,128)(2,1)S(1)}, u32[]{:S(2)}, u32[]{:S(2)}) collective-permute-start(bf16[32,72,128]{2,1,0:T(8,128)(2,1)S(1)} %all-to-all-done.arrived.after), channel_id=1, source_target_pairs={{0,4},{4,0},{1,5},{5,1},{2,6},{6,2},{3,7},{7,3},{8,12},{12,8},{9,1... | collective-permute-start | bytes 1769480 | tf_op jit(solution)/shard_map/ppermute | solution.py:332
  55.4 19.0 %collective-permute-start.5 = (s16[264,640]{1,0:T(8,128)(2,1)}, s16[264,640]{1,0:T(8,128)(2,1)S(1)}, u32[]{:S(2)}, u32[]{:S(2)}) collective-permute-start(s16[264,640]{1,0:T(8,128)(2,1)} %get-tuple-element.31.after), channel_id=1, source_target_pairs={{0,8},{8,0},{16,24},{24,16},{1,9},{9,1},{17,25},{25,17},{2,10},{10... | collective-permute-start | bytes 1013768 | tf_op jit(solution)/shard_map/ppermute | solution.py:352
  56.0 18.4 %collective-permute-start.6 = (s16[264,640]{1,0:T(8,128)(2,1)S(1)}, s16[264,640]{1,0:T(8,128)(2,1)S(1)}, u32[]{:S(2)}, u32[]{:S(2)}) collective-permute-start(s16[264,640]{1,0:T(8,128)(2,1)S(1)} %get-tuple-element.33), channel_id=1, source_target_pairs={{0,24},{8,16},{16,8},{24,0},{1,25},{9,17},{17,9},{25,1},{2,26},{10... | collective-permute-start | bytes 1013768 | tf_op jit(solution)/shard_map/ppermute | solution.py:353
  64.8 11.0 %collective-permute-start.16 = (s16[264,640]{1,0:T(8,128)(2,1)}, s16[264,640]{1,0:T(8,128)(2,1)S(1)}, u32[]{:S(2)}, u32[]{:S(2)}) collective-permute-start(s16[264,640]{1,0:T(8,128)(2,1)} %get-tuple-element.32.after), channel_id=1, source_target_pairs={{0,8},{8,0},{16,24},{24,16},{1,9},{9,1},{17,25},{25,17},{2,10},{10... | collective-permute-start | bytes 1013768 | tf_op jit(solution)/shard_map/ppermute | solution.py:352
  65.0 10.8 %collective-permute-start.17 = (s16[264,640]{1,0:T(8,128)(2,1)S(1)}, s16[264,640]{1,0:T(8,128)(2,1)S(1)}, u32[]{:S(2)}, u32[]{:S(2)}) collective-permute-start(s16[264,640]{1,0:T(8,128)(2,1)S(1)} %get-tuple-element.45), channel_id=1, source_target_pairs={{0,24},{8,16},{16,8},{24,0},{1,25},{9,17},{17,9},{25,1},{2,26},{10... | collective-permute-start | bytes 1013768 | tf_op jit(solution)/shard_map/ppermute | solution.py:353
  82.0 6.1 %collective-permute-start.18 = (s16[136,640]{1,0:T(8,128)(2,1)S(1)}, s16[136,640]{1,0:T(8,128)(2,1)S(1)}, u32[]{:S(2)}, u32[]{:S(2)}) collective-permute-start(s16[136,640]{1,0:T(8,128)(2,1)S(1)} %get-tuple-element.47), channel_id=1, source_target_pairs={{0,24},{8,16},{16,8},{24,0},{1,25},{9,17},{17,9},{25,1},{2,26},{10... | collective-permute-start | bytes 522248 | tf_op jit(solution)/shard_map/ppermute | solution.py:352
  84.0 11.2 %collective-permute-start.7 = (s16[136,640]{1,0:T(8,128)(2,1)}, s16[136,640]{1,0:T(8,128)(2,1)S(1)}, u32[]{:S(2)}, u32[]{:S(2)}) collective-permute-start(s16[136,640]{1,0:T(8,128)(2,1)} %get-tuple-element.35.after), channel_id=1, source_target_pairs={{0,24},{8,16},{16,8},{24,0},{1,25},{9,17},{17,9},{25,1},{2,26},{10... | collective-permute-start | bytes 522248 | tf_op jit(solution)/shard_map/ppermute | solution.py:352
  84.8 12.0 %collective-permute-start.8 = (s16[136,640]{1,0:T(8,128)(2,1)S(1)}, s16[136,640]{1,0:T(8,128)(2,1)S(1)}, u32[]{:S(2)}, u32[]{:S(2)}) collective-permute-start(s16[136,640]{1,0:T(8,128)(2,1)S(1)} %get-tuple-element.36), channel_id=1, source_target_pairs={{0,8},{8,0},{16,24},{24,16},{1,9},{9,1},{17,25},{25,17},{2,10},{10... | collective-permute-start | bytes 522248 | tf_op jit(solution)/shard_map/ppermute | solution.py:353
  89.6 12.2 %collective-permute-start.20 = (s16[32,768]{1,0:T(8,128)(2,1)S(1)}, s16[32,768]{1,0:T(8,128)(2,1)S(1)}, u32[]{:S(2)}, u32[]{:S(2)}) collective-permute-start(s16[32,768]{1,0:T(8,128)(2,1)S(1)} %get-tuple-element.49), channel_id=1, source_target_pairs={{0,4},{4,0},{32,36},{36,32},{64,68},{68,64},{96,100},{100,96},{128... | collective-permute-start | bytes 147464 | tf_op jit(solution)/shard_map/ppermute | solution.py:402
  93.8 8.6 %collective-permute-start.21 = (s16[32,768]{1,0:T(8,128)(2,1)S(1)}, s16[32,768]{1,0:T(8,128)(2,1)S(1)}, u32[]{:S(2)}, u32[]{:S(2)}) collective-permute-start(s16[32,768]{1,0:T(8,128)(2,1)S(1)} %get-tuple-element.50), channel_id=1, source_target_pairs={{0,36},{4,32},{32,68},{36,64},{64,100},{68,96},{96,132},{100,128},... | collective-permute-start | bytes 147464 | tf_op jit(solution)/shard_map/ppermute | solution.py:402
  94.1 11.2 %collective-permute-start.22 = (s16[32,768]{1,0:T(8,128)(2,1)S(1)}, s16[32,768]{1,0:T(8,128)(2,1)S(1)}, u32[]{:S(2)}, u32[]{:S(2)}) collective-permute-start(s16[32,768]{1,0:T(8,128)(2,1)S(1)} %get-tuple-element.51), channel_id=1, source_target_pairs={{0,68},{4,64},{32,100},{36,96},{64,132},{68,128},{96,164},{100,160... | collective-permute-start | bytes 147464 | tf_op jit(solution)/shard_map/ppermute | solution.py:402
  95.1 10.9 %collective-permute-start.23 = (s16[32,768]{1,0:T(8,128)(2,1)S(1)}, s16[32,768]{1,0:T(8,128)(2,1)S(1)}, u32[]{:S(2)}, u32[]{:S(2)}) collective-permute-start(s16[32,768]{1,0:T(8,128)(2,1)S(1)} %get-tuple-element.52), channel_id=1, source_target_pairs={{0,100},{4,96},{32,132},{36,128},{64,164},{68,160},{96,196},{100,1... | collective-permute-start | bytes 147464 | tf_op jit(solution)/shard_map/ppermute | solution.py:402
  96.8 10.6 %collective-permute-start.24 = (s16[32,768]{1,0:T(8,128)(2,1)S(1)}, s16[32,768]{1,0:T(8,128)(2,1)S(1)}, u32[]{:S(2)}, u32[]{:S(2)}) collective-permute-start(s16[32,768]{1,0:T(8,128)(2,1)S(1)} %get-tuple-element.53), channel_id=1, source_target_pairs={{0,132},{4,128},{32,164},{36,160},{64,196},{68,192},{96,228},{100,... | collective-permute-start | bytes 147464 | tf_op jit(solution)/shard_map/ppermute | solution.py:402
  101.7 9.2 %collective-permute-start.25 = (s16[32,768]{1,0:T(8,128)(2,1)S(1)}, s16[32,768]{1,0:T(8,128)(2,1)S(1)}, u32[]{:S(2)}, u32[]{:S(2)}) collective-permute-start(s16[32,768]{1,0:T(8,128)(2,1)S(1)} %get-tuple-element.54), channel_id=1, source_target_pairs={{0,164},{4,160},{32,196},{36,192},{64,228},{68,224},{96,4},{100,0}... | collective-permute-start | bytes 147464 | tf_op jit(solution)/shard_map/ppermute | solution.py:402
  102.4 9.7 %collective-permute-start.26 = (s16[32,768]{1,0:T(8,128)(2,1)S(1)}, s16[32,768]{1,0:T(8,128)(2,1)S(1)}, u32[]{:S(2)}, u32[]{:S(2)}) collective-permute-start(s16[32,768]{1,0:T(8,128)(2,1)S(1)} %get-tuple-element.55), channel_id=1, source_target_pairs={{0,196},{4,192},{32,228},{36,224},{64,4},{68,0},{96,36},{100,32},{... | collective-permute-start | bytes 147464 | tf_op jit(solution)/shard_map/ppermute | solution.py:402
  105.3 10.0 %collective-permute-start.27 = (s16[32,768]{1,0:T(8,128)(2,1)S(1)}, s16[32,768]{1,0:T(8,128)(2,1)S(1)}, u32[]{:S(2)}, u32[]{:S(2)}) collective-permute-start(s16[32,768]{1,0:T(8,128)(2,1)S(1)} %get-tuple-element.56), channel_id=1, source_target_pairs={{0,228},{4,224},{32,4},{36,0},{64,36},{68,32},{96,68},{100,64},{12... | collective-permute-start | bytes 147464 | tf_op jit(solution)/shard_map/ppermute | solution.py:402
  106.0 12.7 %collective-permute-start.10 = (s16[32,768]{1,0:T(8,128)(2,1)S(1)}, s16[32,768]{1,0:T(8,128)(2,1)S(1)}, u32[]{:S(2)}, u32[]{:S(2)}) collective-permute-start(s16[32,768]{1,0:T(8,128)(2,1)S(1)} %get-tuple-element.39), channel_id=1, source_target_pairs={{0,64},{32,96},{64,128},{96,160},{128,192},{160,224},{192,0},{224,... | collective-permute-start | bytes 147464 | tf_op jit(solution)/shard_map/ppermute | solution.py:395
  107.4 11.8 %collective-permute-start.11 = (s16[32,768]{1,0:T(8,128)(2,1)S(1)}, s16[32,768]{1,0:T(8,128)(2,1)S(1)}, u32[]{:S(2)}, u32[]{:S(2)}) collective-permute-start(s16[32,768]{1,0:T(8,128)(2,1)S(1)} %get-tuple-element.40), channel_id=1, source_target_pairs={{0,96},{32,128},{64,160},{96,192},{128,224},{160,0},{192,32},{224,... | collective-permute-start | bytes 147464 | tf_op jit(solution)/shard_map/ppermute | solution.py:395
  111.0 9.2 %collective-permute-start.12 = (s16[32,768]{1,0:T(8,128)(2,1)S(1)}, s16[32,768]{1,0:T(8,128)(2,1)S(1)}, u32[]{:S(2)}, u32[]{:S(2)}) collective-permute-start(s16[32,768]{1,0:T(8,128)(2,1)S(1)} %get-tuple-element.41), channel_id=1, source_target_pairs={{0,128},{32,160},{64,192},{96,224},{128,0},{160,32},{192,64},{224,... | collective-permute-start | bytes 147464 | tf_op jit(solution)/shard_map/ppermute | solution.py:395
  112.1 8.6 %collective-permute-start.13 = (s16[32,768]{1,0:T(8,128)(2,1)S(1)}, s16[32,768]{1,0:T(8,128)(2,1)S(1)}, u32[]{:S(2)}, u32[]{:S(2)}) collective-permute-start(s16[32,768]{1,0:T(8,128)(2,1)S(1)} %get-tuple-element.42), channel_id=1, source_target_pairs={{0,160},{32,192},{64,224},{96,0},{128,32},{160,64},{192,96},{224,1... | collective-permute-start | bytes 147464 | tf_op jit(solution)/shard_map/ppermute | solution.py:395
  115.3 9.0 %collective-permute-start.14 = (s16[32,768]{1,0:T(8,128)(2,1)S(1)}, s16[32,768]{1,0:T(8,128)(2,1)S(1)}, u32[]{:S(2)}, u32[]{:S(2)}) collective-permute-start(s16[32,768]{1,0:T(8,128)(2,1)S(1)} %get-tuple-element.43), channel_id=1, source_target_pairs={{0,192},{32,224},{64,0},{96,32},{128,64},{160,96},{192,128},{224,1... | collective-permute-start | bytes 147464 | tf_op jit(solution)/shard_map/ppermute | solution.py:395
  118.7 6.2 %collective-permute-start.15 = (s16[32,768]{1,0:T(8,128)(2,1)S(1)}, s16[32,768]{1,0:T(8,128)(2,1)S(1)}, u32[]{:S(2)}, u32[]{:S(2)}) collective-permute-start(s16[32,768]{1,0:T(8,128)(2,1)S(1)} %get-tuple-element.44), channel_id=1, source_target_pairs={{0,224},{32,0},{64,32},{96,64},{128,96},{160,128},{192,160},{224,1... | collective-permute-start | bytes 147464 | tf_op jit(solution)/shard_map/ppermute | solution.py:395
  (12 other events, 94.6 us)

commit v6 on v4

--- a/solution.py
+++ b/solution.py
@@ -31,8 +31,8 @@
 HBM = pl.BlockSpec(memory_space=pltpu.HBM)
 ANY = pl.BlockSpec(memory_space=pl.ANY)
 PIECES = 4
-GRANT = 48
-WEIGHT_GRANT = 50
+GRANT = 18
+WEIGHT_GRANT = 8
 
 
 def ring(n, k):
@@ -55,8 +55,18 @@
     return jnp.transpose(jnp.broadcast_to(row, (128, 128)))
 
 
-def wrap_kernel(counts, coeffs, ids, out_ref):
+def wrap_kernel(counts_in, coeffs_in, ids_in, out_ref, counts, coeffs, ids, sems):
     n = OWN * ACTIVE
+    copies = [
+        pltpu.make_async_copy(ref, to, sems.at[k])
+        for k, (ref, to) in enumerate(
+            ((counts_in, counts), (coeffs_in, coeffs), (ids_in, ids))
+        )
+    ]
+    for copy in copies:
+        copy.start()
+    for copy in copies:
+        copy.wait()
     slot = lax.broadcasted_iota(jnp.int32, (ACTIVE, BLOCK), 0)
     for i in range(OWN):
         live = slot < counts[i]
@@ -194,12 +204,15 @@
         copy.wait()
 
 
-def build(info, tok, coef, x_buf):
+def build(rows_of, tok, coef, x_buf):
     t = lax.broadcasted_iota(jnp.int32, (TOK, 128), 0).astype(jnp.float32) + 1.0
 
     def source(i, carry):
         h, j, z = i // 8, (i // 4) % 2, i % 4
-        n = (h * 4 + z) * NY + info[1 + h * 2 + j]
+        first, second = jnp.where(h == 0, rows_of[0], rows_of[2]), jnp.where(
+            h == 0, rows_of[1], rows_of[3]
+        )
+        n = (h * 4 + z) * NY + jnp.where(j == 0, first, second)
         base = pl.multiple_of(i * TOK, TOK)
         for b in range(BLOCKS_CHIP):
             row = jnp.zeros((TOK, 128), jnp.float32)
@@ -213,37 +226,33 @@
     lax.fori_loop(0, 4 * PART // TOK, source, 0)
 
 
-def multiply(info, arrived, weights, tok, coef, x_buf, w_buf, sems, acc):
-    deep = w_buf.shape[0] // PIECES
-    copies = []
-    for g in range(PIECES):
-        here = slice(g * deep, (g + 1) * deep)
-        copies.append(pltpu.make_async_copy(weights.at[here], w_buf.at[here], sems.at[g]))
-    for copy in copies:
-        copy.start()
-    prepare(info, arrived, tok, coef)
-    build(info, tok, coef, x_buf)
-    for g, copy in enumerate(copies):
-        here = slice(g * deep, (g + 1) * deep)
-        copy.wait()
-        term = jnp.dot(x_buf[:, here], w_buf[here, :], preferred_element_type=jnp.float32)
-        acc[...] = term if g == 0 else acc[...] + term
-
-
-def send_kernel(info, arrived, weights, after, out0, out1, acc, *scratch):
-    multiply(info, arrived, weights, *scratch, acc)
+def multiply(send, core, y_ref, arrived, weights, tok, coef, x_buf, acc):
+    y = y_ref[0]
+    a, b = y + 1 - 2 * lax.rem(y, 2), NY - 1 - y
+    opposite = NY - 1 - a
+    prepare(core, arrived, tok, coef)
+    build((a, opposite, b, opposite) if send else (y, b, y, a), tok, coef, x_buf)
+    for h in range(2):
+        here = slice(h * 2 * PART, (h + 1) * 2 * PART)
+        acc[here, :] = jnp.dot(
+            x_buf[here, :], weights[...], preferred_element_type=jnp.float32
+        )
+
+
+def send_kernel(core, y, arrived, weights, after, out0, out1, acc, *scratch):
+    multiply(True, core, y, arrived, weights, *scratch, acc)
     for h, out in enumerate((out0, out1)):
         write_message(out, acc[h * 2 * PART : (h + 1) * 2 * PART, :])
 
 
-def keep_kernel(info, arrived, weights, after, out_ref, *scratch):
-    multiply(info, arrived, weights, *scratch, out_ref)
+def keep_kernel(core, y, arrived, weights, after, out_ref, *scratch):
+    multiply(False, core, y, arrived, weights, *scratch, out_ref)
 
 
 def keep_middle_kernel(
-    info, arrived, weights, after, in0, in1, keep_ref, out0, out1, acc, *scratch
+    core, y, arrived, weights, after, in0, in1, keep_ref, out0, out1, acc, *scratch
 ):
-    multiply(info, arrived, weights, *scratch, acc)
+    multiply(False, core, y, arrived, weights, *scratch, acc)
     for h, (ref, out) in enumerate(((in0, out0), (in1, out1))):
         low, high = 2 * h * PART, (2 * h + 1) * PART
         keep_ref[h * PART : (h + 1) * PART, :] = acc[low:high, :] + read_message(ref, 0)
@@ -298,7 +307,16 @@
 
     shape = jax.ShapeDtypeStruct
     packed = call(
-        wrap_kernel, shape((OWN * (ACTIVE + 1), BLOCK), jnp.bfloat16), [SMEM, VMEM, VMEM], 10
+        wrap_kernel,
+        shape((OWN * (ACTIVE + 1), BLOCK), jnp.bfloat16),
+        [HBM, HBM, HBM],
+        10,
+        scratch=[
+            pltpu.SMEM((OWN,), jnp.int32),
+            pltpu.VMEM((OWN, ACTIVE, BLOCK), jnp.bfloat16),
+            pltpu.VMEM((OWN, ACTIVE), jnp.int32),
+            pltpu.SemaphoreType.DMA((3,)),
+        ],
     )(counts, coefficients, block_ids)
     parts = [packed] + [lax.ppermute(packed, "x", ring(NX, k)) for k in range(1, NX)]
     outgoing = call(
@@ -315,10 +333,7 @@
     )(core.reshape(1), decoder, w_other, outgoing)
     other = lax.ppermute(own, "c", ring(NC, 1))
     pair_a, pair_b = [(i, i ^ 1) for i in range(NY)], [(i, NY - 1 - i) for i in range(NY)]
-    a, b = y ^ 1, NY - 1 - y
-    opposite = NY - 1 - a
-    sent_to = jnp.stack([core, a, opposite, b, opposite])
-    kept_for = jnp.stack([core, y, b, y, a])
+    place = (core.reshape(1), y.reshape(1))
     message = shape((2 * PART + 8, width), jnp.int16)
     small = shape((PART + 8, width), jnp.int16)
 
@@ -329,10 +344,8 @@
         pltpu.VMEM((CHIPS, SLOTS, BLOCK), jnp.float32),
         pltpu.VMEM((CHIPS, SLOTS, BLOCK), jnp.float32),
         pltpu.VMEM((4 * PART, NC * depth), jnp.bfloat16),
-        pltpu.VMEM((NC * depth, width), jnp.bfloat16),
-        pltpu.SemaphoreType.DMA((PIECES,)),
     ]
-    given = [SMEM, VMEM, HBM, ANY]
+    given = [SMEM, SMEM, VMEM, VMEM, ANY]
 
     def cross(m0, m1, pair0, pair1):
         m0 = lax.ppermute(m0, "y", pair0)
@@ -341,11 +354,11 @@
 
     m0, m1 = call(
         send_kernel, [message, message], given, GRANT, scratch=[total] + scratch, **product
-    )(sent_to, own, weights, own)
+    )(*place, own, weights, own)
     crossing0 = cross(m0, m1, pair_a, pair_b)
     m0, m1 = call(
         send_kernel, [message, message], given, GRANT, scratch=[total] + scratch, **product
-    )(sent_to, other, weights, m0)
+    )(*place, other, weights, m0)
     crossing1 = cross(m0, m1, pair_a, pair_b)
     (sums,) = call(
         keep_kernel,
@@ -354,7 +367,7 @@
         GRANT,
         scratch=scratch,
         **product,
-    )(kept_for, own, weights, m0)
+    )(*place, own, weights, m0)
     kept0, m0, m1 = call(middle_kernel, [kept, small, small], [VMEM] * 3, 10)(sums, *crossing0)
     arrived0 = cross(m0, m1, pair_b, pair_a)
     kept1, m0, m1 = call(
@@ -364,7 +377,7 @@
         GRANT,
         scratch=[total] + scratch,
         **product,
-    )(kept_for, other, weights, m0, *crossing1)
+    )(*place, other, weights, m0, *crossing1)
     arrived1 = cross(m0, m1, pair_b, pair_a)
     out = call(
         last_kernel, shape((NZ * NC, TOK, width + 128), jnp.int16), [SMEM] + [VMEM] * 6, 10

time: 126 us -> 119 us (0.944)
  Pallas kernels: 41.6 us -> 29.7 us
  local copies, waits for them, and re-layouts: 2.27 us -> 4.59 us
    pallas_call x2, Pallas kernels: 17.3 us -> 11.6 us  [run(): call(send_kernel, [message, message], given, GRANT, scratch=[total] + scr...]
    pallas_call x1, Pallas kernels: 4.86 us -> 1.97 us  [run(): call(weights_kernel, shape((NC * depth, width), jnp.bfloat16), [SMEM, HBM...]
    unnamed x8 -> x10, local copies, waits for them, and re-layouts: 2.1 us -> 4.59 us
    ppermute x4, waiting for transfers between devices: 3.13 us -> 5.58 us  [cross(): m1 = lax.ppermute(m1, 'y', pair1)]
    pallas_call x1, Pallas kernels: 7.86 us -> 5.55 us  [run(): call(keep_kernel, [shape((4 * PART, width), jnp.float32)], given, GRANT,...]
    ppermute x4, waiting for transfers between devices: 3.7 us -> 2.2 us  [cross(): m0 = lax.ppermute(m0, 'y', pair0)]
  transfers between devices with their start and end apart: 14 -> 14, of which waited for: 6 -> 8; matrix products, arithmetic and copies ran while one was open for 0% -> 0% of each run, Pallas kernels for 32% -> 24%
where the time goes in v6:
time: 119 us; the launch traced here: 118 us
  Pallas kernels  29.7 us (25%)
  starting transfers between devices  29.6 us (25%)
  blocking collectives  27.8 us (23%)
  waiting for transfers between devices  26.5 us (22%)
  local copies, waits for them, and re-layouts  4.59 us (4%)
    all_to_all x1, blocking collectives, run(): lax.all_to_all(out, ('z', 'c'), 0, 0, tiled=True)  27.8 us
    all_to_all x1, waiting for transfers between devices, run(): own = lax.all_to_all(outgoing, ('z', 'y'), 0, 0, tiled=True)  16.6 us
    pallas_call x2, Pallas kernels, run(): call(send_kernel, [message, message], given, GRANT, scratch=[total] + scr...  11.6 us
    all_to_all x1, starting transfers between devices, run(): own = lax.all_to_all(outgoing, ('z', 'y'), 0, 0, tiled=True)  10.8 us
    pallas_call x1, Pallas kernels, run(): call(keep_middle_kernel, [kept, small, small], given + [VMEM] * 2, GRANT,...  5.78 us
    ppermute x4, waiting for transfers between devices, cross(): m1 = lax.ppermute(m1, 'y', pair1)  5.58 us
    pallas_call x1, Pallas kernels, run(): call(keep_kernel, [shape((4 * PART, width), jnp.float32)], given, GRANT,...  5.55 us
    ppermute x4, starting transfers between devices, cross(): m0 = lax.ppermute(m0, 'y', pair0)  4.72 us
  transfers between devices with their start and end apart: 14, of which 8 were waited for; matrix products, arithmetic and copies ran while one was open for 0% of the time, Pallas kernels for 24%

profile of v6, /device:TPU:1, one launch (start us, length us, event | category | flops | bytes accessed | tf_op | source)
XLA Modules:
  0.0 118.2 jit_solution(17078511548489205136)
XLA Ops:
  0.0 3.2 %collective-permute-start.3 = (bf16[1,2048,1280]{2,1,0:T(8,128)(2,1)}, bf16[1,2048,1280]{2,1,0:T(8,128)(2,1)}, u32[]{:S(2)}, u32[]{:S(2)}) collective-permute-start(bf16[1,2048,1280]{2,1,0:T(8,128)(2,1)} %w_own.1), channel_id=1, source_target_pairs={{0,4},{4,0},{1,5},{5,1},{2,6},{6,2},{3,7},{7,3},{8,12},{12,8},{9,1... | collective-permute-start | bytes 15728648 | tf_op jit(solution)/shard_map/ppermute | solution.py:306
  6.1 1.9 %collective-permute-start.1 = (bf16[136,128]{1,0:T(8,128)(2,1)S(1)}, bf16[136,128]{1,0:T(8,128)(2,1)S(1)}, u32[]{:S(2)}, u32[]{:S(2)}) collective-permute-start(bf16[136,128]{1,0:T(8,128)(2,1)S(1)} %shard_map.55.part0), channel_id=1, source_target_pairs={{0,2},{1,3},{2,0},{3,1},{4,6},{5,7},{6,4},{7,5},{8,10},{9,11},{10,... | collective-permute-start | bytes 104456 | tf_op jit(solution)/shard_map/ppermute | solution.py:321
  8.1 1.2 collective-permute-start.2
  9.2 0.9 collective-permute-done.part1
  11.3 1.8 %shard_map.56.after = bf16[32,72,128]{2,1,0:T(8,128)(2,1)} custom-call(s32[1]{0:T(128)} %bitcast.2.info, bf16[136,128]{1,0:T(8,128)(2,1)S(1)} %shard_map.55.part0, bf16[136,128]{1,0:T(8,128)(2,1)S(1)} %collective-permute-done.part1, bf16[136,128]{1,0:T(8,128)(2,1)S(1)} %collective-permute-done.1.part2, bf16[136,128]{1,0:T(8,128)(2,1)S(1)} %collective-permute-done.2.part3), custom_call_target="tpu_custom_call" | custom-call | bytes 2097152 | tf_op jit(solution)/shard_map/pallas_call | solution.py:322
  13.1 10.8 %all-to-all-start = ((bf16[32,72,128]{2,1,0:T(8,128)(2,1)}), bf16[32,72,128]{2,1,0:T(8,128)(2,1)S(1)}, u32[]{:S(2)}, u32[]{:S(2)}) async-start(bf16[32,72,128]{2,1,0:T(8,128)(2,1)} %shard_map.56.after), calls=%async_computation | async-start | bytes 1179648 | tf_op jit(solution)/shard_map/all_to_all | solution.py:325
  23.9 16.6 %all-to-all-done.arrived.after = bf16[32,72,128]{2,1,0:T(8,128)(2,1)S(1)} async-done(((bf16[32,72,128]{2,1,0:T(8,128)(2,1)}), bf16[32,72,128]{2,1,0:T(8,128)(2,1)S(1)}, u32[]{:S(2)}, u32[]{:S(2)}) %all-to-all-start) | async-done | bytes 589856 | tf_op jit(solution)/shard_map/all_to_all | solution.py:325
  40.5 3.5 %collective-permute-start.4 = (bf16[32,72,128]{2,1,0:T(8,128)(2,1)S(1)}, bf16[32,72,128]{2,1,0:T(8,128)(2,1)S(1)}, u32[]{:S(2)}, u32[]{:S(2)}) collective-permute-start(bf16[32,72,128]{2,1,0:T(8,128)(2,1)S(1)} %all-to-all-done.arrived.after), channel_id=1, source_target_pairs={{0,4},{4,0},{1,5},{5,1},{2,6},{6,2},{3,7},{7,3},{8,12},{12,8},{9,1... | collective-permute-start | bytes 1769480 | tf_op jit(solution)/shard_map/ppermute | solution.py:334
  44.0 2.5 %copy-done.4 = bf16[1,2048,1280]{2,1,0:T(8,128)(2,1)S(1)} copy-done((bf16[1,2048,1280]{2,1,0:T(8,128)(2,1)S(1)}, bf16[1,2048,1280]{2,1,0:T(8,128)(2,1)}, u32[]{:S(2)}) %copy-start.4) | copy-done | bytes 5242904
  46.5 2.0 %shard_map.57.weights = bf16[4096,640]{1,0:T(8,128)(2,1)S(1)} custom-call(s32[1]{0:T(128)} %bitcast.core_ref.core.info, bf16[1,2048,1280]{2,1,0:T(8,128)(2,1)S(1)} %copy-done.4, bf16[1,2048,1280]{2,1,0:T(8,128)(2,1)} %collective-permute-done.3.w_other, bf16[32,72,128]{2,1,0:T(8,128)(2,1)} %shard_map.56.after), custom_call_target="tpu_custom_call" | custom-call | flops 10000000000 | bytes 2097152 | tf_op jit(solution)/shard_map/pallas_call | solution.py:326
  48.5 5.8 %shard_map.58 = (s16[264,640]{1,0:T(8,128)(2,1)S(1)}, s16[264,640]{1,0:T(8,128)(2,1)S(1)}) custom-call(s32[1]{0:T(128)} %bitcast.core_ref.core.info, s32[1]{0:T(128)} %bitcast.1.y, bf16[32,72,128]{2,1,0:T(8,128)(2,1)S(1)} %all-to-all-done.arrived.after, bf16[4096,640]{1,0:T(8,128)(2,1)S(1)} %shard_map.57.weights, ...), custom_call_target="tpu_custom_call" | custom-call | flops 2684354560 | bytes 2097152 | tf_op jit(solution)/shard_map/pallas_call | solution.py:355
  55.0 1.8 %collective-permute-start.6 = (s16[264,640]{1,0:T(8,128)(2,1)S(1)}, s16[264,640]{1,0:T(8,128)(2,1)S(1)}, u32[]{:S(2)}, u32[]{:S(2)}) collective-permute-start(s16[264,640]{1,0:T(8,128)(2,1)S(1)} %get-tuple-element.17), channel_id=1, source_target_pairs={{0,24},{8,16},{16,8},{24,0},{1,25},{9,17},{17,9},{25,1},{2,26},{10... | collective-permute-start | bytes 1013768 | tf_op jit(solution)/shard_map/ppermute | solution.py:352
  56.8 5.8 %shard_map.59 = (s16[264,640]{1,0:T(8,128)(2,1)S(1)}, s16[264,640]{1,0:T(8,128)(2,1)S(1)}) custom-call(s32[1]{0:T(128)} %bitcast.core_ref.core.info, s32[1]{0:T(128)} %bitcast.1.y, bf16[32,72,128]{2,1,0:T(8,128)(2,1)S(1)} %collective-permute-done.4.arrived, bf16[4096,640]{1,0:T(8,128)(2,1)S(1)} %shard_map.57.weights, s16[264,640]{1,0:T(8,128)(2,1)S(1)} %get-tuple-element.15.after), custom_call_target="tpu_custom_call" | custom-call | flops 2684354560 | bytes 2097152 | tf_op jit(solution)/shard_map/pallas_call | solution.py:359
  62.5 1.0 collective-permute-start.10
  63.5 5.5 %shard_map.60.kept = f32[512,640]{1,0:T(8,128)S(1)} custom-call(s32[1]{0:T(128)} %bitcast.core_ref.core.info, s32[1]{0:T(128)} %bitcast.1.y, bf16[32,72,128]{2,1,0:T(8,128)(2,1)S(1)} %all-to-all-done.arrived.after, bf16[4096,640]{1,0:T(8,128)(2,1)S(1)} %shard_map.57.weights, s16[264,640]{1,0:T(8,128)(2,1)S(1)} %get-tuple-element.16.after), custom_call_target="tpu_custom_call" | custom-call | flops 2684354560 | bytes 2097152 | tf_op jit(solution)/shard_map/pallas_call | solution.py:363
  69.8 2.1 %collective-permute-start.7 = (s16[136,640]{1,0:T(8,128)(2,1)S(1)}, s16[136,640]{1,0:T(8,128)(2,1)S(1)}, u32[]{:S(2)}, u32[]{:S(2)}) collective-permute-start(s16[136,640]{1,0:T(8,128)(2,1)S(1)} %get-tuple-element.19.after), channel_id=1, source_target_pairs={{0,24},{8,16},{16,8},{24,0},{1,25},{9,17},{17,9},{25,1},{2,26},{10... | collective-permute-start | bytes 522248 | tf_op jit(solution)/shard_map/ppermute | solution.py:351
  71.9 0.9 collective-permute-done.10.in1
  72.8 5.8 %shard_map.62 = (f32[256,640]{1,0:T(8,128)S(1)}, s16[136,640]{1,0:T(8,128)(2,1)S(1)}, s16[136,640]{1,0:T(8,128)(2,1)S(1)}) custom-call(s32[1]{0:T(128)} %bitcast.core_ref.core.info, s32[1]{0:T(128)} %bitcast.1.y, bf16[32,72,128]{2,1,0:T(8,128)(2,1)S(1)} %collective-permute-done.4.arrived, bf16[4096,640]{1,0:T(8,128)(2,1)S(1)} %shard_map.57.weights, ...), custom_call_target="tpu_custom_call" | custom-call | flops 2684354560 | bytes 2097152 | tf_op jit(solution)/shard_map/pallas_call | solution.py:373
  78.5 1.9 %collective-permute-start.11 = (s16[136,640]{1,0:T(8,128)(2,1)S(1)}, s16[136,640]{1,0:T(8,128)(2,1)S(1)}, u32[]{:S(2)}, u32[]{:S(2)}) collective-permute-start(s16[136,640]{1,0:T(8,128)(2,1)S(1)} %get-tuple-element.23), channel_id=1, source_target_pairs={{0,24},{8,16},{16,8},{24,0},{1,25},{9,17},{17,9},{25,1},{2,26},{10... | collective-permute-start | bytes 522248 | tf_op jit(solution)/shard_map/ppermute | solution.py:351
  80.5 1.5 %collective-permute-start.8 = (s16[136,640]{1,0:T(8,128)(2,1)S(1)}, s16[136,640]{1,0:T(8,128)(2,1)S(1)}, u32[]{:S(2)}, u32[]{:S(2)}) collective-permute-start(s16[136,640]{1,0:T(8,128)(2,1)S(1)} %get-tuple-element.20), channel_id=1, source_target_pairs={{0,8},{8,0},{16,24},{24,16},{1,9},{9,1},{17,25},{25,17},{2,10},{10... | collective-permute-start | bytes 522248 | tf_op jit(solution)/shard_map/ppermute | solution.py:352
  81.9 2.2 %collective-permute-done.11.refs_4_ = s16[136,640]{1,0:T(8,128)(2,1)S(1)} collective-permute-done((s16[136,640]{1,0:T(8,128)(2,1)S(1)}, s16[136,640]{1,0:T(8,128)(2,1)S(1)}, u32[]{:S(2)}, u32[]{:S(2)}) %collective-permute-start.11) | collective-permute-done | bytes 174112 | tf_op jit(solution)/shard_map/ppermute | solution.py:351
  84.1 1.0 collective-permute-done.12.refs_5_
  85.1 3.7 %collective-permute-done.8.refs_2_ = s16[136,640]{1,0:T(8,128)(2,1)S(1)} collective-permute-done((s16[136,640]{1,0:T(8,128)(2,1)S(1)}, s16[136,640]{1,0:T(8,128)(2,1)S(1)}, u32[]{:S(2)}, u32[]{:S(2)}) %collective-permute-start.8) | collective-permute-done | bytes 174112 | tf_op jit(solution)/shard_map/ppermute | solution.py:352
  89.6 27.8 %all_to_all.10.ref = s16[16,32,768]{2,1,0:T(8,128)(2,1)S(1)} all-to-all(s16[16,32,768]{2,1,0:T(8,128)(2,1)S(1)} %shard_map.63), channel_id=1, replica_groups=mesh['z'=8,'y'=4,'c'=2,'x'=4] {'z','c'}, dimensions={0} | all-to-all | bytes 1572864 | tf_op jit(solution)/shard_map/all_to_all | solution.py:387
  (25 shorter events, 7.2 us)
Async XLA Ops:
  0.0 44.0 %collective-permute-start.3 = (bf16[1,2048,1280]{2,1,0:T(8,128)(2,1)}, bf16[1,2048,1280]{2,1,0:T(8,128)(2,1)}, u32[]{:S(2)}, u32[]{:S(2)}) collective-permute-start(bf16[1,2048,1280]{2,1,0:T(8,128)(2,1)} %w_own.1), channel_id=1, source_target_pairs={{0,4},{4,0},{1,5},{5,1},{2,6},{6,2},{3,7},{7,3},{8,12},{12,8},{9,1... | collective-permute-start | bytes 15728648 | tf_op jit(solution)/shard_map/ppermute | solution.py:306
  3.2 0.8 copy-start
  4.0 0.7 copy-start.2
  4.6 0.7 copy-start.3
  6.0 4.1 %collective-permute-start = (bf16[136,128]{1,0:T(8,128)(2,1)S(1)}, bf16[136,128]{1,0:T(8,128)(2,1)S(1)}, u32[]{:S(2)}, u32[]{:S(2)}) collective-permute-start(bf16[136,128]{1,0:T(8,128)(2,1)S(1)} %shard_map.55.part0), channel_id=1, source_target_pairs={{0,1},{1,2},{2,3},{3,0},{4,5},{5,6},{6,7},{7,4},{8,9},{9,10},{10,1... | collective-permute-start | bytes 104456 | tf_op jit(solution)/shard_map/ppermute | solution.py:321
  6.1 4.4 %collective-permute-start.1 = (bf16[136,128]{1,0:T(8,128)(2,1)S(1)}, bf16[136,128]{1,0:T(8,128)(2,1)S(1)}, u32[]{:S(2)}, u32[]{:S(2)}) collective-permute-start(bf16[136,128]{1,0:T(8,128)(2,1)S(1)} %shard_map.55.part0), channel_id=1, source_target_pairs={{0,2},{1,3},{2,0},{3,1},{4,6},{5,7},{6,4},{7,5},{8,10},{9,11},{10,... | collective-permute-start | bytes 104456 | tf_op jit(solution)/shard_map/ppermute | solution.py:321
  8.1 3.3 %collective-permute-start.2 = (bf16[136,128]{1,0:T(8,128)(2,1)S(1)}, bf16[136,128]{1,0:T(8,128)(2,1)S(1)}, u32[]{:S(2)}, u32[]{:S(2)}) collective-permute-start(bf16[136,128]{1,0:T(8,128)(2,1)S(1)} %shard_map.55.part0), channel_id=1, source_target_pairs={{0,3},{1,0},{2,1},{3,2},{4,7},{5,4},{6,5},{7,6},{8,11},{9,8},{10,9... | collective-permute-start | bytes 104456 | tf_op jit(solution)/shard_map/ppermute | solution.py:321
  13.1 27.4 %all-to-all-start = ((bf16[32,72,128]{2,1,0:T(8,128)(2,1)}), bf16[32,72,128]{2,1,0:T(8,128)(2,1)S(1)}, u32[]{:S(2)}, u32[]{:S(2)}) async-start(bf16[32,72,128]{2,1,0:T(8,128)(2,1)} %shard_map.56.after), calls=%async_computation | async-start | bytes 1179648 | tf_op jit(solution)/shard_map/all_to_all | solution.py:325
  40.5 16.3 %collective-permute-start.4 = (bf16[32,72,128]{2,1,0:T(8,128)(2,1)S(1)}, bf16[32,72,128]{2,1,0:T(8,128)(2,1)S(1)}, u32[]{:S(2)}, u32[]{:S(2)}) collective-permute-start(bf16[32,72,128]{2,1,0:T(8,128)(2,1)S(1)} %all-to-all-done.arrived.after), channel_id=1, source_target_pairs={{0,4},{4,0},{1,5},{5,1},{2,6},{6,2},{3,7},{7,3},{8,12},{12,8},{9,1... | collective-permute-start | bytes 1769480 | tf_op jit(solution)/shard_map/ppermute | solution.py:334
  44.0 2.5 %copy-start.4 = (bf16[1,2048,1280]{2,1,0:T(8,128)(2,1)S(1)}, bf16[1,2048,1280]{2,1,0:T(8,128)(2,1)}, u32[]{:S(2)}) copy-start(bf16[1,2048,1280]{2,1,0:T(8,128)(2,1)} %w_own.1) | copy-start | bytes 15728644
  54.2 14.8 %collective-permute-start.5 = (s16[264,640]{1,0:T(8,128)(2,1)S(1)}, s16[264,640]{1,0:T(8,128)(2,1)S(1)}, u32[]{:S(2)}, u32[]{:S(2)}) collective-permute-start(s16[264,640]{1,0:T(8,128)(2,1)S(1)} %get-tuple-element.15.after), channel_id=1, source_target_pairs={{0,8},{8,0},{16,24},{24,16},{1,9},{9,1},{17,25},{25,17},{2,10},{10... | collective-permute-start | bytes 1013768 | tf_op jit(solution)/shard_map/ppermute | solution.py:351
  55.0 14.1 %collective-permute-start.6 = (s16[264,640]{1,0:T(8,128)(2,1)S(1)}, s16[264,640]{1,0:T(8,128)(2,1)S(1)}, u32[]{:S(2)}, u32[]{:S(2)}) collective-permute-start(s16[264,640]{1,0:T(8,128)(2,1)S(1)} %get-tuple-element.17), channel_id=1, source_target_pairs={{0,24},{8,16},{16,8},{24,0},{1,25},{9,17},{17,9},{25,1},{2,26},{10... | collective-permute-start | bytes 1013768 | tf_op jit(solution)/shard_map/ppermute | solution.py:352
  62.5 10.2 %collective-permute-start.10 = (s16[264,640]{1,0:T(8,128)(2,1)S(1)}, s16[264,640]{1,0:T(8,128)(2,1)S(1)}, u32[]{:S(2)}, u32[]{:S(2)}) collective-permute-start(s16[264,640]{1,0:T(8,128)(2,1)S(1)} %get-tuple-element.21), channel_id=1, source_target_pairs={{0,24},{8,16},{16,8},{24,0},{1,25},{9,17},{17,9},{25,1},{2,26},{10... | collective-permute-start | bytes 1013768 | tf_op jit(solution)/shard_map/ppermute | solution.py:352
  63.5 9.2 %collective-permute-start.9 = (s16[264,640]{1,0:T(8,128)(2,1)S(1)}, s16[264,640]{1,0:T(8,128)(2,1)S(1)}, u32[]{:S(2)}, u32[]{:S(2)}) collective-permute-start(s16[264,640]{1,0:T(8,128)(2,1)S(1)} %get-tuple-element.16.after), channel_id=1, source_target_pairs={{0,8},{8,0},{16,24},{24,16},{1,9},{9,1},{17,25},{25,17},{2,10},{10... | collective-permute-start | bytes 1013768 | tf_op jit(solution)/shard_map/ppermute | solution.py:351
  69.8 47.6 %copy-start.1 = (f32[1,1280]{1,0:T(1,128)S(1)}, f32[1,1280]{1,0:T(1,128)}, u32[]{:S(2)}) copy-start(f32[1,1280]{1,0:T(1,128)} %bias.1) | copy-start | bytes 15364
  69.8 15.3 %collective-permute-start.7 = (s16[136,640]{1,0:T(8,128)(2,1)S(1)}, s16[136,640]{1,0:T(8,128)(2,1)S(1)}, u32[]{:S(2)}, u32[]{:S(2)}) collective-permute-start(s16[136,640]{1,0:T(8,128)(2,1)S(1)} %get-tuple-element.19.after), channel_id=1, source_target_pairs={{0,24},{8,16},{16,8},{24,0},{1,25},{9,17},{17,9},{25,1},{2,26},{10... | collective-permute-start | bytes 522248 | tf_op jit(solution)/shard_map/ppermute | solution.py:351
  78.5 5.6 %collective-permute-start.11 = (s16[136,640]{1,0:T(8,128)(2,1)S(1)}, s16[136,640]{1,0:T(8,128)(2,1)S(1)}, u32[]{:S(2)}, u32[]{:S(2)}) collective-permute-start(s16[136,640]{1,0:T(8,128)(2,1)S(1)} %get-tuple-element.23), channel_id=1, source_target_pairs={{0,24},{8,16},{16,8},{24,0},{1,25},{9,17},{17,9},{25,1},{2,26},{10... | collective-permute-start | bytes 522248 | tf_op jit(solution)/shard_map/ppermute | solution.py:351
  80.5 4.6 %collective-permute-start.12 = (s16[136,640]{1,0:T(8,128)(2,1)S(1)}, s16[136,640]{1,0:T(8,128)(2,1)S(1)}, u32[]{:S(2)}, u32[]{:S(2)}) collective-permute-start(s16[136,640]{1,0:T(8,128)(2,1)S(1)} %get-tuple-element.24), channel_id=1, source_target_pairs={{0,8},{8,0},{16,24},{24,16},{1,9},{9,1},{17,25},{25,17},{2,10},{10... | collective-permute-start | bytes 522248 | tf_op jit(solution)/shard_map/ppermute | solution.py:352
  80.5 8.4 %collective-permute-start.8 = (s16[136,640]{1,0:T(8,128)(2,1)S(1)}, s16[136,640]{1,0:T(8,128)(2,1)S(1)}, u32[]{:S(2)}, u32[]{:S(2)}) collective-permute-start(s16[136,640]{1,0:T(8,128)(2,1)S(1)} %get-tuple-element.20), channel_id=1, source_target_pairs={{0,8},{8,0},{16,24},{24,16},{1,9},{9,1},{17,25},{25,17},{2,10},{10... | collective-permute-start | bytes 522248 | tf_op jit(solution)/shard_map/ppermute | solution.py:352

commit v7 on v6

--- a/solution.py
+++ b/solution.py
@@ -32,7 +32,9 @@
 ANY = pl.BlockSpec(memory_space=pl.ANY)
 PIECES = 4
 GRANT = 18
-WEIGHT_GRANT = 8
+FIRST_GRANT = 44
+FIRST = 1024
+WEIGHT_GRANT = 50
 
 
 def ring(n, k):
@@ -90,7 +92,7 @@
     out_ref[n : n + OWN, :] = meta.astype(jnp.bfloat16)
 
 
-def pack_kernel(info, part0, part1, part2, part3, out_ref):
+def pack_kernel(info, part0, part1, part2, part3, out_ref, buf, sems):
     parts = (part0, part1, part2, part3)
     n_part = OWN * ACTIVE
     ids = []
@@ -122,6 +124,10 @@
         put = jnp.where(column(slot[:, here]) == slot_lane, named, 0.0).astype(jnp.bfloat16)
         meta = meta + jnp.dot(pick, put, preferred_element_type=jnp.float32)
     group = 4
+    copies = []
+    for g in range(CHIPS // group):
+        here = slice(g * group, (g + 1) * group)
+        copies.append(pltpu.make_async_copy(buf.at[here], out_ref.at[here], sems.at[g]))
     row = lax.broadcasted_iota(jnp.int32, (group * SLOTS, n_part), 0)
     for g in range(CHIPS // group):
         acc = jnp.zeros((group * SLOTS, BLOCK), jnp.float32)
@@ -133,10 +139,15 @@
         acc = acc.astype(jnp.bfloat16)
         for k in range(group):
             d = g * group + k
-            out_ref[d, 0:SLOTS, :] = acc[k * SLOTS : (k + 1) * SLOTS, :]
-            out_ref[d, SLOTS:ROWS, :] = jnp.broadcast_to(meta[d : d + 1, :], (8, 128)).astype(
+            buf[d, 0:SLOTS, :] = acc[k * SLOTS : (k + 1) * SLOTS, :]
+            buf[d, SLOTS:ROWS, :] = jnp.broadcast_to(meta[d : d + 1, :], (8, 128)).astype(
                 jnp.bfloat16
             )
+        if g > 0:
+            copies[g - 1].start()
+    copies[-1].start()
+    for copy in copies:
+        copy.wait()
 
 
 def prepare(info, arrived, tok_ref, coef_ref):
@@ -237,6 +248,31 @@
         acc[here, :] = jnp.dot(
             x_buf[here, :], weights[...], preferred_element_type=jnp.float32
         )
+
+
+def first_kernel(core, y, arrived, weights, out0, out1, w_ref, acc, tok, coef, x_buf, sems):
+    pieces = (slice(0, FIRST), slice(FIRST, w_ref.shape[0]))
+    copies = [
+        pltpu.make_async_copy(weights.at[here], w_ref.at[here], sems.at[g])
+        for g, here in enumerate(pieces)
+    ]
+    copies[0].start()
+    a, b = y[0] + 1 - 2 * lax.rem(y[0], 2), NY - 1 - y[0]
+    opposite = NY - 1 - a
+    prepare(core, arrived, tok, coef)
+    copies[1].start()
+    build((a, opposite, b, opposite), tok, coef, x_buf)
+    for g, (copy, here) in enumerate(zip(copies, pieces, strict=True)):
+        copy.wait()
+        for h in range(2):
+            rows = slice(h * 2 * PART, (h + 1) * 2 * PART)
+            term = jnp.dot(
+                x_buf[rows, here], w_ref[here, :], preferred_element_type=jnp.float32
+            )
+            if g == 0:
+                acc[rows, :] = term
+            else:
+                write_message((out0, out1)[h], acc[rows, :] + term)
 
 
 def send_kernel(core, y, arrived, weights, after, out0, out1, acc, *scratch):
@@ -319,8 +355,17 @@
         ],
     )(counts, coefficients, block_ids)
     parts = [packed] + [lax.ppermute(packed, "x", ring(NX, k)) for k in range(1, NX)]
-    outgoing = call(
-        pack_kernel, shape((CHIPS, ROWS, BLOCK), jnp.bfloat16), [SMEM] + [VMEM] * NX, 10
+    outgoing = pl.pallas_call(
+        pack_kernel,
+        out_shape=shape((CHIPS, ROWS, BLOCK), jnp.bfloat16),
+        in_specs=[SMEM] + [VMEM] * NX,
+        out_specs=HBM,
+        scratch_shapes=[
+            pltpu.VMEM((CHIPS, ROWS, BLOCK), jnp.bfloat16),
+            pltpu.SemaphoreType.DMA((CHIPS // 4,)),
+        ],
+        compiler_params=pltpu.CompilerParams(vmem_limit_bytes=10 * MIB),
+        name="pack",
     )(x.reshape(1), *parts)
     own = lax.all_to_all(outgoing, ("z", "y"), 0, 0, tiled=True)
     weights = call(
@@ -352,9 +397,14 @@
         m1 = lax.ppermute(m1, "y", pair1)
         return m0, m1
 
-    m0, m1 = call(
-        send_kernel, [message, message], given, GRANT, scratch=[total] + scratch, **product
-    )(*place, own, weights, own)
+    m0, m1, weights = call(
+        first_kernel,
+        [message, message, shape((NC * depth, width), jnp.bfloat16)],
+        [SMEM, SMEM, VMEM, HBM],
+        FIRST_GRANT,
+        scratch=[total, *scratch, pltpu.SemaphoreType.DMA((2,))],
+        **product,
+    )(*place, own, weights)
     crossing0 = cross(m0, m1, pair_a, pair_b)
     m0, m1 = call(
         send_kernel, [message, message], given, GRANT, scratch=[total] + scratch, **product

time: 119 us -> 119 us (level)
  Pallas kernels: 29.7 us -> 32.3 us
  local copies, waits for them, and re-layouts: 4.59 us -> 2.1 us
    pallas_call x2 -> x1, Pallas kernels: 11.6 us -> 5.66 us  [run(): call(send_kernel, [message, message], given, GRANT, scratch=[total] + scr...]
    pallas_call x1 -> x2, Pallas kernels: 1.76 us -> 7.55 us  [the longest x1 5.87 us: run(): call(first_kernel, [message, message, shape((NC * depth, width), jnp.bflo...]
    pallas_call x1, Pallas kernels: 1.97 us -> 4.9 us  [run(): call(weights_kernel, shape((NC * depth, width), jnp.bfloat16), [SMEM, HBM...]
    unnamed x10 -> x8, local copies, waits for them, and re-layouts: 4.59 us -> 2.1 us
  transfers between devices with their start and end apart: 14 -> 14, of which waited for: 8 -> 8; matrix products, arithmetic and copies ran while one was open for 0% -> 0% of each run, Pallas kernels for 24% -> 26%
where the time goes in v7:
time: 119 us
  Pallas kernels  32.3 us (27%)
  starting transfers between devices  29.7 us (25%)
  blocking collectives  27.7 us (23%)
  waiting for transfers between devices  26.7 us (22%)
  local copies, waits for them, and re-layouts  2.1 us (2%)
    all_to_all x1, blocking collectives, run(): lax.all_to_all(out, ('z', 'c'), 0, 0, tiled=True)  27.7 us
    all_to_all x1, waiting for transfers between devices, run(): own = lax.all_to_all(outgoing, ('z', 'y'), 0, 0, tiled=True)  16.6 us
    all_to_all x1, starting transfers between devices, run(): own = lax.all_to_all(outgoing, ('z', 'y'), 0, 0, tiled=True)  10.8 us
    pallas_call x1, Pallas kernels, run(): call(first_kernel, [message, message, shape((NC * depth, width), jnp.bflo...  5.87 us
    ppermute x4, waiting for transfers between devices, cross(): m1 = lax.ppermute(m1, 'y', pair1)  5.83 us
    pallas_call x1, Pallas kernels, run(): call(keep_middle_kernel, [kept, small, small], given + [VMEM] * 2, GRANT,...  5.68 us
    pallas_call x1, Pallas kernels, run(): call(send_kernel, [message, message], given, GRANT, scratch=[total] + scr...  5.66 us
    pallas_call x1, Pallas kernels, run(): call(keep_kernel, [shape((4 * PART, width), jnp.float32)], given, GRANT,...  5.43 us
  transfers between devices with their start and end apart: 14, of which 8 were waited for; matrix products, arithmetic and copies ran while one was open for 0% of the time, Pallas kernels for 26%

profile of v7, /device:TPU:1, one launch (start us, length us, event | category | flops | bytes accessed | tf_op | source)
XLA Modules:
  0.0 118.6 jit_solution(14640225921208989403)
XLA Ops:
  0.0 3.2 %collective-permute-start.3 = (bf16[1,2048,1280]{2,1,0:T(8,128)(2,1)}, bf16[1,2048,1280]{2,1,0:T(8,128)(2,1)}, u32[]{:S(2)}, u32[]{:S(2)}) collective-permute-start(bf16[1,2048,1280]{2,1,0:T(8,128)(2,1)} %w_own.1), channel_id=1, source_target_pairs={{0,4},{4,0},{1,5},{5,1},{2,6},{6,2},{3,7},{7,3},{8,12},{12,8},{9,1... | collective-permute-start | bytes 15728648 | tf_op jit(solution)/shard_map/ppermute | solution.py:342
  6.1 1.9 %collective-permute-start.1 = (bf16[136,128]{1,0:T(8,128)(2,1)S(1)}, bf16[136,128]{1,0:T(8,128)(2,1)S(1)}, u32[]{:S(2)}, u32[]{:S(2)}) collective-permute-start(bf16[136,128]{1,0:T(8,128)(2,1)S(1)} %shard_map.55.part0), channel_id=1, source_target_pairs={{0,2},{1,3},{2,0},{3,1},{4,6},{5,7},{6,4},{7,5},{8,10},{9,11},{10,... | collective-permute-start | bytes 104456 | tf_op jit(solution)/shard_map/ppermute | solution.py:357
  8.1 1.2 collective-permute-start.2
  9.2 0.9 collective-permute-done.part1
  11.3 1.7 %pack.1.after = bf16[32,72,128]{2,1,0:T(8,128)(2,1)} custom-call(s32[1]{0:T(128)} %bitcast.2.info, bf16[136,128]{1,0:T(8,128)(2,1)S(1)} %shard_map.55.part0, bf16[136,128]{1,0:T(8,128)(2,1)S(1)} %collective-permute-done.part1, bf16[136,128]{1,0:T(8,128)(2,1)S(1)} %collective-permute-done.1.part2, bf16[136,128]{1,0:T(8,128)(2,1)S(1)} %collective-permute-done.2.part3), custom_call_target="tpu_custom_call" | custom-call | tf_op jit(solution)/shard_map/pack/pallas_call | solution.py:358
  13.0 10.8 %all-to-all-start = ((bf16[32,72,128]{2,1,0:T(8,128)(2,1)}), bf16[32,72,128]{2,1,0:T(8,128)(2,1)S(1)}, u32[]{:S(2)}, u32[]{:S(2)}) async-start(bf16[32,72,128]{2,1,0:T(8,128)(2,1)} %pack.1.after), calls=%async_computation | async-start | bytes 1179648 | tf_op jit(solution)/shard_map/all_to_all | solution.py:370
  23.8 16.6 %all-to-all-done.arrived = bf16[32,72,128]{2,1,0:T(8,128)(2,1)S(1)} async-done(((bf16[32,72,128]{2,1,0:T(8,128)(2,1)}), bf16[32,72,128]{2,1,0:T(8,128)(2,1)S(1)}, u32[]{:S(2)}, u32[]{:S(2)}) %all-to-all-start) | async-done | bytes 589856 | tf_op jit(solution)/shard_map/all_to_all | solution.py:370
  40.4 3.5 %collective-permute-start.4 = (bf16[32,72,128]{2,1,0:T(8,128)(2,1)S(1)}, bf16[32,72,128]{2,1,0:T(8,128)(2,1)S(1)}, u32[]{:S(2)}, u32[]{:S(2)}) collective-permute-start(bf16[32,72,128]{2,1,0:T(8,128)(2,1)S(1)} %all-to-all-done.arrived), channel_id=1, source_target_pairs={{0,4},{4,0},{1,5},{5,1},{2,6},{6,2},{3,7},{7,3},{8,12},{12,8},{9,1... | collective-permute-start | bytes 1769480 | tf_op jit(solution)/shard_map/ppermute | solution.py:379
  43.9 4.9 %shard_map.56.weights = bf16[4096,640]{1,0:T(8,128)(2,1)} custom-call(s32[1]{0:T(128)} %bitcast.core_ref.core.info, bf16[1,2048,1280]{2,1,0:T(8,128)(2,1)} %w_own.1, bf16[1,2048,1280]{2,1,0:T(8,128)(2,1)} %collective-permute-done.3.w_other, bf16[32,72,128]{2,1,0:T(8,128)(2,1)} %pack.1.after), custom_call_target="tpu_custom_call" | custom-call | flops 10000000000 | bytes 2097152 | tf_op jit(solution)/shard_map/pallas_call | solution.py:371
  48.8 5.9 %shard_map.57 = (s16[264,640]{1,0:T(8,128)(2,1)S(1)}, s16[264,640]{1,0:T(8,128)(2,1)S(1)}, bf16[4096,640]{1,0:T(8,128)(2,1)S(1)}) custom-call(s32[1]{0:T(128)} %bitcast.core_ref.core.info, s32[1]{0:T(128)} %bitcast.1.y, bf16[32,72,128]{2,1,0:T(8,128)(2,1)S(1)} %all-to-all-done.arrived, bf16[4096,640]{1,0:T(8,128)(2,1)} %shard_map.56.weights), custom_call_target="tpu_custom_call" | custom-call | flops 2684354560 | bytes 2097152 | tf_op jit(solution)/shard_map/pallas_call | solution.py:400
  55.4 1.8 %collective-permute-start.6 = (s16[264,640]{1,0:T(8,128)(2,1)S(1)}, s16[264,640]{1,0:T(8,128)(2,1)S(1)}, u32[]{:S(2)}, u32[]{:S(2)}) collective-permute-start(s16[264,640]{1,0:T(8,128)(2,1)S(1)} %get-tuple-element.19), channel_id=1, source_target_pairs={{0,24},{8,16},{16,8},{24,0},{1,25},{9,17},{17,9},{25,1},{2,26},{10... | collective-permute-start | bytes 1013768 | tf_op jit(solution)/shard_map/ppermute | solution.py:397
  57.2 5.7 %shard_map.58 = (s16[264,640]{1,0:T(8,128)(2,1)S(1)}, s16[264,640]{1,0:T(8,128)(2,1)S(1)}) custom-call(s32[1]{0:T(128)} %bitcast.core_ref.core.info, s32[1]{0:T(128)} %bitcast.1.y, bf16[32,72,128]{2,1,0:T(8,128)(2,1)S(1)} %collective-permute-done.4.arrived, bf16[4096,640]{1,0:T(8,128)(2,1)S(1)} %get-tuple-element.16.weights, ...), custom_call_target="tpu_custom_call" | custom-call | flops 2684354560 | bytes 2097152 | tf_op jit(solution)/shard_map/pallas_call | solution.py:409
  62.9 1.0 collective-permute-start.10
  63.8 5.4 %shard_map.59.kept = f32[512,640]{1,0:T(8,128)S(1)} custom-call(s32[1]{0:T(128)} %bitcast.core_ref.core.info, s32[1]{0:T(128)} %bitcast.1.y, bf16[32,72,128]{2,1,0:T(8,128)(2,1)S(1)} %all-to-all-done.arrived, bf16[4096,640]{1,0:T(8,128)(2,1)S(1)} %get-tuple-element.16.weights, s16[264,640]{1,0:T(8,128)(2,1)S(1)} %get-tuple-element.18.after), custom_call_target="tpu_custom_call" | custom-call | flops 2684354560 | bytes 2097152 | tf_op jit(solution)/shard_map/pallas_call | solution.py:413
  70.0 2.1 %collective-permute-start.7 = (s16[136,640]{1,0:T(8,128)(2,1)S(1)}, s16[136,640]{1,0:T(8,128)(2,1)S(1)}, u32[]{:S(2)}, u32[]{:S(2)}) collective-permute-start(s16[136,640]{1,0:T(8,128)(2,1)S(1)} %get-tuple-element.21.after), channel_id=1, source_target_pairs={{0,24},{8,16},{16,8},{24,0},{1,25},{9,17},{17,9},{25,1},{2,26},{10... | collective-permute-start | bytes 522248 | tf_op jit(solution)/shard_map/ppermute | solution.py:396
  72.1 1.0 collective-permute-done.10.in1
  73.1 5.7 %shard_map.61 = (f32[256,640]{1,0:T(8,128)S(1)}, s16[136,640]{1,0:T(8,128)(2,1)S(1)}, s16[136,640]{1,0:T(8,128)(2,1)S(1)}) custom-call(s32[1]{0:T(128)} %bitcast.core_ref.core.info, s32[1]{0:T(128)} %bitcast.1.y, bf16[32,72,128]{2,1,0:T(8,128)(2,1)S(1)} %collective-permute-done.4.arrived, bf16[4096,640]{1,0:T(8,128)(2,1)S(1)} %get-tuple-element.16.weights, ...), custom_call_target="tpu_custom_call" | custom-call | flops 2684354560 | bytes 2097152 | tf_op jit(solution)/shard_map/pallas_call | solution.py:423
  78.8 2.0 %collective-permute-start.11 = (s16[136,640]{1,0:T(8,128)(2,1)S(1)}, s16[136,640]{1,0:T(8,128)(2,1)S(1)}, u32[]{:S(2)}, u32[]{:S(2)}) collective-permute-start(s16[136,640]{1,0:T(8,128)(2,1)S(1)} %get-tuple-element.25), channel_id=1, source_target_pairs={{0,24},{8,16},{16,8},{24,0},{1,25},{9,17},{17,9},{25,1},{2,26},{10... | collective-permute-start | bytes 522248 | tf_op jit(solution)/shard_map/ppermute | solution.py:396
  80.8 1.5 %collective-permute-start.8 = (s16[136,640]{1,0:T(8,128)(2,1)S(1)}, s16[136,640]{1,0:T(8,128)(2,1)S(1)}, u32[]{:S(2)}, u32[]{:S(2)}) collective-permute-start(s16[136,640]{1,0:T(8,128)(2,1)S(1)} %get-tuple-element.22), channel_id=1, source_target_pairs={{0,8},{8,0},{16,24},{24,16},{1,9},{9,1},{17,25},{25,17},{2,10},{10... | collective-permute-start | bytes 522248 | tf_op jit(solution)/shard_map/ppermute | solution.py:397
  82.2 2.1 %collective-permute-done.11.refs_4_ = s16[136,640]{1,0:T(8,128)(2,1)S(1)} collective-permute-done((s16[136,640]{1,0:T(8,128)(2,1)S(1)}, s16[136,640]{1,0:T(8,128)(2,1)S(1)}, u32[]{:S(2)}, u32[]{:S(2)}) %collective-permute-start.11) | collective-permute-done | bytes 174112 | tf_op jit(solution)/shard_map/ppermute | solution.py:396
  84.3 1.1 collective-permute-done.12.refs_5_
  85.5 3.7 %collective-permute-done.8.refs_2_ = s16[136,640]{1,0:T(8,128)(2,1)S(1)} collective-permute-done((s16[136,640]{1,0:T(8,128)(2,1)S(1)}, s16[136,640]{1,0:T(8,128)(2,1)S(1)}, u32[]{:S(2)}, u32[]{:S(2)}) %collective-permute-start.8) | collective-permute-done | bytes 174112 | tf_op jit(solution)/shard_map/ppermute | solution.py:397
  90.0 27.7 %all_to_all.10.ref = s16[16,32,768]{2,1,0:T(8,128)(2,1)S(1)} all-to-all(s16[16,32,768]{2,1,0:T(8,128)(2,1)S(1)} %shard_map.62), channel_id=1, replica_groups=mesh['z'=8,'y'=4,'c'=2,'x'=4] {'z','c'}, dimensions={0} | all-to-all | bytes 1572864 | tf_op jit(solution)/shard_map/all_to_all | solution.py:437
  117.7 0.9 shard_map.63
  (23 shorter events, 6.4 us)
Async XLA Ops:
  0.0 43.9 %collective-permute-start.3 = (bf16[1,2048,1280]{2,1,0:T(8,128)(2,1)}, bf16[1,2048,1280]{2,1,0:T(8,128)(2,1)}, u32[]{:S(2)}, u32[]{:S(2)}) collective-permute-start(bf16[1,2048,1280]{2,1,0:T(8,128)(2,1)} %w_own.1), channel_id=1, source_target_pairs={{0,4},{4,0},{1,5},{5,1},{2,6},{6,2},{3,7},{7,3},{8,12},{12,8},{9,1... | collective-permute-start | bytes 15728648 | tf_op jit(solution)/shard_map/ppermute | solution.py:342
  3.2 0.8 copy-start
  4.0 0.7 copy-start.2
  4.6 0.7 copy-start.3
  6.0 4.1 %collective-permute-start = (bf16[136,128]{1,0:T(8,128)(2,1)S(1)}, bf16[136,128]{1,0:T(8,128)(2,1)S(1)}, u32[]{:S(2)}, u32[]{:S(2)}) collective-permute-start(bf16[136,128]{1,0:T(8,128)(2,1)S(1)} %shard_map.55.part0), channel_id=1, source_target_pairs={{0,1},{1,2},{2,3},{3,0},{4,5},{5,6},{6,7},{7,4},{8,9},{9,10},{10,1... | collective-permute-start | bytes 104456 | tf_op jit(solution)/shard_map/ppermute | solution.py:357
  6.1 4.4 %collective-permute-start.1 = (bf16[136,128]{1,0:T(8,128)(2,1)S(1)}, bf16[136,128]{1,0:T(8,128)(2,1)S(1)}, u32[]{:S(2)}, u32[]{:S(2)}) collective-permute-start(bf16[136,128]{1,0:T(8,128)(2,1)S(1)} %shard_map.55.part0), channel_id=1, source_target_pairs={{0,2},{1,3},{2,0},{3,1},{4,6},{5,7},{6,4},{7,5},{8,10},{9,11},{10,... | collective-permute-start | bytes 104456 | tf_op jit(solution)/shard_map/ppermute | solution.py:357
  8.1 3.3 %collective-permute-start.2 = (bf16[136,128]{1,0:T(8,128)(2,1)S(1)}, bf16[136,128]{1,0:T(8,128)(2,1)S(1)}, u32[]{:S(2)}, u32[]{:S(2)}) collective-permute-start(bf16[136,128]{1,0:T(8,128)(2,1)S(1)} %shard_map.55.part0), channel_id=1, source_target_pairs={{0,3},{1,0},{2,1},{3,2},{4,7},{5,4},{6,5},{7,6},{8,11},{9,8},{10,9... | collective-permute-start | bytes 104456 | tf_op jit(solution)/shard_map/ppermute | solution.py:357
  13.0 27.4 %all-to-all-start = ((bf16[32,72,128]{2,1,0:T(8,128)(2,1)}), bf16[32,72,128]{2,1,0:T(8,128)(2,1)S(1)}, u32[]{:S(2)}, u32[]{:S(2)}) async-start(bf16[32,72,128]{2,1,0:T(8,128)(2,1)} %pack.1.after), calls=%async_computation | async-start | bytes 1179648 | tf_op jit(solution)/shard_map/all_to_all | solution.py:370
  40.4 16.8 %collective-permute-start.4 = (bf16[32,72,128]{2,1,0:T(8,128)(2,1)S(1)}, bf16[32,72,128]{2,1,0:T(8,128)(2,1)S(1)}, u32[]{:S(2)}, u32[]{:S(2)}) collective-permute-start(bf16[32,72,128]{2,1,0:T(8,128)(2,1)S(1)} %all-to-all-done.arrived), channel_id=1, source_target_pairs={{0,4},{4,0},{1,5},{5,1},{2,6},{6,2},{3,7},{7,3},{8,12},{12,8},{9,1... | collective-permute-start | bytes 1769480 | tf_op jit(solution)/shard_map/ppermute | solution.py:379
  54.7 14.6 %collective-permute-start.5 = (s16[264,640]{1,0:T(8,128)(2,1)S(1)}, s16[264,640]{1,0:T(8,128)(2,1)S(1)}, u32[]{:S(2)}, u32[]{:S(2)}) collective-permute-start(s16[264,640]{1,0:T(8,128)(2,1)S(1)} %get-tuple-element.17.after), channel_id=1, source_target_pairs={{0,8},{8,0},{16,24},{24,16},{1,9},{9,1},{17,25},{25,17},{2,10},{10... | collective-permute-start | bytes 1013768 | tf_op jit(solution)/shard_map/ppermute | solution.py:396
  55.4 13.9 %collective-permute-start.6 = (s16[264,640]{1,0:T(8,128)(2,1)S(1)}, s16[264,640]{1,0:T(8,128)(2,1)S(1)}, u32[]{:S(2)}, u32[]{:S(2)}) collective-permute-start(s16[264,640]{1,0:T(8,128)(2,1)S(1)} %get-tuple-element.19), channel_id=1, source_target_pairs={{0,24},{8,16},{16,8},{24,0},{1,25},{9,17},{17,9},{25,1},{2,26},{10... | collective-permute-start | bytes 1013768 | tf_op jit(solution)/shard_map/ppermute | solution.py:397
  62.9 10.2 %collective-permute-start.10 = (s16[264,640]{1,0:T(8,128)(2,1)S(1)}, s16[264,640]{1,0:T(8,128)(2,1)S(1)}, u32[]{:S(2)}, u32[]{:S(2)}) collective-permute-start(s16[264,640]{1,0:T(8,128)(2,1)S(1)} %get-tuple-element.23), channel_id=1, source_target_pairs={{0,24},{8,16},{16,8},{24,0},{1,25},{9,17},{17,9},{25,1},{2,26},{10... | collective-permute-start | bytes 1013768 | tf_op jit(solution)/shard_map/ppermute | solution.py:397
  63.8 9.2 %collective-permute-start.9 = (s16[264,640]{1,0:T(8,128)(2,1)S(1)}, s16[264,640]{1,0:T(8,128)(2,1)S(1)}, u32[]{:S(2)}, u32[]{:S(2)}) collective-permute-start(s16[264,640]{1,0:T(8,128)(2,1)S(1)} %get-tuple-element.18.after), channel_id=1, source_target_pairs={{0,8},{8,0},{16,24},{24,16},{1,9},{9,1},{17,25},{25,17},{2,10},{10... | collective-permute-start | bytes 1013768 | tf_op jit(solution)/shard_map/ppermute | solution.py:396
  70.0 47.7 %copy-start.1 = (f32[1,1280]{1,0:T(1,128)S(1)}, f32[1,1280]{1,0:T(1,128)}, u32[]{:S(2)}) copy-start(f32[1,1280]{1,0:T(1,128)} %bias.1) | copy-start | bytes 15364
  70.0 15.5 %collective-permute-start.7 = (s16[136,640]{1,0:T(8,128)(2,1)S(1)}, s16[136,640]{1,0:T(8,128)(2,1)S(1)}, u32[]{:S(2)}, u32[]{:S(2)}) collective-permute-start(s16[136,640]{1,0:T(8,128)(2,1)S(1)} %get-tuple-element.21.after), channel_id=1, source_target_pairs={{0,24},{8,16},{16,8},{24,0},{1,25},{9,17},{17,9},{25,1},{2,26},{10... | collective-permute-start | bytes 522248 | tf_op jit(solution)/shard_map/ppermute | solution.py:396
  78.8 5.6 %collective-permute-start.11 = (s16[136,640]{1,0:T(8,128)(2,1)S(1)}, s16[136,640]{1,0:T(8,128)(2,1)S(1)}, u32[]{:S(2)}, u32[]{:S(2)}) collective-permute-start(s16[136,640]{1,0:T(8,128)(2,1)S(1)} %get-tuple-element.25), channel_id=1, source_target_pairs={{0,24},{8,16},{16,8},{24,0},{1,25},{9,17},{17,9},{25,1},{2,26},{10... | collective-permute-start | bytes 522248 | tf_op jit(solution)/shard_map/ppermute | solution.py:396
  80.8 4.7 %collective-permute-start.12 = (s16[136,640]{1,0:T(8,128)(2,1)S(1)}, s16[136,640]{1,0:T(8,128)(2,1)S(1)}, u32[]{:S(2)}, u32[]{:S(2)}) collective-permute-start(s16[136,640]{1,0:T(8,128)(2,1)S(1)} %get-tuple-element.26), channel_id=1, source_target_pairs={{0,8},{8,0},{16,24},{24,16},{1,9},{9,1},{17,25},{25,17},{2,10},{10... | collective-permute-start | bytes 522248 | tf_op jit(solution)/shard_map/ppermute | solution.py:397
  80.8 8.4 %collective-permute-start.8 = (s16[136,640]{1,0:T(8,128)(2,1)S(1)}, s16[136,640]{1,0:T(8,128)(2,1)S(1)}, u32[]{:S(2)}, u32[]{:S(2)}) collective-permute-start(s16[136,640]{1,0:T(8,128)(2,1)S(1)} %get-tuple-element.22), channel_id=1, source_target_pairs={{0,8},{8,0},{16,24},{24,16},{1,9},{9,1},{17,25},{25,17},{2,10},{10... | collective-permute-start | bytes 522248 | tf_op jit(solution)/shard_map/ppermute | solution.py:397

commit v8 on v7

--- a/solution.py
+++ b/solution.py
@@ -1,3 +1,5 @@
+import functools
+
 import jax
 import jax.numpy as jnp
 from jax import lax
@@ -219,11 +221,12 @@
     t = lax.broadcasted_iota(jnp.int32, (TOK, 128), 0).astype(jnp.float32) + 1.0
 
     def source(i, carry):
-        h, j, z = i // 8, (i // 4) % 2, i % 4
-        first, second = jnp.where(h == 0, rows_of[0], rows_of[2]), jnp.where(
-            h == 0, rows_of[1], rows_of[3]
-        )
-        n = (h * 4 + z) * NY + jnp.where(j == 0, first, second)
+        each = len(rows_of) // 2
+        h, j, z = i // (4 * each), (i // 4) % each, i % 4
+        y = rows_of[-1]
+        for k in range(len(rows_of) - 1):
+            y = jnp.where(h * each + j == k, rows_of[k], y)
+        n = (h * 4 + z) * NY + y
         base = pl.multiple_of(i * TOK, TOK)
         for b in range(BLOCKS_CHIP):
             row = jnp.zeros((TOK, 128), jnp.float32)
@@ -234,7 +237,7 @@
             x_buf[pl.ds(base, TOK), b * BLOCK : (b + 1) * BLOCK] = row.astype(jnp.bfloat16)
         return carry
 
-    lax.fori_loop(0, 4 * PART // TOK, source, 0)
+    lax.fori_loop(0, len(rows_of) * PART // TOK, source, 0)
 
 
 def multiply(send, core, y_ref, arrived, weights, tok, coef, x_buf, acc):
@@ -285,14 +288,18 @@
     multiply(False, core, y, arrived, weights, *scratch, out_ref)
 
 
-def keep_middle_kernel(
-    core, y, arrived, weights, after, in0, in1, keep_ref, out0, out1, acc, *scratch
-):
-    multiply(False, core, y, arrived, weights, *scratch, acc)
-    for h, (ref, out) in enumerate(((in0, out0), (in1, out1))):
-        low, high = 2 * h * PART, (2 * h + 1) * PART
-        keep_ref[h * PART : (h + 1) * PART, :] = acc[low:high, :] + read_message(ref, 0)
-        write_message(out, acc[high : high + PART, :] + read_message(ref, 1))
+def half_kernel(leave, core, y_ref, arrived, weights, after, in0, in1, *rest):
+    outs, (tok, coef, x_buf) = rest[:-3], rest[-3:]
+    y = y_ref[0]
+    prepare(core, arrived, tok, coef)
+    build((NY - 1 - y, y + 1 - 2 * lax.rem(y, 2)) if leave else (y, y), tok, coef, x_buf)
+    acc = jnp.dot(x_buf[...], weights[...], preferred_element_type=jnp.float32)
+    for h, ref in enumerate((in0, in1)):
+        part = acc[h * PART : (h + 1) * PART, :] + read_message(ref, 1 if leave else 0)
+        if leave:
+            write_message(outs[h], part)
+        else:
+            outs[0][h * PART : (h + 1) * PART, :] = part
 
 
 def middle_kernel(kept, in0, in1, keep_ref, out0, out1):
@@ -354,7 +361,9 @@
             pltpu.SemaphoreType.DMA((3,)),
         ],
     )(counts, coefficients, block_ids)
-    parts = [packed] + [lax.ppermute(packed, "x", ring(NX, k)) for k in range(1, NX)]
+    parts = [packed]
+    for k in range(1, NX):
+        parts.append(lax.ppermute(packed, "x", ring(NX, k)))
     outgoing = pl.pallas_call(
         pack_kernel,
         out_shape=shape((CHIPS, ROWS, BLOCK), jnp.bfloat16),
@@ -420,15 +429,21 @@
     )(*place, own, weights, m0)
     kept0, m0, m1 = call(middle_kernel, [kept, small, small], [VMEM] * 3, 10)(sums, *crossing0)
     arrived0 = cross(m0, m1, pair_b, pair_a)
-    kept1, m0, m1 = call(
-        keep_middle_kernel,
-        [kept, small, small],
-        given + [VMEM] * 2,
-        GRANT,
-        scratch=[total] + scratch,
-        **product,
-    )(*place, other, weights, m0, *crossing1)
+    half = scratch[:2] + [pltpu.VMEM((2 * PART, NC * depth), jnp.bfloat16)]
+
+    def second_half(leave, out_shape, after):
+        return call(
+            functools.partial(half_kernel, leave),
+            out_shape,
+            given + [VMEM] * 2,
+            GRANT,
+            flops=2 * 2 * PART * NC * depth * width,
+            scratch=half,
+        )(*place, other, weights, after, *crossing1)
+
+    m0, m1 = second_half(True, [small, small], m0)
     arrived1 = cross(m0, m1, pair_b, pair_a)
+    (kept1,) = second_half(False, [kept], m0)
     out = call(
         last_kernel, shape((NZ * NC, TOK, width + 128), jnp.int16), [SMEM] + [VMEM] * 6, 10
     )(core.reshape(1), kept0, *arrived0, kept1, *arrived1)

time: 119 us -> 116 us (0.975)
  waiting for transfers between devices: 26.7 us -> 23.9 us
    ppermute x4, waiting for transfers between devices: 2.11 us -> 0.01 us  [cross(): m0 = lax.ppermute(m0, 'y', pair0)]
    pallas_call x1 -> x2, Pallas kernels: 5.68 us -> 6.1 us  [second_half(): call(functools.partial(half_kernel, leave), out_shape, given + [VMEM] * 2...]
  transfers between devices with their start and end apart: 14 -> 14, of which waited for: 8 -> 7; matrix products, arithmetic and copies ran while one was open for 0% -> 0% of each run, Pallas kernels for 26% -> 27%
where the time goes in v8:
time: 116 us
  Pallas kernels  32.8 us (28%)
  starting transfers between devices  29.5 us (25%)
  blocking collectives  27.7 us (24%)
  waiting for transfers between devices  23.9 us (21%)
  local copies, waits for them, and re-layouts  2.1 us (2%)
    all_to_all x1, blocking collectives, run(): lax.all_to_all(out, ('z', 'c'), 0, 0, tiled=True)  27.7 us
    all_to_all x1, waiting for transfers between devices, run(): own = lax.all_to_all(outgoing, ('z', 'y'), 0, 0, tiled=True)  16.6 us
    all_to_all x1, starting transfers between devices, run(): own = lax.all_to_all(outgoing, ('z', 'y'), 0, 0, tiled=True)  10.8 us
    pallas_call x2, Pallas kernels, second_half(): call(functools.partial(half_kernel, leave), out_shape, given + [VMEM] * 2...  6.1 us
    pallas_call x1, Pallas kernels, run(): call(first_kernel, [message, message, shape((NC * depth, width), jnp.bflo...  5.89 us
    pallas_call x1, Pallas kernels, run(): call(send_kernel, [message, message], given, GRANT, scratch=[total] + scr...  5.69 us
    pallas_call x1, Pallas kernels, run(): call(keep_kernel, [shape((4 * PART, width), jnp.float32)], given, GRANT,...  5.46 us
    ppermute x4, waiting for transfers between devices, cross(): m1 = lax.ppermute(m1, 'y', pair1)  5.23 us
  transfers between devices with their start and end apart: 14, of which 7 were waited for; matrix products, arithmetic and copies ran while one was open for 0% of the time, Pallas kernels for 27%

profile of v8, /device:TPU:1, one launch (start us, length us, event | category | flops | bytes accessed | tf_op | source)
XLA Modules:
  0.0 116.1 jit_solution(2021089171562971067)
XLA Ops:
  0.0 3.2 %collective-permute-start.3 = (bf16[1,2048,1280]{2,1,0:T(8,128)(2,1)}, bf16[1,2048,1280]{2,1,0:T(8,128)(2,1)}, u32[]{:S(2)}, u32[]{:S(2)}) collective-permute-start(bf16[1,2048,1280]{2,1,0:T(8,128)(2,1)} %w_own.1), channel_id=1, source_target_pairs={{0,4},{4,0},{1,5},{5,1},{2,6},{6,2},{3,7},{7,3},{8,12},{12,8},{9,1... | collective-permute-start | bytes 15728648 | tf_op jit(solution)/shard_map/ppermute | solution.py:349
  6.1 1.9 %collective-permute-start.1 = (bf16[136,128]{1,0:T(8,128)(2,1)S(1)}, bf16[136,128]{1,0:T(8,128)(2,1)S(1)}, u32[]{:S(2)}, u32[]{:S(2)}) collective-permute-start(bf16[136,128]{1,0:T(8,128)(2,1)S(1)} %shard_map.55.part0), channel_id=1, source_target_pairs={{0,2},{1,3},{2,0},{3,1},{4,6},{5,7},{6,4},{7,5},{8,10},{9,11},{10,... | collective-permute-start | bytes 104456 | tf_op jit(solution)/shard_map/ppermute | solution.py:366
  8.1 1.2 collective-permute-start.2
  9.2 0.9 collective-permute-done.part1
  10.5 0.8 collective-permute-done.2.part3
  11.3 1.7 %pack.1.after = bf16[32,72,128]{2,1,0:T(8,128)(2,1)} custom-call(s32[1]{0:T(128)} %bitcast.2.info, bf16[136,128]{1,0:T(8,128)(2,1)S(1)} %shard_map.55.part0, bf16[136,128]{1,0:T(8,128)(2,1)S(1)} %collective-permute-done.part1, bf16[136,128]{1,0:T(8,128)(2,1)S(1)} %collective-permute-done.1.part2, bf16[136,128]{1,0:T(8,128)(2,1)S(1)} %collective-permute-done.2.part3), custom_call_target="tpu_custom_call" | custom-call | tf_op jit(solution)/shard_map/pack/pallas_call | solution.py:367
  13.0 10.8 %all-to-all-start = ((bf16[32,72,128]{2,1,0:T(8,128)(2,1)}), bf16[32,72,128]{2,1,0:T(8,128)(2,1)S(1)}, u32[]{:S(2)}, u32[]{:S(2)}) async-start(bf16[32,72,128]{2,1,0:T(8,128)(2,1)} %pack.1.after), calls=%async_computation | async-start | bytes 1179648 | tf_op jit(solution)/shard_map/all_to_all | solution.py:379
  23.8 16.6 %all-to-all-done.arrived = bf16[32,72,128]{2,1,0:T(8,128)(2,1)S(1)} async-done(((bf16[32,72,128]{2,1,0:T(8,128)(2,1)}), bf16[32,72,128]{2,1,0:T(8,128)(2,1)S(1)}, u32[]{:S(2)}, u32[]{:S(2)}) %all-to-all-start) | async-done | bytes 589856 | tf_op jit(solution)/shard_map/all_to_all | solution.py:379
  40.4 3.5 %collective-permute-start.4 = (bf16[32,72,128]{2,1,0:T(8,128)(2,1)S(1)}, bf16[32,72,128]{2,1,0:T(8,128)(2,1)S(1)}, u32[]{:S(2)}, u32[]{:S(2)}) collective-permute-start(bf16[32,72,128]{2,1,0:T(8,128)(2,1)S(1)} %all-to-all-done.arrived), channel_id=1, source_target_pairs={{0,4},{4,0},{1,5},{5,1},{2,6},{6,2},{3,7},{7,3},{8,12},{12,8},{9,1... | collective-permute-start | bytes 1769480 | tf_op jit(solution)/shard_map/ppermute | solution.py:388
  43.9 4.9 %shard_map.56.weights = bf16[4096,640]{1,0:T(8,128)(2,1)} custom-call(s32[1]{0:T(128)} %bitcast.core_ref.core.info, bf16[1,2048,1280]{2,1,0:T(8,128)(2,1)} %w_own.1, bf16[1,2048,1280]{2,1,0:T(8,128)(2,1)} %collective-permute-done.3.w_other, bf16[32,72,128]{2,1,0:T(8,128)(2,1)} %pack.1.after), custom_call_target="tpu_custom_call" | custom-call | flops 10000000000 | bytes 2097152 | tf_op jit(solution)/shard_map/pallas_call | solution.py:380
  48.8 5.9 %shard_map.57 = (s16[264,640]{1,0:T(8,128)(2,1)S(1)}, s16[264,640]{1,0:T(8,128)(2,1)S(1)}, bf16[4096,640]{1,0:T(8,128)(2,1)S(1)}) custom-call(s32[1]{0:T(128)} %bitcast.core_ref.core.info, s32[1]{0:T(128)} %bitcast.1.y.y_ref, bf16[32,72,128]{2,1,0:T(8,128)(2,1)S(1)} %all-to-all-done.arrived, bf16[4096,640]{1,0:T(8,128)(2,1)} %shard_map.56.weights), custom_call_target="tpu_custom_call" | custom-call | flops 2684354560 | bytes 2097152 | tf_op jit(solution)/shard_map/pallas_call | solution.py:409
  55.4 1.8 %collective-permute-start.6 = (s16[264,640]{1,0:T(8,128)(2,1)S(1)}, s16[264,640]{1,0:T(8,128)(2,1)S(1)}, u32[]{:S(2)}, u32[]{:S(2)}) collective-permute-start(s16[264,640]{1,0:T(8,128)(2,1)S(1)} %get-tuple-element.18), channel_id=1, source_target_pairs={{0,24},{8,16},{16,8},{24,0},{1,25},{9,17},{17,9},{25,1},{2,26},{10... | collective-permute-start | bytes 1013768 | tf_op jit(solution)/shard_map/ppermute | solution.py:406
  57.2 5.7 %shard_map.58 = (s16[264,640]{1,0:T(8,128)(2,1)S(1)}, s16[264,640]{1,0:T(8,128)(2,1)S(1)}) custom-call(s32[1]{0:T(128)} %bitcast.core_ref.core.info, s32[1]{0:T(128)} %bitcast.1.y.y_ref, bf16[32,72,128]{2,1,0:T(8,128)(2,1)S(1)} %collective-permute-done.4.arrived, bf16[4096,640]{1,0:T(8,128)(2,1)S(1)} %get-tuple-element.15.weights, ...), custom_call_target="tpu_custom_call" | custom-call | flops 2684354560 | bytes 2097152 | tf_op jit(solution)/shard_map/pallas_call | solution.py:418
  62.9 1.0 collective-permute-start.10
  63.9 5.5 %shard_map.59.kept = f32[512,640]{1,0:T(8,128)S(1)} custom-call(s32[1]{0:T(128)} %bitcast.core_ref.core.info, s32[1]{0:T(128)} %bitcast.1.y.y_ref, bf16[32,72,128]{2,1,0:T(8,128)(2,1)S(1)} %all-to-all-done.arrived, bf16[4096,640]{1,0:T(8,128)(2,1)S(1)} %get-tuple-element.15.weights, s16[264,640]{1,0:T(8,128)(2,1)S(1)} %get-tuple-element.17.after), custom_call_target="tpu_custom_call" | custom-call | flops 2684354560 | bytes 2097152 | tf_op jit(solution)/shard_map/pallas_call | solution.py:422
  70.1 1.9 %collective-permute-start.7 = (s16[136,640]{1,0:T(8,128)(2,1)S(1)}, s16[136,640]{1,0:T(8,128)(2,1)S(1)}, u32[]{:S(2)}, u32[]{:S(2)}) collective-permute-start(s16[136,640]{1,0:T(8,128)(2,1)S(1)} %get-tuple-element.20.after), channel_id=1, source_target_pairs={{0,24},{8,16},{16,8},{24,0},{1,25},{9,17},{17,9},{25,1},{2,26},{10... | collective-permute-start | bytes 522248 | tf_op jit(solution)/shard_map/ppermute | solution.py:405
  71.9 1.2 %collective-permute-done.10.in1 = s16[264,640]{1,0:T(8,128)(2,1)S(1)} collective-permute-done((s16[264,640]{1,0:T(8,128)(2,1)S(1)}, s16[264,640]{1,0:T(8,128)(2,1)S(1)}, u32[]{:S(2)}, u32[]{:S(2)}) %collective-permute-start.10) | collective-permute-done | bytes 337952 | tf_op jit(solution)/shard_map/ppermute | solution.py:406
  73.1 3.2 %shard_map.61 = (s16[136,640]{1,0:T(8,128)(2,1)S(1)}, s16[136,640]{1,0:T(8,128)(2,1)S(1)}) custom-call(s32[1]{0:T(128)} %bitcast.core_ref.core.info, s32[1]{0:T(128)} %bitcast.1.y.y_ref, bf16[32,72,128]{2,1,0:T(8,128)(2,1)S(1)} %collective-permute-done.4.arrived, bf16[4096,640]{1,0:T(8,128)(2,1)S(1)} %get-tuple-element.15.weights, ...), custom_call_target="tpu_custom_call" | custom-call | flops 1342177280 | bytes 2097152 | tf_op jit(solution)/shard_map/pallas_call | solution.py:435
  76.3 2.0 %collective-permute-start.11 = (s16[136,640]{1,0:T(8,128)(2,1)S(1)}, s16[136,640]{1,0:T(8,128)(2,1)S(1)}, u32[]{:S(2)}, u32[]{:S(2)}) collective-permute-start(s16[136,640]{1,0:T(8,128)(2,1)S(1)} %get-tuple-element.23.after), channel_id=1, source_target_pairs={{0,24},{8,16},{16,8},{24,0},{1,25},{9,17},{17,9},{25,1},{2,26},{10... | collective-permute-start | bytes 522248 | tf_op jit(solution)/shard_map/ppermute | solution.py:405
  78.3 1.5 %collective-permute-start.8 = (s16[136,640]{1,0:T(8,128)(2,1)S(1)}, s16[136,640]{1,0:T(8,128)(2,1)S(1)}, u32[]{:S(2)}, u32[]{:S(2)}) collective-permute-start(s16[136,640]{1,0:T(8,128)(2,1)S(1)} %get-tuple-element.21), channel_id=1, source_target_pairs={{0,8},{8,0},{16,24},{24,16},{1,9},{9,1},{17,25},{25,17},{2,10},{10... | collective-permute-start | bytes 522248 | tf_op jit(solution)/shard_map/ppermute | solution.py:406
  79.8 2.9 %shard_map.62.refs_3_ = f32[256,640]{1,0:T(8,128)S(1)} custom-call(s32[1]{0:T(128)} %bitcast.core_ref.core.info, s32[1]{0:T(128)} %bitcast.1.y.y_ref, bf16[32,72,128]{2,1,0:T(8,128)(2,1)S(1)} %collective-permute-done.4.arrived, bf16[4096,640]{1,0:T(8,128)(2,1)S(1)} %get-tuple-element.15.weights, s16[136,640]{1,0:T(8,128)(2,1)S(1)} %get-tuple-element.23.after, ...), custom_call_target="tpu_custom_call" | custom-call | flops 1342177280 | bytes 2097152 | tf_op jit(solution)/shard_map/pallas_call | solution.py:435
  83.0 3.7 %collective-permute-done.8.refs_2_ = s16[136,640]{1,0:T(8,128)(2,1)S(1)} collective-permute-done((s16[136,640]{1,0:T(8,128)(2,1)S(1)}, s16[136,640]{1,0:T(8,128)(2,1)S(1)}, u32[]{:S(2)}, u32[]{:S(2)}) %collective-permute-start.8) | collective-permute-done | bytes 174112 | tf_op jit(solution)/shard_map/ppermute | solution.py:406
  87.6 27.7 %all_to_all.10.ref = s16[16,32,768]{2,1,0:T(8,128)(2,1)S(1)} all-to-all(s16[16,32,768]{2,1,0:T(8,128)(2,1)S(1)} %shard_map.63), channel_id=1, replica_groups=mesh['z'=8,'y'=4,'c'=2,'x'=4] {'z','c'}, dimensions={0} | all-to-all | bytes 1572864 | tf_op jit(solution)/shard_map/all_to_all | solution.py:452
  115.2 0.9 shard_map.64
  (24 shorter events, 5.8 us)
Async XLA Ops:
  0.0 43.9 %collective-permute-start.3 = (bf16[1,2048,1280]{2,1,0:T(8,128)(2,1)}, bf16[1,2048,1280]{2,1,0:T(8,128)(2,1)}, u32[]{:S(2)}, u32[]{:S(2)}) collective-permute-start(bf16[1,2048,1280]{2,1,0:T(8,128)(2,1)} %w_own.1), channel_id=1, source_target_pairs={{0,4},{4,0},{1,5},{5,1},{2,6},{6,2},{3,7},{7,3},{8,12},{12,8},{9,1... | collective-permute-start | bytes 15728648 | tf_op jit(solution)/shard_map/ppermute | solution.py:349
  3.2 0.8 copy-start
  4.0 0.7 copy-start.2
  4.6 0.7 copy-start.3
  6.0 4.1 %collective-permute-start = (bf16[136,128]{1,0:T(8,128)(2,1)S(1)}, bf16[136,128]{1,0:T(8,128)(2,1)S(1)}, u32[]{:S(2)}, u32[]{:S(2)}) collective-permute-start(bf16[136,128]{1,0:T(8,128)(2,1)S(1)} %shard_map.55.part0), channel_id=1, source_target_pairs={{0,1},{1,2},{2,3},{3,0},{4,5},{5,6},{6,7},{7,4},{8,9},{9,10},{10,1... | collective-permute-start | bytes 104456 | tf_op jit(solution)/shard_map/ppermute | solution.py:366
  6.1 4.4 %collective-permute-start.1 = (bf16[136,128]{1,0:T(8,128)(2,1)S(1)}, bf16[136,128]{1,0:T(8,128)(2,1)S(1)}, u32[]{:S(2)}, u32[]{:S(2)}) collective-permute-start(bf16[136,128]{1,0:T(8,128)(2,1)S(1)} %shard_map.55.part0), channel_id=1, source_target_pairs={{0,2},{1,3},{2,0},{3,1},{4,6},{5,7},{6,4},{7,5},{8,10},{9,11},{10,... | collective-permute-start | bytes 104456 | tf_op jit(solution)/shard_map/ppermute | solution.py:366
  8.1 3.3 %collective-permute-start.2 = (bf16[136,128]{1,0:T(8,128)(2,1)S(1)}, bf16[136,128]{1,0:T(8,128)(2,1)S(1)}, u32[]{:S(2)}, u32[]{:S(2)}) collective-permute-start(bf16[136,128]{1,0:T(8,128)(2,1)S(1)} %shard_map.55.part0), channel_id=1, source_target_pairs={{0,3},{1,0},{2,1},{3,2},{4,7},{5,4},{6,5},{7,6},{8,11},{9,8},{10,9... | collective-permute-start | bytes 104456 | tf_op jit(solution)/shard_map/ppermute | solution.py:366
  13.0 27.4 %all-to-all-start = ((bf16[32,72,128]{2,1,0:T(8,128)(2,1)}), bf16[32,72,128]{2,1,0:T(8,128)(2,1)S(1)}, u32[]{:S(2)}, u32[]{:S(2)}) async-start(bf16[32,72,128]{2,1,0:T(8,128)(2,1)} %pack.1.after), calls=%async_computation | async-start | bytes 1179648 | tf_op jit(solution)/shard_map/all_to_all | solution.py:379
  40.4 16.8 %collective-permute-start.4 = (bf16[32,72,128]{2,1,0:T(8,128)(2,1)S(1)}, bf16[32,72,128]{2,1,0:T(8,128)(2,1)S(1)}, u32[]{:S(2)}, u32[]{:S(2)}) collective-permute-start(bf16[32,72,128]{2,1,0:T(8,128)(2,1)S(1)} %all-to-all-done.arrived), channel_id=1, source_target_pairs={{0,4},{4,0},{1,5},{5,1},{2,6},{6,2},{3,7},{7,3},{8,12},{12,8},{9,1... | collective-permute-start | bytes 1769480 | tf_op jit(solution)/shard_map/ppermute | solution.py:388
  54.7 14.6 %collective-permute-start.5 = (s16[264,640]{1,0:T(8,128)(2,1)S(1)}, s16[264,640]{1,0:T(8,128)(2,1)S(1)}, u32[]{:S(2)}, u32[]{:S(2)}) collective-permute-start(s16[264,640]{1,0:T(8,128)(2,1)S(1)} %get-tuple-element.16.after), channel_id=1, source_target_pairs={{0,8},{8,0},{16,24},{24,16},{1,9},{9,1},{17,25},{25,17},{2,10},{10... | collective-permute-start | bytes 1013768 | tf_op jit(solution)/shard_map/ppermute | solution.py:405
  55.4 13.9 %collective-permute-start.6 = (s16[264,640]{1,0:T(8,128)(2,1)S(1)}, s16[264,640]{1,0:T(8,128)(2,1)S(1)}, u32[]{:S(2)}, u32[]{:S(2)}) collective-permute-start(s16[264,640]{1,0:T(8,128)(2,1)S(1)} %get-tuple-element.18), channel_id=1, source_target_pairs={{0,24},{8,16},{16,8},{24,0},{1,25},{9,17},{17,9},{25,1},{2,26},{10... | collective-permute-start | bytes 1013768 | tf_op jit(solution)/shard_map/ppermute | solution.py:406
  62.9 10.2 %collective-permute-start.10 = (s16[264,640]{1,0:T(8,128)(2,1)S(1)}, s16[264,640]{1,0:T(8,128)(2,1)S(1)}, u32[]{:S(2)}, u32[]{:S(2)}) collective-permute-start(s16[264,640]{1,0:T(8,128)(2,1)S(1)} %get-tuple-element.22), channel_id=1, source_target_pairs={{0,24},{8,16},{16,8},{24,0},{1,25},{9,17},{17,9},{25,1},{2,26},{10... | collective-permute-start | bytes 1013768 | tf_op jit(solution)/shard_map/ppermute | solution.py:406
  63.9 9.2 %collective-permute-start.9 = (s16[264,640]{1,0:T(8,128)(2,1)S(1)}, s16[264,640]{1,0:T(8,128)(2,1)S(1)}, u32[]{:S(2)}, u32[]{:S(2)}) collective-permute-start(s16[264,640]{1,0:T(8,128)(2,1)S(1)} %get-tuple-element.17.after), channel_id=1, source_target_pairs={{0,8},{8,0},{16,24},{24,16},{1,9},{9,1},{17,25},{25,17},{2,10},{10... | collective-permute-start | bytes 1013768 | tf_op jit(solution)/shard_map/ppermute | solution.py:405
  70.1 13.0 %collective-permute-start.7 = (s16[136,640]{1,0:T(8,128)(2,1)S(1)}, s16[136,640]{1,0:T(8,128)(2,1)S(1)}, u32[]{:S(2)}, u32[]{:S(2)}) collective-permute-start(s16[136,640]{1,0:T(8,128)(2,1)S(1)} %get-tuple-element.20.after), channel_id=1, source_target_pairs={{0,24},{8,16},{16,8},{24,0},{1,25},{9,17},{17,9},{25,1},{2,26},{10... | collective-permute-start | bytes 522248 | tf_op jit(solution)/shard_map/ppermute | solution.py:405
  76.3 6.4 %collective-permute-start.11 = (s16[136,640]{1,0:T(8,128)(2,1)S(1)}, s16[136,640]{1,0:T(8,128)(2,1)S(1)}, u32[]{:S(2)}, u32[]{:S(2)}) collective-permute-start(s16[136,640]{1,0:T(8,128)(2,1)S(1)} %get-tuple-element.23.after), channel_id=1, source_target_pairs={{0,24},{8,16},{16,8},{24,0},{1,25},{9,17},{17,9},{25,1},{2,26},{10... | collective-permute-start | bytes 522248 | tf_op jit(solution)/shard_map/ppermute | solution.py:405
  78.3 4.7 %collective-permute-start.12 = (s16[136,640]{1,0:T(8,128)(2,1)S(1)}, s16[136,640]{1,0:T(8,128)(2,1)S(1)}, u32[]{:S(2)}, u32[]{:S(2)}) collective-permute-start(s16[136,640]{1,0:T(8,128)(2,1)S(1)} %get-tuple-element.24), channel_id=1, source_target_pairs={{0,8},{8,0},{16,24},{24,16},{1,9},{9,1},{17,25},{25,17},{2,10},{10... | collective-permute-start | bytes 522248 | tf_op jit(solution)/shard_map/ppermute | solution.py:406
  78.3 36.9 %copy-start.1 = (f32[1,1280]{1,0:T(1,128)S(1)}, f32[1,1280]{1,0:T(1,128)}, u32[]{:S(2)}) copy-start(f32[1,1280]{1,0:T(1,128)} %bias.1) | copy-start | bytes 15364
  78.3 8.4 %collective-permute-start.8 = (s16[136,640]{1,0:T(8,128)(2,1)S(1)}, s16[136,640]{1,0:T(8,128)(2,1)S(1)}, u32[]{:S(2)}, u32[]{:S(2)}) collective-permute-start(s16[136,640]{1,0:T(8,128)(2,1)S(1)} %get-tuple-element.21), channel_id=1, source_target_pairs={{0,8},{8,0},{16,24},{24,16},{1,9},{9,1},{17,25},{25,17},{2,10},{10... | collective-permute-start | bytes 522248 | tf_op jit(solution)/shard_map/ppermute | solution.py:406
